TPU v7x, 256 devices: a 2x2x32 block of a 4x8x32 slice. The times are simulated.
256 devices in a mesh: member: 4 (over x, y), region: 64 (over z, core).
Axes of the slice: x: 2, y: 2, z: 32, core: 2. Of those that a mesh axis runs over, the one named last changes fastest.
The devices are a block of a 4x8x32 slice.
Arguments:
- mesh_nodes: bfloat16 [131072, 512], P(('member', 'region')), parts along dimension 0, may hold values from -6 to 6
- mesh_edges: bfloat16 [131072, 512], P('region'), may hold values from -6 to 6
- grid_nodes: bfloat16 [98304, 512], P(('member', 'region')), parts along dimension 0, may hold values from -6 to 6
- grid_edges: bfloat16 [73728, 512], P('region'), may hold values from -6 to 6
- boundary: int32 [64, 32], P('region'), may hold values from 0 to 511
- mesh_need: int32 [64, 64, 8], P('region'), may hold values from 0 to 31
- mesh_sender: int32 [64, 2048], P('region'), may hold values from 0 to 1023, as said below
- mesh_receiver: int32 [64, 2048], P('region'), may hold values from 0 to 511
- mesh_live: int32 [64], P('region'), may hold values from 512 to 2048, as said below
- grid_need: int32 [64, 4, 8], P('region'), may hold values from 0 to 31
- grid_sender: int32 [64, 1152], P('region'), may hold values from 0 to 543, as said below
- grid_receiver: int32 [64, 1152], P('region'), may hold values from 0 to 383
- process_edge_in: bfloat16 [1536, 512], replicated, may hold values from -0.15625 to 0.15625
- process_edge_bias: float32 [512], replicated, may hold values from -3 to 3
- process_edge_out: bfloat16 [512, 512], replicated, may hold values from -0.25 to 0.25
- process_edge_gain: float32 [512], replicated, may hold values from 0.5 to 1.5
- process_node_in: bfloat16 [1024, 512], replicated, may hold values from -0.1875 to 0.1875
- process_node_bias: float32 [512], replicated, may hold values from -3 to 3
- process_node_out: bfloat16 [512, 512], replicated, may hold values from -0.25 to 0.25
- process_node_gain: float32 [512], replicated, may hold values from 0.5 to 1.5
- decode_edge_in: bfloat16 [1536, 512], replicated, may hold values from -0.15625 to 0.15625
- decode_edge_bias: float32 [512], replicated, may hold values from -3 to 3
- decode_edge_out: bfloat16 [512, 512], replicated, may hold values from -0.25 to 0.25
- decode_edge_gain: float32 [512], replicated, may hold values from 0.5 to 1.5
- decode_node_in: bfloat16 [1024, 512], replicated, may hold values from -0.1875 to 0.1875
- decode_node_bias: float32 [512], replicated, may hold values from -3 to 3
- decode_node_out: bfloat16 [512, 512], replicated, may hold values from -0.25 to 0.25
- decode_node_gain: float32 [512], replicated, may hold values from 0.5 to 1.5
Outputs:
- mesh_out: bfloat16 [131072, 512], P(('member', 'region')), parts along dimension 0
- grid_out: bfloat16 [98304, 512], P(('member', 'region')), parts along dimension 0
There are 4 independent parts, one for each index of `member`. A program takes and returns all parts, laid end to end along the dimension named above; an argument that names none is the same for every part. Nothing has to cross between parts.
Inputs may be any that keep to these rules, and one draw needn't show every extreme that they name: The first mesh_live[d] slots of region d are live and the rest are padding; in every draw some region has all 2048 slots live. `mesh_sender`: a value below 512 names a node of the region itself; 512 + s * 8 + k names the k-th node that the region reads from region s; most slots name the region's own nodes, most remote reads come from its four neighbours, and a few reach any region. `grid_sender`: a value below 512 names a node of the region's mesh_out; 512 + j * 8 + k names the k-th node read from its j-th neighbour; most edges name the region's own nodes.
All inputs are finite; a program needn't handle non-finite values.
Results may differ from a plain program's by a relative error of at most 0.007.
Values may be sent and summed in bfloat16 or wider, within the bound.
No kernel may reach another device: no remote copies, remote signals or barrier semaphores. Data moves between devices by JAX's collectives and lax.ppermute only.
A program may use at most 64 MiB of HBM per device.

v0:
```python
import functools

import jax
import jax.numpy as jnp
from jax import lax
from jax.experimental import pallas as pl
from jax.experimental.pallas import tpu as pltpu
from jax.sharding import Mesh
from jax.sharding import PartitionSpec as P

REGION = ("z", "core")
MEMBER_REGION = ("member", "z", "core")
BF = jnp.bfloat16
F32 = jnp.float32
I32 = jnp.int32
HBM = pltpu.MemorySpace.HBM
SEED = 12
LEAD = 3
STEPS = 4
BLOCK = 512
GRID_BLOCK = 384
LIMIT = 36 * 2**20


def iota(shape, dim):
    return lax.broadcasted_iota(I32, shape, dim)


def ones_where(mask):
    return jnp.where(mask, 1.0, 0.0).astype(BF)


def dot(a, b):
    return jnp.dot(a, b, preferred_element_type=F32)


def dot_t(a, b):
    return lax.dot_general(a, b, (((0,), (0,)), ((), ())), preferred_element_type=F32)


def columns(rows):
    lines = [rows[i : i + 1, j : j + 128] for i in range(rows.shape[0]) for j in range(0, rows.shape[1], 128)]
    eye = iota((128, 128), 0) == iota((128, 128), 1)
    return [jnp.sum(jnp.where(eye, jnp.broadcast_to(line, (128, 128)), 0), axis=1, keepdims=True) for line in lines]


def rows_hot(rows, count):
    return jnp.concatenate([ones_where(iota((128, count), 1) == c) for c in columns(rows)], axis=0)


def silu(x):
    return x * (0.5 + 0.5 * jnp.tanh(0.5 * x))


def finish(pre, bias, w_out, gain):
    hidden = silu(pre + bias).astype(BF)
    y = dot(hidden, w_out)
    y = y - jnp.mean(y, axis=1, keepdims=True)
    spread = jnp.mean(y * y, axis=1, keepdims=True)
    return y * lax.rsqrt(spread + 0.25) * gain


def whole(shape):
    return pl.BlockSpec(shape, lambda *_: (0,) * len(shape))


def call(body, grid, ins, outs, scratch=(), flops=0, nbytes=0):
    place = lambda a, s, *near: a if near or s.memory_space not in (None, HBM) else pltpu.with_memory_space_constraint(a, HBM)
    result = lambda s, d, p, *far: HBM(s, d) if far or p.memory_space == HBM else jax.ShapeDtypeStruct(s, d)
    return pl.pallas_call(
        body,
        grid=grid,
        in_specs=[i[1] for i in ins],
        out_specs=[o[2] for o in outs],
        out_shape=[result(*o) for o in outs],
        scratch_shapes=list(scratch),
        compiler_params=pltpu.CompilerParams(vmem_limit_bytes=LIMIT),
        cost_estimate=pl.CostEstimate(flops=flops, bytes_accessed=nbytes, transcendentals=0),
    )(*[place(*i) for i in ins])


def publish_body(boundary_hbm, nodes_hbm, out, boundary, nodes, sems):
    copies = [pltpu.make_async_copy(boundary_hbm, boundary, sems.at[0]), pltpu.make_async_copy(nodes_hbm, nodes, sems.at[1])]
    for copy in copies:
        copy.start()
    for copy in copies:
        copy.wait()
    hot = ones_where(iota((nodes.shape[0], boundary.shape[1]), 0) == boundary[...])
    out[...] = dot_t(hot, nodes[...]).astype(BF)


def before_body(sender, receiver, nodes, w_in, edges, ready, out, table_r, table_s):
    n, f = nodes.shape

    @pl.when(pl.program_id(0) == 0)
    def _():
        table_s[...] = dot(nodes[...], w_in[0:f, :]).astype(BF)
        table_r[...] = dot(nodes[...], w_in[f : 2 * f, :]).astype(BF)

    total = dot(edges[...], w_in[2 * f : 3 * f, :])
    total += dot(rows_hot(sender[0], n), table_s[...])
    total += dot(rows_hot(receiver[0], n), table_r[...])
    out[...] = total


def grid_before_body(receiver, nodes, w_in, edges, ready, out, table_r):
    n, f = nodes.shape

    @pl.when(pl.program_id(0) == 0)
    def _():
        table_r[...] = dot(nodes[...], w_in[f : 2 * f, :]).astype(BF)

    out[...] = dot(edges[...], w_in[2 * f : 3 * f, :]) + dot(rows_hot(receiver[0], n), table_r[...])


def pieces_of(chips, offered):
    pair = 2 * offered
    far = [(2, 0), (-2, 1)]
    for step in range(STEPS + 1):
        far += [(LEAD + step, 0), (SEED + step, 0), (step - SEED, 1)]
    far += [(-LEAD, 1)]
    for step in range(1, STEPS + 1):
        far += [(-LEAD - step, 1), (-SEED - step, 1), (SEED - step, 0)]
    table = {}
    for i, (offset, flip) in enumerate(far):
        table.setdefault(offset % chips, (i * pair, flip))
    return table


def relative(sender, n, pair, chips, z, c):
    far = sender - n
    region = far // pair
    sign = 2 * c - 1
    offset = (sign * (region // 2 - z) + 2 * chips) % chips
    half = jnp.where(region % 2 == c, 0, 1)
    return far >= 0, region, offset, half, far % pair


def is_near(offset, chips):
    return (offset <= 1) | (offset == chips - 1)


def main_body(chips, first, place, live, sender, sender_row, receiver_row, need, w_s, both, up, down, edges, before, bias, w_out,
              gain, start, ready, totals, table):
    z, c = place[0], place[1]
    n, _ = totals.shape
    step = pl.program_id(0)
    rows = edges.shape[0]
    pair, regions = need.shape
    offered = both.shape[0] // 2

    @pl.when(step == 0)
    def _():
        totals[...] = start[...]
        r = iota((6 * pair, regions), 0)
        near = r // (2 * pair)
        half = (r // pair) % 2
        moved = jnp.where(near == 2, -1, near)
        chip = (z + (2 * c - 1) * moved + chips) % chips
        region = 2 * chip + jnp.where(half == 1, 1 - c, c)
        wanted = lax.dot_general(ones_where(iota((6 * pair, regions), 1) == region), need[...].astype(F32).astype(BF),
                                 (((1,), (1,)), ((), ())), preferred_element_type=F32)
        lane = iota((6 * pair, pair), 1) == iota((6 * pair, pair), 0) % pair
        column = jnp.sum(jnp.where(lane, wanted, 0.0), axis=1, keepdims=True).astype(I32)
        chosen = []
        for j, (source, flip) in enumerate(((both, 0), (up, 0), (down, 1))):
            own_half = iota((2 * pair, 2 * offered), 0) // pair
            at = (1 - own_half if flip else own_half) * offered + column[j * 2 * pair : (j + 1) * 2 * pair, :]
            chosen.append(dot(ones_where(iota((2 * pair, 2 * offered), 1) == at), source[...]))
        table[...] = dot(jnp.concatenate(chosen, axis=0).astype(BF), w_s[...]).astype(BF)

    remote, _, offset, half, slot = relative(sender[0], n, pair, chips, z, c)
    near = jnp.where(offset == chips - 1, 2, offset)
    place_of = jnp.where(remote & is_near(offset, chips), near * 2 * pair + half * pair + slot, -1)
    pre = before[...] + dot(rows_hot(place_of, 6 * pair), table[...])
    update = finish(pre, bias[...], w_out[...], gain[...])
    message = (edges[...].astype(F32) + update).astype(BF)
    position = (first + step) * rows + iota((1, rows), 1)
    remote, _, offset, _, _ = relative(sender_row[0], n, pair, chips, z, c)
    later = remote & jnp.logical_not(is_near(offset, chips))
    target = jnp.where((position < live[0]) & jnp.logical_not(later), receiver_row[0], -1)
    totals[...] += dot(ones_where(iota((n, rows), 0) == target), message)


def gathered(at, sources, starts):
    out = None
    for source, start in zip(sources, starts):
        hot = ones_where(iota((at.shape[0], source.shape[0]), 1) + start == at)
        part = dot(hot, source[...])
        out = part if out is None else out + part
    return out


def compact_body(chips, offered, starts, place, live, sender, receiver, need, w_in, table_r, edges, *refs):
    sources = refs[: len(starts)]
    outs, count, kept, sems = refs[len(starts) : len(starts) + 5], refs[len(starts) + 5], refs[-6:-1], refs[-1]
    pre, rows, source_rows, at_out, target_out = kept
    z, c = place[0], place[1]
    groups = sender.shape[0]
    n, f = table_r.shape
    pair, regions = need.shape
    where_at = pieces_of(chips, offered)
    send = sender[...]
    remote, _, offset, _, _ = relative(send, n, pair, chips, z, c)
    position = iota((groups, 128), 0) * 128 + iota((groups, 128), 1)
    late = remote & jnp.logical_not(is_near(offset, chips)) & (position < live[0])
    late_bits = ones_where(late)
    within = dot(late_bits, ones_where(iota((128, 128), 0) < iota((128, 128), 1)))
    above = jnp.sum(dot(ones_where(iota((groups, groups), 1) < iota((groups, groups), 0)), late_bits), axis=1, keepdims=True)
    rank = jnp.where(late, (within + above).astype(I32), -1)
    total = jnp.sum(jnp.where(late, 1, 0))
    blocks = (total + 127) // 128
    count[0] = blocks

    def one(block, carry):
        base = pl.multiple_of(block * 128, 128)
        lines = pl.ds(base, 128)
        hot, send_at, receive_at = [], jnp.zeros((128, 128), I32), jnp.zeros((128, 128), I32)
        for g in range(groups):
            match = iota((128, 128), 0) + base == rank[g : g + 1, :]
            hot.append(ones_where(match))
            send_at += jnp.where(match, send[g : g + 1, :] + 1, 0)
            receive_at += jnp.where(match, receiver[g : g + 1, :] + 1, 0)
        edge = dot(jnp.concatenate(hot, axis=1), edges[...]).astype(BF)
        from_ = jnp.sum(send_at, axis=1, keepdims=True) - 1
        to = jnp.sum(receive_at, axis=1, keepdims=True) - 1
        valid, region, offset, half, slot = relative(from_, n, pair, chips, z, c)
        wanted = lax.dot_general(ones_where(iota((128, regions), 1) == region), need[...].astype(F32).astype(BF),
                                 (((1,), (1,)), ((), ())), preferred_element_type=F32)
        chosen = jnp.sum(jnp.where(iota((128, pair), 1) == slot, wanted, 0.0), axis=1, keepdims=True).astype(I32)
        start, flip = jnp.zeros((128, 1), I32), jnp.zeros((128, 1), I32)
        for key, (row, turned) in where_at.items():
            start = jnp.where(offset == key, row, start)
            flip = jnp.where(offset == key, turned, flip)
        at = jnp.where(valid, start + jnp.where(flip == 1, 1 - half, half) * offered + chosen, -1)
        rows[...] = edge
        pre[...] = dot(edge, w_in[2 * f : 3 * f, :]) + dot(ones_where(iota((128, n), 1) == to), table_r[...])
        source_rows[...] = gathered(at, sources, starts).astype(BF)
        at_out[...] = jnp.broadcast_to(at, (128, 128))
        target_out[...] = jnp.broadcast_to(to, (128, 128))
        copies = [pltpu.make_async_copy(v, o.at[lines, :], sems.at[i]) for i, (v, o) in enumerate(zip(kept, outs))]
        for copy in copies:
            copy.start()
        for copy in copies:
            copy.wait()
        return carry

    lax.fori_loop(0, blocks, one, 0)


def far_body(starts, count, nodes, boundary, totals, bias, gain, node_bias, node_gain, *refs):
    k = len(starts)
    sources = refs[:k]
    stored = refs[k : k + 5]
    (w_s_hbm, w_out_hbm, node_in_hbm, node_out_hbm, result, kept_result, published, acc, w_s, w_out, node_in, node_out, sems) = refs[k + 5 : -6]
    kept, late_sems = refs[-6:-1], refs[-1]
    pre, rows, source_rows, at, target = kept
    n, f = nodes.shape
    copies = [
        pltpu.make_async_copy(w_s_hbm.at[pl.ds(0, f), :], w_s, sems.at[0]),
        pltpu.make_async_copy(w_out_hbm, w_out, sems.at[1]),
        pltpu.make_async_copy(node_in_hbm, node_in, sems.at[2]),
        pltpu.make_async_copy(node_out_hbm, node_out, sems.at[3]),
    ]
    for copy in copies:
        copy.start()

    def fetch(block, begin):
        lines = pl.ds(pl.multiple_of(block * 128, 128), 128)
        for i, (v, o) in enumerate(zip(stored, kept)):
            copy = pltpu.make_async_copy(v.at[lines, :], o, late_sems.at[i])
            copy.start() if begin else copy.wait()

    @pl.when(count[0] > 0)
    def _():
        fetch(0, True)

    acc[...] = totals[...]
    copies[0].wait()
    copies[1].wait()

    def one(block, carry):
        fetch(block, False)
        source = (source_rows[...].astype(F32) + gathered(at[...][:, 0:1], sources, starts)).astype(BF)
        update = finish(pre[...] + dot(source, w_s[...]), bias[...], w_out[...], gain[...])
        message = (rows[...].astype(F32) + update).astype(BF)
        eye = iota((128, 128), 0) == iota((128, 128), 1)
        to = jnp.sum(jnp.where(eye, target[...] + 1, 0), axis=0, keepdims=True) - 1
        acc[...] += dot(ones_where(iota((n, 128), 0) == to), message)

        @pl.when(block + 1 < count[0])
        def _():
            fetch(block + 1, True)

        return carry

    lax.fori_loop(0, count[0], one, 0)
    copies[2].wait()
    copies[3].wait()
    pre_node = dot(nodes[...], node_in[0:f, :]) + dot(acc[...].astype(BF), node_in[f : 2 * f, :])
    update = finish(pre_node, node_bias[...], node_out[...], node_gain[...])
    value = (nodes[...].astype(F32) + update).astype(BF)
    result[...] = value
    kept_result[...] = value
    hot = ones_where(iota((n, boundary.shape[1]), 0) == boundary[...])
    published[...] = dot_t(hot, value).astype(BF)


def grid_local_body(sender, mesh_out, w_s, before, out, table):
    n = mesh_out.shape[0]

    @pl.when(pl.program_id(0) == 0)
    def _():
        table[...] = dot(mesh_out[...], w_s[...]).astype(BF)

    out[...] = before[...] + dot(rows_hot(sender[0], n), table[...])


def grid_body(mesh_count, pair, sender, receiver_row, wanted, a, b, c, d, w_s, nodes, edges, before, bias, w_out, gain,
              node_in, node_bias, node_out, node_gain, result, totals, table):
    n, f = nodes.shape
    step = pl.program_id(0)
    rows = edges.shape[0]

    @pl.when(step == 0)
    def _():
        pieces = []
        for j, block in enumerate((a, b, c, d)):
            hot = ones_where(iota((block.shape[0], pair), 0) == wanted[j : j + 1, :])
            pieces.append(dot_t(hot, block[...]))
        chosen = jnp.concatenate(pieces, axis=0).astype(BF)
        table[...] = dot(chosen, w_s[...]).astype(BF)

    pre = before[...] + dot(rows_hot(sender[0] - mesh_count, table.shape[0]), table[...])
    update = finish(pre, bias[...], w_out[...], gain[...])
    message = (edges[...].astype(F32) + update).astype(BF)
    part = dot(ones_where(iota((n, rows), 0) == receiver_row[0]), message)

    @pl.when(step == 0)
    def _():
        totals[...] = part

    @pl.when(step > 0)
    def _():
        totals[...] += part

    @pl.when(step == pl.num_programs(0) - 1)
    def _():
        summed = totals[...].astype(BF)
        pre = dot(nodes[...], node_in[0:f, :]) + dot(summed, node_in[f : 2 * f, :])
        update = finish(pre, node_bias[...], node_out[...], node_gain[...])
        result[...] = (nodes[...].astype(F32) + update).astype(BF)


def local(
    mesh_nodes,
    mesh_edges,
    grid_nodes,
    grid_edges,
    boundary,
    mesh_need,
    mesh_sender,
    mesh_receiver,
    mesh_live,
    grid_need,
    grid_sender,
    grid_receiver,
    process_edge_in,
    process_edge_bias,
    process_edge_out,
    process_edge_gain,
    process_node_in,
    process_node_bias,
    process_node_out,
    process_node_gain,
    decode_edge_in,
    decode_edge_bias,
    decode_edge_out,
    decode_edge_gain,
    decode_node_in,
    decode_node_bias,
    decode_node_out,
    decode_node_gain,
):
    chips = lax.axis_size("z")
    regions = 2 * chips
    place = jnp.stack([lax.axis_index("z"), lax.axis_index("core")]).astype(I32)
    n, f = mesh_nodes.shape
    edges = mesh_edges.shape[0]
    grid_n = grid_nodes.shape[0]
    grid_e = grid_edges.shape[0]
    offered = boundary.shape[1]
    pair = mesh_need.shape[2]
    smem = pl.BlockSpec(memory_space=pltpu.SMEM)
    row = lambda v: v.reshape(1, -1)
    mesh_steps = edges // BLOCK
    grid_steps = grid_e // GRID_BLOCK
    as_blocks = lambda v, b: v.reshape(-1, b // 128, 128)
    as_rows = lambda v, b: v.reshape(-1, 1, b)
    idx_spec = lambda b: pl.BlockSpec((1, b // 128, 128), lambda i: (i, 0, 0))
    row_spec = lambda b: pl.BlockSpec((1, 1, b), lambda i: (i, 0, 0))
    tile = lambda b: pl.BlockSpec((b, f), lambda i: (i, 0))
    full = lambda v: (v, whole(v.shape))
    held = lambda v: (v, whole(v.shape), True)

    def along(steps):
        pairs = []
        for z in range(chips):
            pairs.append((2 * z, 2 * ((z + steps) % chips)))
            pairs.append((2 * z + 1, 2 * ((z - steps) % chips) + 1))
        return pairs

    def shift(v, steps):
        return lax.ppermute(v, REGION, along(steps))

    def swap(v):
        return lax.ppermute(v, "core", [(0, 1), (1, 0)])

    hbm = pl.BlockSpec(memory_space=HBM)
    anywhere = pl.BlockSpec(memory_space=pl.ANY)
    need = jnp.transpose(mesh_need[0])
    send_rows = mesh_sender.reshape(-1, 128)
    receive_rows = mesh_receiver.reshape(-1, 128)

    (own,) = call(publish_body, (1,), [(boundary, hbm), (mesh_nodes, hbm)], [((offered, f), BF, whole((offered, f)))],
                  [pltpu.VMEM((1, offered), I32), pltpu.VMEM((n, f), BF), pltpu.SemaphoreType.DMA((2,))],
                  flops=2 * offered * n * f, nbytes=2 * n * f)
    both = jnp.concatenate([own, swap(own)], axis=0)
    lead = [both]
    lead.append(shift(both, 1))
    seed = shift(both, SEED)
    lead.append(shift(lead[1], 1))
    lead.append(shift(lead[2], 1))
    back = [None]
    for k in range(1, LEAD + 1):
        back.append(swap(lead[k]))
    seed_back = swap(seed)
    before, table_r = call(
        before_body, (mesh_steps,),
        [(as_blocks(mesh_sender, BLOCK), idx_spec(BLOCK)), (as_blocks(mesh_receiver, BLOCK), idx_spec(BLOCK)), full(mesh_nodes),
         full(process_edge_in), (mesh_edges, tile(BLOCK)), (lead[1], anywhere)],
        [((edges, f), F32, tile(BLOCK), True), ((n, f), BF, whole((n, f)))],
        [pltpu.VMEM((n, f), BF)],
        flops=2 * f * f * (edges * 3 + 2 * n), nbytes=6 * edges * f,
    )
    halves = mesh_steps // 2
    totals = jnp.zeros((n, f), F32)
    ready = lead[2]
    current = jnp.concatenate([lead[3], seed, seed_back], axis=0)
    chain, turned = [current], []
    for _ in range(STEPS):
        chain.append(shift(chain[-1], 1))
        turned.append(swap(chain[-1]))
    for part in range(2):
        first = part * halves
        at = lambda spec_rows, rank: pl.BlockSpec((1,) + spec_rows, lambda i: (i + first,) + (0,) * rank)
        moved = pl.BlockSpec((BLOCK, f), lambda i: (i + first, 0))
        (totals,) = call(
            functools.partial(main_body, chips, first), (halves,),
            [(place, smem), (mesh_live, smem), (as_blocks(mesh_sender, BLOCK), at((BLOCK // 128, 128), 2)),
             (as_rows(mesh_sender, BLOCK), at((1, BLOCK), 2)), (as_rows(mesh_receiver, BLOCK), at((1, BLOCK), 2)), full(need),
             (process_edge_in, whole((f, f))), held(lead[0]), held(lead[1]), held(back[1]), (mesh_edges, moved),
             (before, moved), full(row(process_edge_bias)), full(process_edge_out), full(row(process_edge_gain)), full(totals),
             (ready, anywhere)],
            [((n, f), F32, whole((n, f)), True)],
            [pltpu.VMEM((6 * pair, f), BF)],
            flops=2 * f * f * halves * BLOCK * 2, nbytes=6 * halves * BLOCK * f,
        )
        ready = chain[0]
    (grid_before,) = call(
        grid_before_body, (grid_steps,),
        [(as_rows(grid_receiver, GRID_BLOCK), row_spec(GRID_BLOCK)), full(grid_nodes), full(decode_edge_in),
         (grid_edges, tile(GRID_BLOCK)), (chain[1], anywhere)],
        [((grid_e, f), F32, tile(GRID_BLOCK), True)],
        [pltpu.VMEM((grid_n, f), BF)],
        flops=2 * f * f * (grid_e * 2 + grid_n), nbytes=6 * grid_e * f,
    )
    far = [lead[2], back[2]] + chain + [back[3]] + turned
    starts, at_row = [], 0
    for v in far:
        starts.append(at_row)
        at_row += v.shape[0]
    last = [STEPS + 2, len(far) - 2, len(far) - 1]
    early = [i for i in range(len(far)) if i not in last]
    late_buffers = [pltpu.VMEM((128, f), F32), pltpu.VMEM((128, f), BF), pltpu.VMEM((128, f), BF), pltpu.VMEM((128, 128), I32),
                    pltpu.VMEM((128, 128), I32)]
    pre, rows, source_rows, at, target, count = call(
        functools.partial(compact_body, chips, offered, tuple(starts[i] for i in early)), (1,),
        [(place, smem), (mesh_live, smem), full(send_rows), full(receive_rows), full(need), full(process_edge_in), held(table_r),
         full(mesh_edges)] + [held(far[i]) for i in early],
        [((edges, f), F32, hbm), ((edges, f), BF, hbm), ((edges, f), BF, hbm), ((edges, 128), I32, hbm),
         ((edges, 128), I32, hbm), ((1,), I32, smem)],
        late_buffers + [pltpu.SemaphoreType.DMA((5,))],
        flops=2 * f * 128 * (edges + 4 * f), nbytes=2 * edges * f,
    )
    mesh_out, mesh_kept, published = call(
        functools.partial(far_body, tuple(starts[i] for i in last)), (1,),
        [(count, smem), full(mesh_nodes), full(boundary), full(totals), full(row(process_edge_bias)), full(row(process_edge_gain)),
         full(row(process_node_bias)), full(row(process_node_gain))] + [held(far[i]) for i in last]
        + [(v, hbm) for v in (pre, rows, source_rows, at, target)] + [(process_edge_in, hbm), (process_edge_out, hbm), (process_node_in, hbm), (process_node_out, hbm)],
        [((n, f), BF, whole((n, f))), ((n, f), BF, whole((n, f))), ((offered, f), BF, whole((offered, f)))],
        [pltpu.VMEM((n, f), F32), pltpu.VMEM((f, f), BF), pltpu.VMEM((f, f), BF), pltpu.VMEM((2 * f, f), BF), pltpu.VMEM((f, f), BF),
         pltpu.SemaphoreType.DMA((4,))] + late_buffers + [pltpu.SemaphoreType.DMA((5,))],
        flops=2 * f * f * 4 * n, nbytes=8 * n * f,
    )
    pieces = []
    for offset in (-2, -1, 1, 2):
        pieces.append(lax.ppermute(published, REGION, [(s, (s - offset) % regions) for s in range(regions)]))
    (grid_local,) = call(
        grid_local_body, (grid_steps,),
        [(as_rows(grid_sender, GRID_BLOCK), row_spec(GRID_BLOCK)), held(mesh_kept), (decode_edge_in, whole((f, f))),
         (grid_before, tile(GRID_BLOCK))],
        [((grid_e, f), F32, tile(GRID_BLOCK))],
        [pltpu.VMEM((n, f), BF)],
        flops=2 * f * f * (grid_e + n), nbytes=8 * grid_e * f,
    )
    (grid_out,) = call(
        functools.partial(grid_body, n, pair), (grid_steps,),
        [(as_rows(grid_sender, GRID_BLOCK), row_spec(GRID_BLOCK)), (as_rows(grid_receiver, GRID_BLOCK), row_spec(GRID_BLOCK)),
         full(grid_need[0]), held(pieces[0]), held(pieces[1]), held(pieces[2]), held(pieces[3]),
         (decode_edge_in, whole((f, f))), full(grid_nodes), (grid_edges, tile(GRID_BLOCK)), (grid_local, tile(GRID_BLOCK), True),
         full(row(decode_edge_bias)), full(decode_edge_out), full(row(decode_edge_gain)), full(decode_node_in),
         full(row(decode_node_bias)), full(decode_node_out), full(row(decode_node_gain))],
        [((grid_n, f), BF, whole((grid_n, f)))],
        [pltpu.VMEM((grid_n, f), F32), pltpu.VMEM((4 * pair, f), BF)],
        flops=2 * f * f * (grid_e * 2 + 3 * grid_n), nbytes=6 * grid_e * f,
    )
    return (mesh_out, grid_out)


def solution(mesh):
    cores = 2
    finer = Mesh(
        mesh.devices.reshape(mesh.shape["member"], mesh.shape["region"] // cores, cores), ("member", "z", "core")
    )
    in_specs = (
        P(MEMBER_REGION, None),
        P(REGION, None),
        P(MEMBER_REGION, None),
        P(REGION, None),
        P(REGION, None),
        P(REGION, None, None),
        P(REGION, None),
        P(REGION, None),
        P(REGION),
        P(REGION, None, None),
        P(REGION, None),
        P(REGION, None),
    ) + (P(),) * 16
    out_specs = (P(MEMBER_REGION, None), P(MEMBER_REGION, None))

    return jax.shard_map(local, mesh=finer, in_specs=in_specs, out_specs=out_specs, check_vma=False)
```

profile of v0, /device:TPU:44, one launch (start us, length us, event | category | flops | bytes accessed | tf_op | source)
XLA Modules:
  0.0 138.5 jit_solution(3064756751523096532)
XLA Ops:
  0.6 1.3 shard_map.275
  2.1 1.2 collective-permute-done
  3.3 2.1 %collective-permute-start.1 = (bf16[64,512]{1,0:T(8,128)(2,1)S(1)}, bf16[64,512]{1,0:T(8,128)(2,1)S(1)}, u32[]{:S(2)}, u32[]{:S(2)}) collective-permute-start(bf16[64,512]{1,0:T(8,128)(2,1)S(1)} %pad_maximum_fusion.both), channel_id=1, source_target_pairs={{0,2},{1,63},{2,4},{3,1},{4,6},{5,3},{6,8},{7,5},{8,10},{9,7},{10,... | collective-permute-start | bytes 196616 | tf_op jit(solution)/shard_map/ppermute | solution.py:414
  5.4 23.2 %collective-permute-done.1.ready.up = bf16[64,512]{1,0:T(8,128)(2,1)S(1)} collective-permute-done((bf16[64,512]{1,0:T(8,128)(2,1)S(1)}, bf16[64,512]{1,0:T(8,128)(2,1)S(1)}, u32[]{:S(2)}, u32[]{:S(2)}) %collective-permute-start.1) | collective-permute-done | bytes 65568 | tf_op jit(solution)/shard_map/ppermute | solution.py:414
  28.6 4.0 %collective-permute-start.5 = (bf16[64,512]{1,0:T(8,128)(2,1)S(1)}, bf16[64,512]{1,0:T(8,128)(2,1)S(1)}, u32[]{:S(2)}, u32[]{:S(2)}) collective-permute-start(bf16[64,512]{1,0:T(8,128)(2,1)S(1)} %pad_maximum_fusion.both), channel_id=1, source_target_pairs={{0,24},{1,41},{2,26},{3,43},{4,28},{5,45},{6,30},{7,47},{8,32},{9,... | collective-permute-start | bytes 196616 | tf_op jit(solution)/shard_map/ppermute | solution.py:414
  32.5 1.5 %collective-permute-done.2.refs_0_.ready = bf16[64,512]{1,0:T(8,128)(2,1)S(1)} collective-permute-done((bf16[64,512]{1,0:T(8,128)(2,1)S(1)}, bf16[64,512]{1,0:T(8,128)(2,1)S(1)}, u32[]{:S(2)}, u32[]{:S(2)}) %collective-permute-start.2) | collective-permute-done | bytes 65568 | tf_op jit(solution)/shard_map/ppermute | solution.py:414
  34.7 11.8 %collective-permute-done.5 = bf16[64,512]{1,0:T(8,128)(2,1)S(1)} collective-permute-done((bf16[64,512]{1,0:T(8,128)(2,1)S(1)}, bf16[64,512]{1,0:T(8,128)(2,1)S(1)}, u32[]{:S(2)}, u32[]{:S(2)}) %collective-permute-start.5) | collective-permute-done | bytes 65568 | tf_op jit(solution)/shard_map/ppermute | solution.py:414
  46.5 0.7 collective-permute-start.6
  47.2 0.9 collective-permute-done.6
  48.1 13.8 %collective-permute-done.7.refs_3_.ready = bf16[192,512]{1,0:T(8,128)(2,1)S(1)} collective-permute-done((bf16[192,512]{1,0:T(8,128)(2,1)S(1)}, bf16[192,512]{1,0:T(8,128)(2,1)S(1)}, u32[]{:S(2)}, u32[]{:S(2)}) %collective-permute-start.7) | collective-permute-done | bytes 196640 | tf_op jit(solution)/shard_map/ppermute | solution.py:414
  61.9 6.9 %collective-permute-done.8.refs_4_ = bf16[192,512]{1,0:T(8,128)(2,1)S(1)} collective-permute-done((bf16[192,512]{1,0:T(8,128)(2,1)S(1)}, bf16[192,512]{1,0:T(8,128)(2,1)S(1)}, u32[]{:S(2)}, u32[]{:S(2)}) %collective-permute-start.8) | collective-permute-done | bytes 196640 | tf_op jit(solution)/shard_map/ppermute | solution.py:414
  69.5 0.9 collective-permute-start.13
  70.4 5.3 %collective-permute-done.9.refs_5_ = bf16[192,512]{1,0:T(8,128)(2,1)S(1)} collective-permute-done((bf16[192,512]{1,0:T(8,128)(2,1)S(1)}, bf16[192,512]{1,0:T(8,128)(2,1)S(1)}, u32[]{:S(2)}, u32[]{:S(2)}) %collective-permute-start.9) | collective-permute-done | bytes 196640 | tf_op jit(solution)/shard_map/ppermute | solution.py:414
  75.6 8.1 %shard_map.276 = (f32[2048,512]{1,0:T(8,128)}, bf16[512,512]{1,0:T(8,128)(2,1)S(1)}) custom-call(s32[4,4,128]{2,1,0:T(4,128)} %bitcast.22, s32[4,4,128]{2,1,0:T(4,128)} %bitcast.28, bf16[512,512]{1,0:T(8,128)(2,1)} %nodes.5, bf16[1536,512]{1,0:T(8,128)(2,1)} %refs_8_.1, bf16[2048,512]{1,0:T(8,128)(2,1)} %edges.9, ...), custom_call_target="tpu_custom_call" | custom-call | flops 3758096384 | bytes 6291456 | tf_op jit(solution)/shard_map/pallas_call | solution.py:70
  83.8 1.1 broadcast_in_dim.3.start
  84.9 6.6 %shard_map.278.start = f32[512,512]{1,0:T(8,128)} custom-call(s32[2]{0:T(128)S(1)} %pad_add_fusion.place, s32[1]{0:T(128)S(6)} %copy.32.live, s32[4,4,128]{2,1,0:T(4,128)} %bitcast.23, s32[4,1,512]{2,1,0:T(1,128)} %bitcast.24, s32[4,1,512]{2,1,0:T(1,128)} %bitcast.29, s32[8,64]{1,0:T(8,128)} %bitcast.32, bf16[1536,512]{1,0:T(8,128)(2,1)} %refs_8_.1, ...), custom_call_target="tpu_custom_call" | custom-call | flops 1073741824 | bytes 3145728 | tf_op jit(solution)/shard_map/pallas_call | solution.py:70
  92.6 6.5 %shard_map.279.totals = f32[512,512]{1,0:T(8,128)} custom-call(s32[2]{0:T(128)S(1)} %pad_add_fusion.place, s32[1]{0:T(128)S(6)} %copy.32.live, s32[4,4,128]{2,1,0:T(4,128)} %bitcast.25, s32[4,1,512]{2,1,0:T(1,128)} %bitcast.26, s32[4,1,512]{2,1,0:T(1,128)} %bitcast.30, s32[8,64]{1,0:T(8,128)} %bitcast.33, bf16[1536,512]{1,0:T(8,128)(2,1)} %refs_8_.1, ...), custom_call_target="tpu_custom_call" | custom-call | flops 1073741824 | bytes 3145728 | tf_op jit(solution)/shard_map/pallas_call | solution.py:70
  99.7 5.5 %shard_map.281.before = f32[1152,512]{1,0:T(8,128)} custom-call(s32[3,1,384]{2,1,0:T(1,128)} %bitcast.37, bf16[384,512]{1,0:T(8,128)(2,1)} %nodes.7, bf16[1536,512]{1,0:T(8,128)(2,1)} %w_s.7, bf16[1152,512]{1,0:T(8,128)(2,1)} %edges.11, bf16[192,512]{1,0:T(8,128)(2,1)S(1)} %collective-permute-done.7.refs_3_.ready), custom_call_target="tpu_custom_call" | custom-call | flops 1409286144 | bytes 3538944 | tf_op jit(solution)/shard_map/pallas_call | solution.py:70
  105.2 4.8 %shard_map.277 = (f32[2048,512]{1,0:T(8,128)}, bf16[2048,512]{1,0:T(8,128)(2,1)}, bf16[2048,512]{1,0:T(8,128)(2,1)}, s32[2048,128]{1,0:T(8,128)}, s32[2048,128]{1,0:T(8,128)}, /*index=5*/s32[1]{0:T(128)}) custom-call(s32[2]{0:T(128)S(1)} %pad_add_fusion.place, s32[1]{0:T(128)S(6)} %copy.32.live, s32[16,128]{1,0:T(8,128)} %bitcast.27, s32[16,128]{1,0:T(8,128)} %bitcast.31, ...), custom_call_target="tpu_custom_call" | custom-call | flops 536870912 | bytes 2097152 | tf_op jit(solution)/shard_map/pallas_call | solution.py:70
  110.1 7.3 %shard_map.280 = (bf16[512,512]{1,0:T(8,128)(2,1)}, bf16[512,512]{1,0:T(8,128)(2,1)S(1)}, bf16[32,512]{1,0:T(8,128)(2,1)S(1)}) custom-call(s32[1]{0:T(128)} %get-tuple-element.14.count, bf16[512,512]{1,0:T(8,128)(2,1)} %nodes.5, s32[1,32]{1,0:T(1,128)} %boundary.1, f32[512,512]{1,0:T(8,128)} %shard_map.279.totals, f32[1,512]{1,0:T(1,128)} %bitcast.41, ...), custom_call_target="tpu_custom_call" | custom-call | flops 1073741824 | bytes 2097152 | tf_op jit(solution)/shard_map/pallas_call | solution.py:70
  117.4 7.1 %collective-permute-start.20 = (bf16[32,512]{1,0:T(8,128)(2,1)S(1)}, bf16[32,512]{1,0:T(8,128)(2,1)S(1)}, u32[]{:S(2)}, u32[]{:S(2)}) collective-permute-start(bf16[32,512]{1,0:T(8,128)(2,1)S(1)} %get-tuple-element.22), channel_id=1, source_target_pairs={{0,62},{1,63},{2,0},{3,1},{4,2},{5,3},{6,4},{7,5},{8,6},{9,7},{10,... | collective-permute-start | bytes 98312 | tf_op jit(solution)/shard_map/ppermute | solution.py:508
  125.0 1.0 collective-permute-start.17
  126.0 3.8 %shard_map.282.before = f32[1152,512]{1,0:T(8,128)S(1)} custom-call(s32[3,1,384]{2,1,0:T(1,128)} %bitcast.35, bf16[512,512]{1,0:T(8,128)(2,1)S(1)} %get-tuple-element.23.mesh_out, bf16[1536,512]{1,0:T(8,128)(2,1)} %w_s.7, f32[1152,512]{1,0:T(8,128)} %shard_map.281.before), custom_call_target="tpu_custom_call" | custom-call | flops 872415232 | bytes 4718592 | tf_op jit(solution)/shard_map/pallas_call | solution.py:70
  130.4 8.1 %shard_map.283 = bf16[384,512]{1,0:T(8,128)(2,1)} custom-call(s32[3,1,384]{2,1,0:T(1,128)} %bitcast.36, s32[3,1,384]{2,1,0:T(1,128)} %bitcast.38, s32[4,8]{1,0:T(4,128)} %bitcast.45, bf16[32,512]{1,0:T(8,128)(2,1)S(1)} %collective-permute-done.17.a, bf16[32,512]{1,0:T(8,128)(2,1)S(1)} %collective-permute-done.18.b, ...), custom_call_target="tpu_custom_call" | custom-call | flops 1811939328 | bytes 3538944 | tf_op jit(solution)/shard_map/pallas_call | solution.py:70
  (33 shorter events, 3.6 us)
Async XLA Ops:
  1.9 1.3 collective-permute-start
  3.3 25.3 %collective-permute-start.1 = (bf16[64,512]{1,0:T(8,128)(2,1)S(1)}, bf16[64,512]{1,0:T(8,128)(2,1)S(1)}, u32[]{:S(2)}, u32[]{:S(2)}) collective-permute-start(bf16[64,512]{1,0:T(8,128)(2,1)S(1)} %pad_maximum_fusion.both), channel_id=1, source_target_pairs={{0,2},{1,63},{2,4},{3,1},{4,6},{5,3},{6,8},{7,5},{8,10},{9,7},{10,... | collective-permute-start | bytes 196616 | tf_op jit(solution)/shard_map/ppermute | solution.py:414
  28.6 5.5 %collective-permute-start.2 = (bf16[64,512]{1,0:T(8,128)(2,1)S(1)}, bf16[64,512]{1,0:T(8,128)(2,1)S(1)}, u32[]{:S(2)}, u32[]{:S(2)}) collective-permute-start(bf16[64,512]{1,0:T(8,128)(2,1)S(1)} %collective-permute-done.1.ready.up), channel_id=1, source_target_pairs={{0,2},{1,63},{2,4},{3,1},{4,6},{5,3},{6,8},{7,5},{8,10},{9,7},{10,... | collective-permute-start | bytes 196616 | tf_op jit(solution)/shard_map/ppermute | solution.py:414
  28.6 17.9 %collective-permute-start.5 = (bf16[64,512]{1,0:T(8,128)(2,1)S(1)}, bf16[64,512]{1,0:T(8,128)(2,1)S(1)}, u32[]{:S(2)}, u32[]{:S(2)}) collective-permute-start(bf16[64,512]{1,0:T(8,128)(2,1)S(1)} %pad_maximum_fusion.both), channel_id=1, source_target_pairs={{0,24},{1,41},{2,26},{3,43},{4,28},{5,45},{6,30},{7,47},{8,32},{9,... | collective-permute-start | bytes 196616 | tf_op jit(solution)/shard_map/ppermute | solution.py:414
  34.0 13.1 %collective-permute-start.4 = (bf16[64,512]{1,0:T(8,128)(2,1)S(1)}, bf16[64,512]{1,0:T(8,128)(2,1)S(1)}, u32[]{:S(2)}, u32[]{:S(2)}) collective-permute-start(bf16[64,512]{1,0:T(8,128)(2,1)S(1)} %collective-permute-done.2.refs_0_.ready), channel_id=1, source_target_pairs={{0,2},{1,63},{2,4},{3,1},{4,6},{5,3},{6,8},{7,5},{8,10},{9,7},{10,... | collective-permute-start | bytes 196616 | tf_op jit(solution)/shard_map/ppermute | solution.py:414
  46.5 1.6 %collective-permute-start.6 = (bf16[64,512]{1,0:T(8,128)(2,1)S(1)}, bf16[64,512]{1,0:T(8,128)(2,1)S(1)}, u32[]{:S(2)}, u32[]{:S(2)}) collective-permute-start(bf16[64,512]{1,0:T(8,128)(2,1)S(1)} %collective-permute-done.5), channel_id=1, source_target_pairs={{0,1},{1,0},{2,3},{3,2},{4,5},{5,4},{6,7},{7,6},{8,9},{9,8},{10,11... | collective-permute-start | bytes 196616 | tf_op jit(solution)/shard_map/ppermute | solution.py:417
  48.1 13.8 %collective-permute-start.7 = (bf16[192,512]{1,0:T(8,128)(2,1)S(1)}, bf16[192,512]{1,0:T(8,128)(2,1)S(1)}, u32[]{:S(2)}, u32[]{:S(2)}) collective-permute-start(bf16[192,512]{1,0:T(8,128)(2,1)S(1)} %constant_dynamic-update-slice_fusion.refs_2_.ready), channel_id=1, source_target_pairs={{0,2},{1,63},{2,4},{3,1},{4,6},{5,3},{6,8},{7,5},{8,10},{9,7},{10,... | collective-permute-start | bytes 589832 | tf_op jit(solution)/shard_map/ppermute | solution.py:414
  61.9 6.9 %collective-permute-start.8 = (bf16[192,512]{1,0:T(8,128)(2,1)S(1)}, bf16[192,512]{1,0:T(8,128)(2,1)S(1)}, u32[]{:S(2)}, u32[]{:S(2)}) collective-permute-start(bf16[192,512]{1,0:T(8,128)(2,1)S(1)} %collective-permute-done.7.refs_3_.ready), channel_id=1, source_target_pairs={{0,2},{1,63},{2,4},{3,1},{4,6},{5,3},{6,8},{7,5},{8,10},{9,7},{10,... | collective-permute-start | bytes 589832 | tf_op jit(solution)/shard_map/ppermute | solution.py:414
  68.8 6.9 %collective-permute-start.9 = (bf16[192,512]{1,0:T(8,128)(2,1)S(1)}, bf16[192,512]{1,0:T(8,128)(2,1)S(1)}, u32[]{:S(2)}, u32[]{:S(2)}) collective-permute-start(bf16[192,512]{1,0:T(8,128)(2,1)S(1)} %collective-permute-done.8.refs_4_), channel_id=1, source_target_pairs={{0,2},{1,63},{2,4},{3,1},{4,6},{5,3},{6,8},{7,5},{8,10},{9,7},{10,... | collective-permute-start | bytes 589832 | tf_op jit(solution)/shard_map/ppermute | solution.py:414
  69.5 14.3 %collective-permute-start.13 = (bf16[64,512]{1,0:T(8,128)(2,1)S(1)}, bf16[64,512]{1,0:T(8,128)(2,1)S(1)}, u32[]{:S(2)}, u32[]{:S(2)}) collective-permute-start(bf16[64,512]{1,0:T(8,128)(2,1)S(1)} %collective-permute-done.1.ready.up), channel_id=1, source_target_pairs={{0,1},{1,0},{2,3},{3,2},{4,5},{5,4},{6,7},{7,6},{8,9},{9,8},{10,11... | collective-permute-start | bytes 196616 | tf_op jit(solution)/shard_map/ppermute | solution.py:417
  75.6 16.8 %collective-permute-start.14 = (bf16[192,512]{1,0:T(8,128)(2,1)S(1)}, bf16[192,512]{1,0:T(8,128)(2,1)S(1)}, u32[]{:S(2)}, u32[]{:S(2)}) collective-permute-start(bf16[192,512]{1,0:T(8,128)(2,1)S(1)} %collective-permute-done.9.refs_5_), channel_id=1, source_target_pairs={{0,2},{1,63},{2,4},{3,1},{4,6},{5,3},{6,8},{7,5},{8,10},{9,7},{10,... | collective-permute-start | bytes 589832 | tf_op jit(solution)/shard_map/ppermute | solution.py:414
  83.8 15.4 %collective-permute-start.3 = (bf16[64,512]{1,0:T(8,128)(2,1)S(1)}, bf16[64,512]{1,0:T(8,128)(2,1)S(1)}, u32[]{:S(2)}, u32[]{:S(2)}) collective-permute-start(bf16[64,512]{1,0:T(8,128)(2,1)S(1)} %collective-permute-done.2.refs_0_.ready), channel_id=1, source_target_pairs={{0,1},{1,0},{2,3},{3,2},{4,5},{5,4},{6,7},{7,6},{8,9},{9,8},{10,11... | collective-permute-start | bytes 196616 | tf_op jit(solution)/shard_map/ppermute | solution.py:417
  91.5 13.7 %collective-permute-start.11 = (bf16[192,512]{1,0:T(8,128)(2,1)S(1)}, bf16[192,512]{1,0:T(8,128)(2,1)S(1)}, u32[]{:S(2)}, u32[]{:S(2)}) collective-permute-start(bf16[192,512]{1,0:T(8,128)(2,1)S(1)} %collective-permute-done.7.refs_3_.ready), channel_id=1, source_target_pairs={{0,1},{1,0},{2,3},{3,2},{4,5},{5,4},{6,7},{7,6},{8,9},{9,8},{10,11... | collective-permute-start | bytes 589832 | tf_op jit(solution)/shard_map/ppermute | solution.py:417
  92.0 13.2 %collective-permute-start.12 = (bf16[192,512]{1,0:T(8,128)(2,1)S(1)}, bf16[192,512]{1,0:T(8,128)(2,1)S(1)}, u32[]{:S(2)}, u32[]{:S(2)}) collective-permute-start(bf16[192,512]{1,0:T(8,128)(2,1)S(1)} %collective-permute-done.8.refs_4_), channel_id=1, source_target_pairs={{0,1},{1,0},{2,3},{3,2},{4,5},{5,4},{6,7},{7,6},{8,9},{9,8},{10,11... | collective-permute-start | bytes 589832 | tf_op jit(solution)/shard_map/ppermute | solution.py:417
  92.1 17.9 %collective-permute-start.15 = (bf16[192,512]{1,0:T(8,128)(2,1)S(1)}, bf16[192,512]{1,0:T(8,128)(2,1)S(1)}, u32[]{:S(2)}, u32[]{:S(2)}) collective-permute-start(bf16[192,512]{1,0:T(8,128)(2,1)S(1)} %collective-permute-done.9.refs_5_), channel_id=1, source_target_pairs={{0,1},{1,0},{2,3},{3,2},{4,5},{5,4},{6,7},{7,6},{8,9},{9,8},{10,11... | collective-permute-start | bytes 589832 | tf_op jit(solution)/shard_map/ppermute | solution.py:417
  92.5 17.6 %collective-permute-start.16 = (bf16[192,512]{1,0:T(8,128)(2,1)S(1)}, bf16[192,512]{1,0:T(8,128)(2,1)S(1)}, u32[]{:S(2)}, u32[]{:S(2)}) collective-permute-start(bf16[192,512]{1,0:T(8,128)(2,1)S(1)} %collective-permute-done.14.refs_0_), channel_id=1, source_target_pairs={{0,1},{1,0},{2,3},{3,2},{4,5},{5,4},{6,7},{7,6},{8,9},{9,8},{10,11... | collective-permute-start | bytes 589832 | tf_op jit(solution)/shard_map/ppermute | solution.py:417
  99.2 6.0 %collective-permute-start.10 = (bf16[64,512]{1,0:T(8,128)(2,1)S(1)}, bf16[64,512]{1,0:T(8,128)(2,1)S(1)}, u32[]{:S(2)}, u32[]{:S(2)}) collective-permute-start(bf16[64,512]{1,0:T(8,128)(2,1)S(1)} %collective-permute-done.4), channel_id=1, source_target_pairs={{0,1},{1,0},{2,3},{3,2},{4,5},{5,4},{6,7},{7,6},{8,9},{9,8},{10,11... | collective-permute-start | bytes 196616 | tf_op jit(solution)/shard_map/ppermute | solution.py:417
  117.4 12.4 %collective-permute-start.20 = (bf16[32,512]{1,0:T(8,128)(2,1)S(1)}, bf16[32,512]{1,0:T(8,128)(2,1)S(1)}, u32[]{:S(2)}, u32[]{:S(2)}) collective-permute-start(bf16[32,512]{1,0:T(8,128)(2,1)S(1)} %get-tuple-element.22), channel_id=1, source_target_pairs={{0,62},{1,63},{2,0},{3,1},{4,2},{5,3},{6,4},{7,5},{8,6},{9,7},{10,... | collective-permute-start | bytes 98312 | tf_op jit(solution)/shard_map/ppermute | solution.py:508
  124.5 5.3 %collective-permute-start.19 = (bf16[32,512]{1,0:T(8,128)(2,1)S(1)}, bf16[32,512]{1,0:T(8,128)(2,1)S(1)}, u32[]{:S(2)}, u32[]{:S(2)}) collective-permute-start(bf16[32,512]{1,0:T(8,128)(2,1)S(1)} %get-tuple-element.22), channel_id=1, source_target_pairs={{0,63},{1,0},{2,1},{3,2},{4,3},{5,4},{6,5},{7,6},{8,7},{9,8},{10,9... | collective-permute-start | bytes 98312 | tf_op jit(solution)/shard_map/ppermute | solution.py:508
  124.5 5.3 %collective-permute-start.18 = (bf16[32,512]{1,0:T(8,128)(2,1)S(1)}, bf16[32,512]{1,0:T(8,128)(2,1)S(1)}, u32[]{:S(2)}, u32[]{:S(2)}) collective-permute-start(bf16[32,512]{1,0:T(8,128)(2,1)S(1)} %get-tuple-element.22), channel_id=1, source_target_pairs={{0,1},{1,2},{2,3},{3,4},{4,5},{5,6},{6,7},{7,8},{8,9},{9,10},{10,1... | collective-permute-start | bytes 98312 | tf_op jit(solution)/shard_map/ppermute | solution.py:508
  125.0 5.4 %collective-permute-start.17 = (bf16[32,512]{1,0:T(8,128)(2,1)S(1)}, bf16[32,512]{1,0:T(8,128)(2,1)S(1)}, u32[]{:S(2)}, u32[]{:S(2)}) collective-permute-start(bf16[32,512]{1,0:T(8,128)(2,1)S(1)} %get-tuple-element.22), channel_id=1, source_target_pairs={{0,2},{1,3},{2,4},{3,5},{4,6},{5,7},{6,8},{7,9},{8,10},{9,11},{10,... | collective-permute-start | bytes 98312 | tf_op jit(solution)/shard_map/ppermute | solution.py:508
where the time goes:
time: 140 us; the launch traced here: 138 us
  waiting for transfers between devices  65.1 us (46%)
  Pallas kernels  52.1 us (37%)
  starting transfers between devices  18.7 us (13%)
  between operations  1.41 us (1%)
    ppermute x8, waiting for transfers between devices, shift(): return lax.ppermute(v, REGION, along(steps))  62.5 us
    pallas_call x9, Pallas kernels, call(): pl.pallas_call(body, grid=grid, in_specs=[i[1] for i in ins], out_specs=[...  52.1 us
    ppermute x4, starting transfers between devices, local(): lax.ppermute(published, REGION, [(s, (s - offset) % regions) for s in ran...  8.61 us
    ppermute x8, starting transfers between devices, shift(): return lax.ppermute(v, REGION, along(steps))  6.7 us
    ppermute x9, starting transfers between devices, swap(): return lax.ppermute(v, 'core', [(0, 1), (1, 0)])  3.36 us
  transfers between devices with their start and end apart: 21, of which 9 were waited for; matrix products, arithmetic and copies ran while one was open for 1% of the time, Pallas kernels for 26%

commit v1 on v0

--- a/solution.py
+++ b/solution.py
@@ -14,12 +14,15 @@
 F32 = jnp.float32
 I32 = jnp.int32
 HBM = pltpu.MemorySpace.HBM
+VMEM = pltpu.MemorySpace.VMEM
 SEED = 12
 LEAD = 3
 STEPS = 4
+AHEAD_FAR = 6
+AHEAD_GRID = 7
 BLOCK = 512
 GRID_BLOCK = 384
-LIMIT = 36 * 2**20
+LIMIT = 24 * 2**20
 
 
 def iota(shape, dim):
@@ -66,7 +69,7 @@
 
 def call(body, grid, ins, outs, scratch=(), flops=0, nbytes=0):
     place = lambda a, s, *near: a if near or s.memory_space not in (None, HBM) else pltpu.with_memory_space_constraint(a, HBM)
-    result = lambda s, d, p, *far: HBM(s, d) if far or p.memory_space == HBM else jax.ShapeDtypeStruct(s, d)
+    result = lambda s, d, p, *at: at[0](s, d) if at else HBM(s, d) if p.memory_space == HBM else jax.ShapeDtypeStruct(s, d)
     return pl.pallas_call(
         body,
         grid=grid,
@@ -141,7 +144,8 @@
 
 
 def main_body(chips, first, place, live, sender, sender_row, receiver_row, need, w_s, both, up, down, edges, before, bias, w_out,
-              gain, start, ready, totals, table):
+              gain, ready, *refs):
+    totals, table = refs[-2:]
     z, c = place[0], place[1]
     n, _ = totals.shape
     step = pl.program_id(0)
@@ -151,7 +155,7 @@
 
     @pl.when(step == 0)
     def _():
-        totals[...] = start[...]
+        totals[...] = refs[0][...] if first else jnp.zeros_like(totals)
         r = iota((6 * pair, regions), 0)
         near = r // (2 * pair)
         half = (r // pair) % 2
@@ -182,6 +186,13 @@
     totals[...] += dot(ones_where(iota((n, rows), 0) == target), message)
 
 
+def ahead_of(sources, targets, sems):
+    copies = [pltpu.make_async_copy(a.at[pl.ds(0, b.shape[0]), :], b, sems.at[i]) for i, (a, b) in enumerate(zip(sources, targets))]
+    for copy in copies:
+        copy.start()
+    return copies
+
+
 def gathered(at, sources, starts):
     out = None
     for source, start in zip(sources, starts):
@@ -192,9 +203,12 @@
 
 
 def compact_body(chips, offered, starts, place, live, sender, receiver, need, w_in, table_r, edges, *refs):
-    sources = refs[: len(starts)]
-    outs, count, kept, sems = refs[len(starts) : len(starts) + 5], refs[len(starts) + 5], refs[-6:-1], refs[-1]
+    k, m = len(starts), AHEAD_FAR
+    sources, ahead = refs[:k], refs[k : k + m]
+    outs, count, near = refs[k + m : k + m + 5], refs[k + m + 5], refs[k + m + 6 : k + 2 * m + 6]
+    kept, sems, ahead_sems = refs[-7:-2], refs[-2], refs[-1]
     pre, rows, source_rows, at_out, target_out = kept
+    fetches = ahead_of(ahead, near, ahead_sems)
     z, c = place[0], place[1]
     groups = sender.shape[0]
     n, f = table_r.shape
@@ -246,24 +260,18 @@
         return carry
 
     lax.fori_loop(0, blocks, one, 0)
-
-
-def far_body(starts, count, nodes, boundary, totals, bias, gain, node_bias, node_gain, *refs):
-    k = len(starts)
-    sources = refs[:k]
-    stored = refs[k : k + 5]
-    (w_s_hbm, w_out_hbm, node_in_hbm, node_out_hbm, result, kept_result, published, acc, w_s, w_out, node_in, node_out, sems) = refs[k + 5 : -6]
-    kept, late_sems = refs[-6:-1], refs[-1]
+    for fetch in fetches:
+        fetch.wait()
+
+
+def far_body(starts, count, nodes, boundary, totals, bias, gain, node_bias, node_gain, w_s, w_out, node_in, node_out, *refs):
+    k, m = len(starts), AHEAD_GRID
+    sources, stored, ahead = refs[:k], refs[k : k + 5], refs[k + 5 : k + 5 + m]
+    result, kept_result, published = refs[k + 5 + m : k + 8 + m]
+    near, acc = refs[k + 8 + m : k + 8 + 2 * m], refs[k + 8 + 2 * m]
+    kept, late_sems, ahead_sems = refs[-7:-2], refs[-2], refs[-1]
     pre, rows, source_rows, at, target = kept
     n, f = nodes.shape
-    copies = [
-        pltpu.make_async_copy(w_s_hbm.at[pl.ds(0, f), :], w_s, sems.at[0]),
-        pltpu.make_async_copy(w_out_hbm, w_out, sems.at[1]),
-        pltpu.make_async_copy(node_in_hbm, node_in, sems.at[2]),
-        pltpu.make_async_copy(node_out_hbm, node_out, sems.at[3]),
-    ]
-    for copy in copies:
-        copy.start()
 
     def fetch(block, begin):
         lines = pl.ds(pl.multiple_of(block * 128, 128), 128)
@@ -275,9 +283,8 @@
     def _():
         fetch(0, True)
 
+    fetches = ahead_of(ahead, near, ahead_sems)
     acc[...] = totals[...]
-    copies[0].wait()
-    copies[1].wait()
 
     def one(block, carry):
         fetch(block, False)
@@ -295,8 +302,6 @@
         return carry
 
     lax.fori_loop(0, count[0], one, 0)
-    copies[2].wait()
-    copies[3].wait()
     pre_node = dot(nodes[...], node_in[0:f, :]) + dot(acc[...].astype(BF), node_in[f : 2 * f, :])
     update = finish(pre_node, node_bias[...], node_out[...], node_gain[...])
     value = (nodes[...].astype(F32) + update).astype(BF)
@@ -304,6 +309,8 @@
     kept_result[...] = value
     hot = ones_where(iota((n, boundary.shape[1]), 0) == boundary[...])
     published[...] = dot_t(hot, value).astype(BF)
+    for copy in fetches:
+        copy.wait()
 
 
 def grid_local_body(sender, mesh_out, w_s, before, out, table):
@@ -439,12 +446,11 @@
         before_body, (mesh_steps,),
         [(as_blocks(mesh_sender, BLOCK), idx_spec(BLOCK)), (as_blocks(mesh_receiver, BLOCK), idx_spec(BLOCK)), full(mesh_nodes),
          full(process_edge_in), (mesh_edges, tile(BLOCK)), (lead[1], anywhere)],
-        [((edges, f), F32, tile(BLOCK), True), ((n, f), BF, whole((n, f)))],
+        [((edges, f), F32, tile(BLOCK), HBM), ((n, f), BF, whole((n, f)))],
         [pltpu.VMEM((n, f), BF)],
         flops=2 * f * f * (edges * 3 + 2 * n), nbytes=6 * edges * f,
     )
     halves = mesh_steps // 2
-    totals = jnp.zeros((n, f), F32)
     ready = lead[2]
     current = jnp.concatenate([lead[3], seed, seed_back], axis=0)
     chain, turned = [current], []
@@ -460,9 +466,9 @@
             [(place, smem), (mesh_live, smem), (as_blocks(mesh_sender, BLOCK), at((BLOCK // 128, 128), 2)),
              (as_rows(mesh_sender, BLOCK), at((1, BLOCK), 2)), (as_rows(mesh_receiver, BLOCK), at((1, BLOCK), 2)), full(need),
              (process_edge_in, whole((f, f))), held(lead[0]), held(lead[1]), held(back[1]), (mesh_edges, moved),
-             (before, moved), full(row(process_edge_bias)), full(process_edge_out), full(row(process_edge_gain)), full(totals),
-             (ready, anywhere)],
-            [((n, f), F32, whole((n, f)), True)],
+             (before, moved), full(row(process_edge_bias)), full(process_edge_out), full(row(process_edge_gain)),
+             (ready, anywhere)] + ([full(totals)] if part else []),
+            [((n, f), F32, whole((n, f)), HBM)],
             [pltpu.VMEM((6 * pair, f), BF)],
             flops=2 * f * f * halves * BLOCK * 2, nbytes=6 * halves * BLOCK * f,
         )
@@ -471,7 +477,7 @@
         grid_before_body, (grid_steps,),
         [(as_rows(grid_receiver, GRID_BLOCK), row_spec(GRID_BLOCK)), full(grid_nodes), full(decode_edge_in),
          (grid_edges, tile(GRID_BLOCK)), (chain[1], anywhere)],
-        [((grid_e, f), F32, tile(GRID_BLOCK), True)],
+        [((grid_e, f), F32, tile(GRID_BLOCK), HBM)],
         [pltpu.VMEM((grid_n, f), BF)],
         flops=2 * f * f * (grid_e * 2 + grid_n), nbytes=6 * grid_e * f,
     )
@@ -484,23 +490,27 @@
     early = [i for i in range(len(far)) if i not in last]
     late_buffers = [pltpu.VMEM((128, f), F32), pltpu.VMEM((128, f), BF), pltpu.VMEM((128, f), BF), pltpu.VMEM((128, 128), I32),
                     pltpu.VMEM((128, 128), I32)]
-    pre, rows, source_rows, at, target, count = call(
+    vmem = lambda v: ((f if v is process_edge_in or v is decode_edge_in else v.shape[0], f), v.dtype, pl.BlockSpec(memory_space=VMEM), VMEM)
+    far_needs = [mesh_nodes, totals, process_edge_in, process_edge_out, process_node_in, process_node_out]
+    grid_needs = [grid_before, decode_edge_in, grid_nodes, grid_edges, decode_edge_out, decode_node_in, decode_node_out]
+    *stored, count, nodes_near, totals_near, head_near, out_near, node_in_near, node_out_near = call(
         functools.partial(compact_body, chips, offered, tuple(starts[i] for i in early)), (1,),
         [(place, smem), (mesh_live, smem), full(send_rows), full(receive_rows), full(need), full(process_edge_in), held(table_r),
-         full(mesh_edges)] + [held(far[i]) for i in early],
+         full(mesh_edges)] + [held(far[i]) for i in early] + [(v, hbm) for v in far_needs],
         [((edges, f), F32, hbm), ((edges, f), BF, hbm), ((edges, f), BF, hbm), ((edges, 128), I32, hbm),
-         ((edges, 128), I32, hbm), ((1,), I32, smem)],
-        late_buffers + [pltpu.SemaphoreType.DMA((5,))],
+         ((edges, 128), I32, hbm), ((1,), I32, smem)] + [vmem(v) for v in far_needs],
+        late_buffers + [pltpu.SemaphoreType.DMA((5,)), pltpu.SemaphoreType.DMA((AHEAD_FAR,))],
         flops=2 * f * 128 * (edges + 4 * f), nbytes=2 * edges * f,
     )
-    mesh_out, mesh_kept, published = call(
+    mesh_out, mesh_kept, published, grid_before, grid_head, nodes_g, edges_g, out_g, node_in_g, node_out_g = call(
         functools.partial(far_body, tuple(starts[i] for i in last)), (1,),
-        [(count, smem), full(mesh_nodes), full(boundary), full(totals), full(row(process_edge_bias)), full(row(process_edge_gain)),
-         full(row(process_node_bias)), full(row(process_node_gain))] + [held(far[i]) for i in last]
-        + [(v, hbm) for v in (pre, rows, source_rows, at, target)] + [(process_edge_in, hbm), (process_edge_out, hbm), (process_node_in, hbm), (process_node_out, hbm)],
-        [((n, f), BF, whole((n, f))), ((n, f), BF, whole((n, f))), ((offered, f), BF, whole((offered, f)))],
-        [pltpu.VMEM((n, f), F32), pltpu.VMEM((f, f), BF), pltpu.VMEM((f, f), BF), pltpu.VMEM((2 * f, f), BF), pltpu.VMEM((f, f), BF),
-         pltpu.SemaphoreType.DMA((4,))] + late_buffers + [pltpu.SemaphoreType.DMA((5,))],
+        [(count, smem), held(nodes_near), full(boundary), held(totals_near), full(row(process_edge_bias)),
+         full(row(process_edge_gain)), full(row(process_node_bias)), full(row(process_node_gain)), held(head_near), held(out_near),
+         held(node_in_near), held(node_out_near)] + [held(far[i]) for i in last] + [(v, hbm) for v in stored]
+        + [(v, hbm) for v in grid_needs],
+        [((n, f), BF, whole((n, f))), ((n, f), BF, whole((n, f)), VMEM), ((offered, f), BF, whole((offered, f)), VMEM)]
+        + [vmem(v) for v in grid_needs],
+        [pltpu.VMEM((n, f), F32)] + late_buffers + [pltpu.SemaphoreType.DMA((5,)), pltpu.SemaphoreType.DMA((AHEAD_GRID,))],
         flops=2 * f * f * 4 * n, nbytes=8 * n * f,
     )
     pieces = []
@@ -508,9 +518,9 @@
         pieces.append(lax.ppermute(published, REGION, [(s, (s - offset) % regions) for s in range(regions)]))
     (grid_local,) = call(
         grid_local_body, (grid_steps,),
-        [(as_rows(grid_sender, GRID_BLOCK), row_spec(GRID_BLOCK)), held(mesh_kept), (decode_edge_in, whole((f, f))),
-         (grid_before, tile(GRID_BLOCK))],
-        [((grid_e, f), F32, tile(GRID_BLOCK))],
+        [(as_rows(grid_sender, GRID_BLOCK), row_spec(GRID_BLOCK)), held(mesh_kept), held(grid_head),
+         (grid_before, tile(GRID_BLOCK), True)],
+        [((grid_e, f), F32, tile(GRID_BLOCK), VMEM)],
         [pltpu.VMEM((n, f), BF)],
         flops=2 * f * f * (grid_e + n), nbytes=8 * grid_e * f,
     )
@@ -518,9 +528,9 @@
         functools.partial(grid_body, n, pair), (grid_steps,),
         [(as_rows(grid_sender, GRID_BLOCK), row_spec(GRID_BLOCK)), (as_rows(grid_receiver, GRID_BLOCK), row_spec(GRID_BLOCK)),
          full(grid_need[0]), held(pieces[0]), held(pieces[1]), held(pieces[2]), held(pieces[3]),
-         (decode_edge_in, whole((f, f))), full(grid_nodes), (grid_edges, tile(GRID_BLOCK)), (grid_local, tile(GRID_BLOCK), True),
-         full(row(decode_edge_bias)), full(decode_edge_out), full(row(decode_edge_gain)), full(decode_node_in),
-         full(row(decode_node_bias)), full(decode_node_out), full(row(decode_node_gain))],
+         held(grid_head), held(nodes_g), (edges_g, tile(GRID_BLOCK), True), (grid_local, tile(GRID_BLOCK), True),
+         full(row(decode_edge_bias)), held(out_g), full(row(decode_edge_gain)), held(node_in_g),
+         full(row(decode_node_bias)), held(node_out_g), full(row(decode_node_gain))],
         [((grid_n, f), BF, whole((grid_n, f)))],
         [pltpu.VMEM((grid_n, f), F32), pltpu.VMEM((4 * pair, f), BF)],
         flops=2 * f * f * (grid_e * 2 + 3 * grid_n), nbytes=6 * grid_e * f,

time: 140 us -> 138 us (0.986)
  Pallas kernels: 52.1 us -> 50 us
    pallas_call x9, Pallas kernels: 52.1 us -> 50 us  [call(): pl.pallas_call(body, grid=grid, in_specs=[i[1] for i in ins], out_specs=[...]
  transfers between devices with their start and end apart: 21 -> 21, of which waited for: 9 -> 10; matrix products, arithmetic and copies ran while one was open for 1% -> 0% of each run, Pallas kernels for 26% -> 25%
where the time goes in v1:
time: 138 us; the launch traced here: 136 us
  waiting for transfers between devices  66.2 us (48%)
  Pallas kernels  50 us (36%)
  starting transfers between devices  18.5 us (13%)
  between operations  1.41 us (1%)
    ppermute x8, waiting for transfers between devices, shift(): return lax.ppermute(v, REGION, along(steps))  62.5 us
    pallas_call x9, Pallas kernels, call(): pl.pallas_call(body, grid=grid, in_specs=[i[1] for i in ins], out_specs=[...  50 us
    ppermute x4, starting transfers between devices, local(): lax.ppermute(published, REGION, [(s, (s - offset) % regions) for s in ran...  8.42 us
    ppermute x8, starting transfers between devices, shift(): return lax.ppermute(v, REGION, along(steps))  6.7 us
    ppermute x9, starting transfers between devices, swap(): return lax.ppermute(v, 'core', [(0, 1), (1, 0)])  3.35 us
  transfers between devices with their start and end apart: 21, of which 10 were waited for; matrix products, arithmetic and copies ran while one was open for 0% of the time, Pallas kernels for 25%

profile of v1, /device:TPU:44, one launch (start us, length us, event | category | flops | bytes accessed | tf_op | source)
XLA Modules:
  0.0 136.2 jit_solution(3256239592601821136)
XLA Ops:
  0.6 1.3 shard_map.275
  2.1 1.2 collective-permute-done
  3.3 2.1 %collective-permute-start.1 = (bf16[64,512]{1,0:T(8,128)(2,1)S(1)}, bf16[64,512]{1,0:T(8,128)(2,1)S(1)}, u32[]{:S(2)}, u32[]{:S(2)}) collective-permute-start(bf16[64,512]{1,0:T(8,128)(2,1)S(1)} %pad_maximum_fusion.both), channel_id=1, source_target_pairs={{0,2},{1,63},{2,4},{3,1},{4,6},{5,3},{6,8},{7,5},{8,10},{9,7},{10,... | collective-permute-start | bytes 196616 | tf_op jit(solution)/shard_map/ppermute | solution.py:421
  5.4 23.2 %collective-permute-done.1.ready.up = bf16[64,512]{1,0:T(8,128)(2,1)S(1)} collective-permute-done((bf16[64,512]{1,0:T(8,128)(2,1)S(1)}, bf16[64,512]{1,0:T(8,128)(2,1)S(1)}, u32[]{:S(2)}, u32[]{:S(2)}) %collective-permute-start.1) | collective-permute-done | bytes 65568 | tf_op jit(solution)/shard_map/ppermute | solution.py:421
  28.6 4.0 %collective-permute-start.5 = (bf16[64,512]{1,0:T(8,128)(2,1)S(1)}, bf16[64,512]{1,0:T(8,128)(2,1)S(1)}, u32[]{:S(2)}, u32[]{:S(2)}) collective-permute-start(bf16[64,512]{1,0:T(8,128)(2,1)S(1)} %pad_maximum_fusion.both), channel_id=1, source_target_pairs={{0,24},{1,41},{2,26},{3,43},{4,28},{5,45},{6,30},{7,47},{8,32},{9,... | collective-permute-start | bytes 196616 | tf_op jit(solution)/shard_map/ppermute | solution.py:421
  32.5 1.5 %collective-permute-done.2.ready.refs_0_ = bf16[64,512]{1,0:T(8,128)(2,1)S(1)} collective-permute-done((bf16[64,512]{1,0:T(8,128)(2,1)S(1)}, bf16[64,512]{1,0:T(8,128)(2,1)S(1)}, u32[]{:S(2)}, u32[]{:S(2)}) %collective-permute-start.2) | collective-permute-done | bytes 65568 | tf_op jit(solution)/shard_map/ppermute | solution.py:421
  34.7 11.8 %collective-permute-done.5 = bf16[64,512]{1,0:T(8,128)(2,1)S(1)} collective-permute-done((bf16[64,512]{1,0:T(8,128)(2,1)S(1)}, bf16[64,512]{1,0:T(8,128)(2,1)S(1)}, u32[]{:S(2)}, u32[]{:S(2)}) %collective-permute-start.5) | collective-permute-done | bytes 65568 | tf_op jit(solution)/shard_map/ppermute | solution.py:421
  46.5 0.7 collective-permute-start.6
  47.2 0.9 collective-permute-done.6
  48.1 13.8 %collective-permute-done.7.refs_3_.ready = bf16[192,512]{1,0:T(8,128)(2,1)S(1)} collective-permute-done((bf16[192,512]{1,0:T(8,128)(2,1)S(1)}, bf16[192,512]{1,0:T(8,128)(2,1)S(1)}, u32[]{:S(2)}, u32[]{:S(2)}) %collective-permute-start.7) | collective-permute-done | bytes 196640 | tf_op jit(solution)/shard_map/ppermute | solution.py:421
  61.9 6.9 %collective-permute-done.8.refs_4_ = bf16[192,512]{1,0:T(8,128)(2,1)S(1)} collective-permute-done((bf16[192,512]{1,0:T(8,128)(2,1)S(1)}, bf16[192,512]{1,0:T(8,128)(2,1)S(1)}, u32[]{:S(2)}, u32[]{:S(2)}) %collective-permute-start.8) | collective-permute-done | bytes 196640 | tf_op jit(solution)/shard_map/ppermute | solution.py:421
  69.5 0.9 collective-permute-start.13
  70.4 5.3 %collective-permute-done.9.refs_5_ = bf16[192,512]{1,0:T(8,128)(2,1)S(1)} collective-permute-done((bf16[192,512]{1,0:T(8,128)(2,1)S(1)}, bf16[192,512]{1,0:T(8,128)(2,1)S(1)}, u32[]{:S(2)}, u32[]{:S(2)}) %collective-permute-start.9) | collective-permute-done | bytes 196640 | tf_op jit(solution)/shard_map/ppermute | solution.py:421
  75.6 8.1 %shard_map.276 = (f32[2048,512]{1,0:T(8,128)}, bf16[512,512]{1,0:T(8,128)(2,1)S(1)}) custom-call(s32[4,4,128]{2,1,0:T(4,128)} %bitcast.22, s32[4,4,128]{2,1,0:T(4,128)} %bitcast.28, bf16[512,512]{1,0:T(8,128)(2,1)} %refs_9_.2, bf16[1536,512]{1,0:T(8,128)(2,1)} %refs_11_.2, bf16[2048,512]{1,0:T(8,128)(2,1)} %edges.8, ...), custom_call_target="tpu_custom_call" | custom-call | flops 3758096384 | bytes 6291456 | tf_op jit(solution)/shard_map/pallas_call | solution.py:73
  83.8 6.0 %shard_map.277.refs_0_ = f32[512,512]{1,0:T(8,128)} custom-call(s32[2]{0:T(128)S(1)} %pad_add_fusion.place, s32[1]{0:T(128)S(6)} %copy.32.live, s32[4,4,128]{2,1,0:T(4,128)} %bitcast.23, s32[4,1,512]{2,1,0:T(1,128)} %bitcast.24, s32[4,1,512]{2,1,0:T(1,128)} %bitcast.29, s32[8,64]{1,0:T(8,128)} %bitcast.32, bf16[1536,512]{1,0:T(8,128)(2,1)} %refs_11_.2, ...), custom_call_target="tpu_custom_call" | custom-call | flops 1073741824 | bytes 3145728 | tf_op jit(solution)/shard_map/pallas_call | solution.py:73
  90.9 6.5 %shard_map.278.refs_10_ = f32[512,512]{1,0:T(8,128)} custom-call(s32[2]{0:T(128)S(1)} %pad_add_fusion.place, s32[1]{0:T(128)S(6)} %copy.32.live, s32[4,4,128]{2,1,0:T(4,128)} %bitcast.25, s32[4,1,512]{2,1,0:T(1,128)} %bitcast.26, s32[4,1,512]{2,1,0:T(1,128)} %bitcast.30, s32[8,64]{1,0:T(8,128)} %bitcast.33, bf16[1536,512]{1,0:T(8,128)(2,1)} %refs_11_.2, ...), custom_call_target="tpu_custom_call" | custom-call | flops 1073741824 | bytes 3145728 | tf_op jit(solution)/shard_map/pallas_call | solution.py:73
  98.0 5.5 %shard_map.280.refs_8_ = f32[1152,512]{1,0:T(8,128)} custom-call(s32[3,1,384]{2,1,0:T(1,128)} %bitcast.35, bf16[384,512]{1,0:T(8,128)(2,1)} %refs_10_.1, bf16[1536,512]{1,0:T(8,128)(2,1)} %refs_9_.3, bf16[1152,512]{1,0:T(8,128)(2,1)} %refs_11_.3, bf16[192,512]{1,0:T(8,128)(2,1)S(1)} %collective-permute-done.7.refs_3_.ready), custom_call_target="tpu_custom_call" | custom-call | flops 1409286144 | bytes 3538944 | tf_op jit(solution)/shard_map/pallas_call | solution.py:73
  103.5 5.1 %shard_map.279 = (f32[2048,512]{1,0:T(8,128)}, bf16[2048,512]{1,0:T(8,128)(2,1)}, bf16[2048,512]{1,0:T(8,128)(2,1)}, s32[2048,128]{1,0:T(8,128)}, s32[2048,128]{...) custom-call(s32[2]{0:T(128)S(1)} %pad_add_fusion.place, ...), custom_call_target="tpu_custom_call" | custom-call | flops 536870912 | bytes 2097152 | tf_op jit(solution)/shard_map/pallas_call | solution.py:73
  108.7 7.8 %shard_map.281 = (bf16[512,512]{1,0:T(8,128)(2,1)}, bf16[512,512]{1,0:T(8,128)(2,1)S(1)}, bf16[32,512]{1,0:T(8,128)(2,1)S(1)}, f32[1152,512]{1,0:T(8,128)S(1)}, ...) custom-call(s32[1]{0:T(128)} %get-tuple-element.28.count, ...), custom_call_target="tpu_custom_call" | custom-call | flops 1073741824 | bytes 2097152 | tf_op jit(solution)/shard_map/pallas_call | solution.py:73
  116.5 7.0 %collective-permute-start.20 = (bf16[32,512]{1,0:T(8,128)(2,1)S(1)}, bf16[32,512]{1,0:T(8,128)(2,1)S(1)}, u32[]{:S(2)}, u32[]{:S(2)}) collective-permute-start(bf16[32,512]{1,0:T(8,128)(2,1)S(1)} %get-tuple-element.41), channel_id=1, source_target_pairs={{0,62},{1,63},{2,0},{3,1},{4,2},{5,3},{6,4},{7,5},{8,6},{9,7},{10,... | collective-permute-start | bytes 98312 | tf_op jit(solution)/shard_map/ppermute | solution.py:518
  124.0 1.0 collective-permute-start.17
  124.9 2.7 %shard_map.282.before = f32[1152,512]{1,0:T(8,128)S(1)} custom-call(s32[3,1,384]{2,1,0:T(1,128)} %bitcast.37, bf16[512,512]{1,0:T(8,128)(2,1)S(1)} %get-tuple-element.45.mesh_out, bf16[512,512]{1,0:T(8,128)(2,1)S(1)} %get-tuple-element.42.w_s, f32[1152,512]{1,0:T(8,128)S(1)} %get-tuple-element.46.before), custom_call_target="tpu_custom_call" | custom-call | flops 872415232 | bytes 4718592 | tf_op jit(solution)/shard_map/pallas_call | solution.py:73
  128.0 1.3 collective-permute-done.17.a
  129.3 6.8 %shard_map.283 = bf16[384,512]{1,0:T(8,128)(2,1)} custom-call(s32[3,1,384]{2,1,0:T(1,128)} %bitcast.38, s32[3,1,384]{2,1,0:T(1,128)} %bitcast.36, s32[4,8]{1,0:T(4,128)} %bitcast.45, bf16[32,512]{1,0:T(8,128)(2,1)S(1)} %collective-permute-done.17.a, bf16[32,512]{1,0:T(8,128)(2,1)S(1)} %collective-permute-done.18.b, ...), custom_call_target="tpu_custom_call" | custom-call | flops 1811939328 | bytes 3538944 | tf_op jit(solution)/shard_map/pallas_call | solution.py:73
  (32 shorter events, 3.4 us)
Async XLA Ops:
  1.9 1.3 collective-permute-start
  3.3 25.3 %collective-permute-start.1 = (bf16[64,512]{1,0:T(8,128)(2,1)S(1)}, bf16[64,512]{1,0:T(8,128)(2,1)S(1)}, u32[]{:S(2)}, u32[]{:S(2)}) collective-permute-start(bf16[64,512]{1,0:T(8,128)(2,1)S(1)} %pad_maximum_fusion.both), channel_id=1, source_target_pairs={{0,2},{1,63},{2,4},{3,1},{4,6},{5,3},{6,8},{7,5},{8,10},{9,7},{10,... | collective-permute-start | bytes 196616 | tf_op jit(solution)/shard_map/ppermute | solution.py:421
  28.6 5.5 %collective-permute-start.2 = (bf16[64,512]{1,0:T(8,128)(2,1)S(1)}, bf16[64,512]{1,0:T(8,128)(2,1)S(1)}, u32[]{:S(2)}, u32[]{:S(2)}) collective-permute-start(bf16[64,512]{1,0:T(8,128)(2,1)S(1)} %collective-permute-done.1.ready.up), channel_id=1, source_target_pairs={{0,2},{1,63},{2,4},{3,1},{4,6},{5,3},{6,8},{7,5},{8,10},{9,7},{10,... | collective-permute-start | bytes 196616 | tf_op jit(solution)/shard_map/ppermute | solution.py:421
  28.6 17.9 %collective-permute-start.5 = (bf16[64,512]{1,0:T(8,128)(2,1)S(1)}, bf16[64,512]{1,0:T(8,128)(2,1)S(1)}, u32[]{:S(2)}, u32[]{:S(2)}) collective-permute-start(bf16[64,512]{1,0:T(8,128)(2,1)S(1)} %pad_maximum_fusion.both), channel_id=1, source_target_pairs={{0,24},{1,41},{2,26},{3,43},{4,28},{5,45},{6,30},{7,47},{8,32},{9,... | collective-permute-start | bytes 196616 | tf_op jit(solution)/shard_map/ppermute | solution.py:421
  34.0 13.1 %collective-permute-start.4 = (bf16[64,512]{1,0:T(8,128)(2,1)S(1)}, bf16[64,512]{1,0:T(8,128)(2,1)S(1)}, u32[]{:S(2)}, u32[]{:S(2)}) collective-permute-start(bf16[64,512]{1,0:T(8,128)(2,1)S(1)} %collective-permute-done.2.ready.refs_0_), channel_id=1, source_target_pairs={{0,2},{1,63},{2,4},{3,1},{4,6},{5,3},{6,8},{7,5},{8,10},{9,7},{10,... | collective-permute-start | bytes 196616 | tf_op jit(solution)/shard_map/ppermute | solution.py:421
  46.5 1.6 %collective-permute-start.6 = (bf16[64,512]{1,0:T(8,128)(2,1)S(1)}, bf16[64,512]{1,0:T(8,128)(2,1)S(1)}, u32[]{:S(2)}, u32[]{:S(2)}) collective-permute-start(bf16[64,512]{1,0:T(8,128)(2,1)S(1)} %collective-permute-done.5), channel_id=1, source_target_pairs={{0,1},{1,0},{2,3},{3,2},{4,5},{5,4},{6,7},{7,6},{8,9},{9,8},{10,11... | collective-permute-start | bytes 196616 | tf_op jit(solution)/shard_map/ppermute | solution.py:424
  48.1 13.8 %collective-permute-start.7 = (bf16[192,512]{1,0:T(8,128)(2,1)S(1)}, bf16[192,512]{1,0:T(8,128)(2,1)S(1)}, u32[]{:S(2)}, u32[]{:S(2)}) collective-permute-start(bf16[192,512]{1,0:T(8,128)(2,1)S(1)} %constant_dynamic-update-slice_fusion.ready.refs_2_), channel_id=1, source_target_pairs={{0,2},{1,63},{2,4},{3,1},{4,6},{5,3},{6,8},{7,5},{8,10},{9,7},{10,... | collective-permute-start | bytes 589832 | tf_op jit(solution)/shard_map/ppermute | solution.py:421
  61.9 6.9 %collective-permute-start.8 = (bf16[192,512]{1,0:T(8,128)(2,1)S(1)}, bf16[192,512]{1,0:T(8,128)(2,1)S(1)}, u32[]{:S(2)}, u32[]{:S(2)}) collective-permute-start(bf16[192,512]{1,0:T(8,128)(2,1)S(1)} %collective-permute-done.7.refs_3_.ready), channel_id=1, source_target_pairs={{0,2},{1,63},{2,4},{3,1},{4,6},{5,3},{6,8},{7,5},{8,10},{9,7},{10,... | collective-permute-start | bytes 589832 | tf_op jit(solution)/shard_map/ppermute | solution.py:421
  68.8 6.9 %collective-permute-start.9 = (bf16[192,512]{1,0:T(8,128)(2,1)S(1)}, bf16[192,512]{1,0:T(8,128)(2,1)S(1)}, u32[]{:S(2)}, u32[]{:S(2)}) collective-permute-start(bf16[192,512]{1,0:T(8,128)(2,1)S(1)} %collective-permute-done.8.refs_4_), channel_id=1, source_target_pairs={{0,2},{1,63},{2,4},{3,1},{4,6},{5,3},{6,8},{7,5},{8,10},{9,7},{10,... | collective-permute-start | bytes 589832 | tf_op jit(solution)/shard_map/ppermute | solution.py:421
  69.5 14.3 %collective-permute-start.13 = (bf16[64,512]{1,0:T(8,128)(2,1)S(1)}, bf16[64,512]{1,0:T(8,128)(2,1)S(1)}, u32[]{:S(2)}, u32[]{:S(2)}) collective-permute-start(bf16[64,512]{1,0:T(8,128)(2,1)S(1)} %collective-permute-done.1.ready.up), channel_id=1, source_target_pairs={{0,1},{1,0},{2,3},{3,2},{4,5},{5,4},{6,7},{7,6},{8,9},{9,8},{10,11... | collective-permute-start | bytes 196616 | tf_op jit(solution)/shard_map/ppermute | solution.py:424
  75.6 15.2 %collective-permute-start.14 = (bf16[192,512]{1,0:T(8,128)(2,1)S(1)}, bf16[192,512]{1,0:T(8,128)(2,1)S(1)}, u32[]{:S(2)}, u32[]{:S(2)}) collective-permute-start(bf16[192,512]{1,0:T(8,128)(2,1)S(1)} %collective-permute-done.9.refs_5_), channel_id=1, source_target_pairs={{0,2},{1,63},{2,4},{3,1},{4,6},{5,3},{6,8},{7,5},{8,10},{9,7},{10,... | collective-permute-start | bytes 589832 | tf_op jit(solution)/shard_map/ppermute | solution.py:421
  83.8 13.7 %collective-permute-start.3 = (bf16[64,512]{1,0:T(8,128)(2,1)S(1)}, bf16[64,512]{1,0:T(8,128)(2,1)S(1)}, u32[]{:S(2)}, u32[]{:S(2)}) collective-permute-start(bf16[64,512]{1,0:T(8,128)(2,1)S(1)} %collective-permute-done.2.ready.refs_0_), channel_id=1, source_target_pairs={{0,1},{1,0},{2,3},{3,2},{4,5},{5,4},{6,7},{7,6},{8,9},{9,8},{10,11... | collective-permute-start | bytes 196616 | tf_op jit(solution)/shard_map/ppermute | solution.py:424
  89.8 13.7 %collective-permute-start.11 = (bf16[192,512]{1,0:T(8,128)(2,1)S(1)}, bf16[192,512]{1,0:T(8,128)(2,1)S(1)}, u32[]{:S(2)}, u32[]{:S(2)}) collective-permute-start(bf16[192,512]{1,0:T(8,128)(2,1)S(1)} %collective-permute-done.7.refs_3_.ready), channel_id=1, source_target_pairs={{0,1},{1,0},{2,3},{3,2},{4,5},{5,4},{6,7},{7,6},{8,9},{9,8},{10,11... | collective-permute-start | bytes 589832 | tf_op jit(solution)/shard_map/ppermute | solution.py:424
  90.3 13.2 %collective-permute-start.12 = (bf16[192,512]{1,0:T(8,128)(2,1)S(1)}, bf16[192,512]{1,0:T(8,128)(2,1)S(1)}, u32[]{:S(2)}, u32[]{:S(2)}) collective-permute-start(bf16[192,512]{1,0:T(8,128)(2,1)S(1)} %collective-permute-done.8.refs_4_), channel_id=1, source_target_pairs={{0,1},{1,0},{2,3},{3,2},{4,5},{5,4},{6,7},{7,6},{8,9},{9,8},{10,11... | collective-permute-start | bytes 589832 | tf_op jit(solution)/shard_map/ppermute | solution.py:424
  90.4 18.2 %collective-permute-start.15 = (bf16[192,512]{1,0:T(8,128)(2,1)S(1)}, bf16[192,512]{1,0:T(8,128)(2,1)S(1)}, u32[]{:S(2)}, u32[]{:S(2)}) collective-permute-start(bf16[192,512]{1,0:T(8,128)(2,1)S(1)} %collective-permute-done.9.refs_5_), channel_id=1, source_target_pairs={{0,1},{1,0},{2,3},{3,2},{4,5},{5,4},{6,7},{7,6},{8,9},{9,8},{10,11... | collective-permute-start | bytes 589832 | tf_op jit(solution)/shard_map/ppermute | solution.py:424
  90.8 17.9 %collective-permute-start.16 = (bf16[192,512]{1,0:T(8,128)(2,1)S(1)}, bf16[192,512]{1,0:T(8,128)(2,1)S(1)}, u32[]{:S(2)}, u32[]{:S(2)}) collective-permute-start(bf16[192,512]{1,0:T(8,128)(2,1)S(1)} %collective-permute-done.14.refs_0_), channel_id=1, source_target_pairs={{0,1},{1,0},{2,3},{3,2},{4,5},{5,4},{6,7},{7,6},{8,9},{9,8},{10,11... | collective-permute-start | bytes 589832 | tf_op jit(solution)/shard_map/ppermute | solution.py:424
  97.5 6.0 %collective-permute-start.10 = (bf16[64,512]{1,0:T(8,128)(2,1)S(1)}, bf16[64,512]{1,0:T(8,128)(2,1)S(1)}, u32[]{:S(2)}, u32[]{:S(2)}) collective-permute-start(bf16[64,512]{1,0:T(8,128)(2,1)S(1)} %collective-permute-done.4), channel_id=1, source_target_pairs={{0,1},{1,0},{2,3},{3,2},{4,5},{5,4},{6,7},{7,6},{8,9},{9,8},{10,11... | collective-permute-start | bytes 196616 | tf_op jit(solution)/shard_map/ppermute | solution.py:424
  116.5 11.1 %collective-permute-start.20 = (bf16[32,512]{1,0:T(8,128)(2,1)S(1)}, bf16[32,512]{1,0:T(8,128)(2,1)S(1)}, u32[]{:S(2)}, u32[]{:S(2)}) collective-permute-start(bf16[32,512]{1,0:T(8,128)(2,1)S(1)} %get-tuple-element.41), channel_id=1, source_target_pairs={{0,62},{1,63},{2,0},{3,1},{4,2},{5,3},{6,4},{7,5},{8,6},{9,7},{10,... | collective-permute-start | bytes 98312 | tf_op jit(solution)/shard_map/ppermute | solution.py:518
  123.5 4.2 %collective-permute-start.19 = (bf16[32,512]{1,0:T(8,128)(2,1)S(1)}, bf16[32,512]{1,0:T(8,128)(2,1)S(1)}, u32[]{:S(2)}, u32[]{:S(2)}) collective-permute-start(bf16[32,512]{1,0:T(8,128)(2,1)S(1)} %get-tuple-element.41), channel_id=1, source_target_pairs={{0,63},{1,0},{2,1},{3,2},{4,3},{5,4},{6,5},{7,6},{8,7},{9,8},{10,9... | collective-permute-start | bytes 98312 | tf_op jit(solution)/shard_map/ppermute | solution.py:518
  123.5 4.6 %collective-permute-start.18 = (bf16[32,512]{1,0:T(8,128)(2,1)S(1)}, bf16[32,512]{1,0:T(8,128)(2,1)S(1)}, u32[]{:S(2)}, u32[]{:S(2)}) collective-permute-start(bf16[32,512]{1,0:T(8,128)(2,1)S(1)} %get-tuple-element.41), channel_id=1, source_target_pairs={{0,1},{1,2},{2,3},{3,4},{4,5},{5,6},{6,7},{7,8},{8,9},{9,10},{10,1... | collective-permute-start | bytes 98312 | tf_op jit(solution)/shard_map/ppermute | solution.py:518
  124.0 5.4 %collective-permute-start.17 = (bf16[32,512]{1,0:T(8,128)(2,1)S(1)}, bf16[32,512]{1,0:T(8,128)(2,1)S(1)}, u32[]{:S(2)}, u32[]{:S(2)}) collective-permute-start(bf16[32,512]{1,0:T(8,128)(2,1)S(1)} %get-tuple-element.41), channel_id=1, source_target_pairs={{0,2},{1,3},{2,4},{3,5},{4,6},{5,7},{6,8},{7,9},{8,10},{9,11},{10,... | collective-permute-start | bytes 98312 | tf_op jit(solution)/shard_map/ppermute | solution.py:518

commit v2 on v1

--- a/solution.py
+++ b/solution.py
@@ -18,7 +18,9 @@
 SEED = 12
 LEAD = 3
 STEPS = 4
-AHEAD_FAR = 6
+LATE = 256
+AHEAD_MESH = 4
+AHEAD_FAR = 2
 AHEAD_GRID = 7
 BLOCK = 512
 GRID_BLOCK = 384
@@ -106,14 +108,22 @@
     out[...] = total
 
 
-def grid_before_body(receiver, nodes, w_in, edges, ready, out, table_r):
+def grid_before_body(receiver, nodes, w_in, edges, ready, *refs):
+    m = AHEAD_MESH
+    ahead, out, near, table_r, sems = refs[:m], refs[m], refs[m + 1 : 2 * m + 1], refs[-2], refs[-1]
     n, f = nodes.shape
 
     @pl.when(pl.program_id(0) == 0)
     def _():
+        ahead_of(ahead, near, sems)
         table_r[...] = dot(nodes[...], w_in[f : 2 * f, :]).astype(BF)
 
     out[...] = dot(edges[...], w_in[2 * f : 3 * f, :]) + dot(rows_hot(receiver[0], n), table_r[...])
+
+    @pl.when(pl.program_id(0) == pl.num_programs(0) - 1)
+    def _():
+        for copy in ahead_of(ahead, near, sems, False):
+            copy.wait()
 
 
 def pieces_of(chips, offered):
@@ -186,9 +196,9 @@
     totals[...] += dot(ones_where(iota((n, rows), 0) == target), message)
 
 
-def ahead_of(sources, targets, sems):
+def ahead_of(sources, targets, sems, begin=True):
     copies = [pltpu.make_async_copy(a.at[pl.ds(0, b.shape[0]), :], b, sems.at[i]) for i, (a, b) in enumerate(zip(sources, targets))]
-    for copy in copies:
+    for copy in copies if begin else ():
         copy.start()
     return copies
 
@@ -202,16 +212,16 @@
     return out
 
 
-def compact_body(chips, offered, starts, place, live, sender, receiver, need, w_in, table_r, edges, *refs):
+def compact_body(chips, offered, starts, place, live, sender, receiver, need, w_e, table_r, edges, *refs):
     k, m = len(starts), AHEAD_FAR
     sources, ahead = refs[:k], refs[k : k + m]
     outs, count, near = refs[k + m : k + m + 5], refs[k + m + 5], refs[k + m + 6 : k + 2 * m + 6]
-    kept, sems, ahead_sems = refs[-7:-2], refs[-2], refs[-1]
-    pre, rows, source_rows, at_out, target_out = kept
+    ahead_sems = refs[-1]
+    pre, rows, source_rows, at_out, target_out = outs
     fetches = ahead_of(ahead, near, ahead_sems)
     z, c = place[0], place[1]
     groups = sender.shape[0]
-    n, f = table_r.shape
+    n, _ = table_r.shape
     pair, regions = need.shape
     where_at = pieces_of(chips, offered)
     send = sender[...]
@@ -223,15 +233,15 @@
     above = jnp.sum(dot(ones_where(iota((groups, groups), 1) < iota((groups, groups), 0)), late_bits), axis=1, keepdims=True)
     rank = jnp.where(late, (within + above).astype(I32), -1)
     total = jnp.sum(jnp.where(late, 1, 0))
-    blocks = (total + 127) // 128
+    blocks = (total + LATE - 1) // LATE
     count[0] = blocks
 
     def one(block, carry):
-        base = pl.multiple_of(block * 128, 128)
-        lines = pl.ds(base, 128)
-        hot, send_at, receive_at = [], jnp.zeros((128, 128), I32), jnp.zeros((128, 128), I32)
+        base = pl.multiple_of(block * LATE, LATE)
+        lines = pl.ds(base, LATE)
+        hot, send_at, receive_at = [], jnp.zeros((LATE, 128), I32), jnp.zeros((LATE, 128), I32)
         for g in range(groups):
-            match = iota((128, 128), 0) + base == rank[g : g + 1, :]
+            match = iota((LATE, 128), 0) + base == rank[g : g + 1, :]
             hot.append(ones_where(match))
             send_at += jnp.where(match, send[g : g + 1, :] + 1, 0)
             receive_at += jnp.where(match, receiver[g : g + 1, :] + 1, 0)
@@ -239,24 +249,19 @@
         from_ = jnp.sum(send_at, axis=1, keepdims=True) - 1
         to = jnp.sum(receive_at, axis=1, keepdims=True) - 1
         valid, region, offset, half, slot = relative(from_, n, pair, chips, z, c)
-        wanted = lax.dot_general(ones_where(iota((128, regions), 1) == region), need[...].astype(F32).astype(BF),
+        wanted = lax.dot_general(ones_where(iota((LATE, regions), 1) == region), need[...].astype(F32).astype(BF),
                                  (((1,), (1,)), ((), ())), preferred_element_type=F32)
-        chosen = jnp.sum(jnp.where(iota((128, pair), 1) == slot, wanted, 0.0), axis=1, keepdims=True).astype(I32)
-        start, flip = jnp.zeros((128, 1), I32), jnp.zeros((128, 1), I32)
+        chosen = jnp.sum(jnp.where(iota((LATE, pair), 1) == slot, wanted, 0.0), axis=1, keepdims=True).astype(I32)
+        start, flip = jnp.zeros((LATE, 1), I32), jnp.zeros((LATE, 1), I32)
         for key, (row, turned) in where_at.items():
             start = jnp.where(offset == key, row, start)
             flip = jnp.where(offset == key, turned, flip)
         at = jnp.where(valid, start + jnp.where(flip == 1, 1 - half, half) * offered + chosen, -1)
-        rows[...] = edge
-        pre[...] = dot(edge, w_in[2 * f : 3 * f, :]) + dot(ones_where(iota((128, n), 1) == to), table_r[...])
-        source_rows[...] = gathered(at, sources, starts).astype(BF)
-        at_out[...] = jnp.broadcast_to(at, (128, 128))
-        target_out[...] = jnp.broadcast_to(to, (128, 128))
-        copies = [pltpu.make_async_copy(v, o.at[lines, :], sems.at[i]) for i, (v, o) in enumerate(zip(kept, outs))]
-        for copy in copies:
-            copy.start()
-        for copy in copies:
-            copy.wait()
+        rows[lines, :] = edge
+        pre[lines, :] = dot(edge, w_e[...]) + dot(ones_where(iota((LATE, n), 1) == to), table_r[...])
+        source_rows[lines, :] = gathered(at, sources, starts).astype(BF)
+        at_out[lines, :] = jnp.broadcast_to(at, (LATE, 128))
+        target_out[lines, :] = jnp.broadcast_to(to, (LATE, 128))
         return carry
 
     lax.fori_loop(0, blocks, one, 0)
@@ -266,39 +271,22 @@
 
 def far_body(starts, count, nodes, boundary, totals, bias, gain, node_bias, node_gain, w_s, w_out, node_in, node_out, *refs):
     k, m = len(starts), AHEAD_GRID
-    sources, stored, ahead = refs[:k], refs[k : k + 5], refs[k + 5 : k + 5 + m]
+    sources, (pre, rows, source_rows, at, target), ahead = refs[:k], refs[k : k + 5], refs[k + 5 : k + 5 + m]
     result, kept_result, published = refs[k + 5 + m : k + 8 + m]
-    near, acc = refs[k + 8 + m : k + 8 + 2 * m], refs[k + 8 + 2 * m]
-    kept, late_sems, ahead_sems = refs[-7:-2], refs[-2], refs[-1]
-    pre, rows, source_rows, at, target = kept
+    near, acc, ahead_sems = refs[k + 8 + m : k + 8 + 2 * m], refs[-2], refs[-1]
     n, f = nodes.shape
-
-    def fetch(block, begin):
-        lines = pl.ds(pl.multiple_of(block * 128, 128), 128)
-        for i, (v, o) in enumerate(zip(stored, kept)):
-            copy = pltpu.make_async_copy(v.at[lines, :], o, late_sems.at[i])
-            copy.start() if begin else copy.wait()
-
-    @pl.when(count[0] > 0)
-    def _():
-        fetch(0, True)
-
     fetches = ahead_of(ahead, near, ahead_sems)
     acc[...] = totals[...]
 
     def one(block, carry):
-        fetch(block, False)
-        source = (source_rows[...].astype(F32) + gathered(at[...][:, 0:1], sources, starts)).astype(BF)
-        update = finish(pre[...] + dot(source, w_s[...]), bias[...], w_out[...], gain[...])
-        message = (rows[...].astype(F32) + update).astype(BF)
+        lines = pl.ds(pl.multiple_of(block * LATE, LATE), LATE)
+        source = (source_rows[lines, :].astype(F32) + gathered(at[lines, :][:, 0:1], sources, starts)).astype(BF)
+        update = finish(pre[lines, :] + dot(source, w_s[...]), bias[...], w_out[...], gain[...])
+        message = (rows[lines, :].astype(F32) + update).astype(BF)
         eye = iota((128, 128), 0) == iota((128, 128), 1)
-        to = jnp.sum(jnp.where(eye, target[...] + 1, 0), axis=0, keepdims=True) - 1
-        acc[...] += dot(ones_where(iota((n, 128), 0) == to), message)
-
-        @pl.when(block + 1 < count[0])
-        def _():
-            fetch(block + 1, True)
-
+        targets = target[lines, :] + 1
+        to = [jnp.sum(jnp.where(eye, targets[i : i + 128, :], 0), axis=0, keepdims=True) for i in range(0, LATE, 128)]
+        acc[...] += dot(ones_where(iota((n, LATE), 0) + 1 == jnp.concatenate(to, axis=1)), message)
         return carry
 
     lax.fori_loop(0, count[0], one, 0)
@@ -442,16 +430,26 @@
     for k in range(1, LEAD + 1):
         back.append(swap(lead[k]))
     seed_back = swap(seed)
+    vmem = lambda v: ((f if v is decode_edge_in else v.shape[0], f), v.dtype, pl.BlockSpec(memory_space=VMEM), VMEM)
+    mesh_needs = [process_edge_in, mesh_nodes, mesh_edges, process_edge_out]
+    grid_before, w_in_near, nodes_near, edges_near, out_near = call(
+        grid_before_body, (grid_steps,),
+        [(as_rows(grid_receiver, GRID_BLOCK), row_spec(GRID_BLOCK)), full(grid_nodes), full(decode_edge_in),
+         (grid_edges, tile(GRID_BLOCK)), (lead[1], anywhere)] + [(v, hbm) for v in mesh_needs],
+        [((grid_e, f), F32, tile(GRID_BLOCK), HBM)] + [vmem(v) for v in mesh_needs],
+        [pltpu.VMEM((grid_n, f), BF), pltpu.SemaphoreType.DMA((AHEAD_MESH,))],
+        flops=2 * f * f * (grid_e * 2 + grid_n), nbytes=6 * grid_e * f,
+    )
     before, table_r = call(
         before_body, (mesh_steps,),
-        [(as_blocks(mesh_sender, BLOCK), idx_spec(BLOCK)), (as_blocks(mesh_receiver, BLOCK), idx_spec(BLOCK)), full(mesh_nodes),
-         full(process_edge_in), (mesh_edges, tile(BLOCK)), (lead[1], anywhere)],
-        [((edges, f), F32, tile(BLOCK), HBM), ((n, f), BF, whole((n, f)))],
+        [(as_blocks(mesh_sender, BLOCK), idx_spec(BLOCK)), (as_blocks(mesh_receiver, BLOCK), idx_spec(BLOCK)), held(nodes_near),
+         held(w_in_near), (edges_near, tile(BLOCK), True), (lead[2], anywhere)],
+        [((edges, f), F32, tile(BLOCK), VMEM), ((n, f), BF, whole((n, f)), VMEM)],
         [pltpu.VMEM((n, f), BF)],
         flops=2 * f * f * (edges * 3 + 2 * n), nbytes=6 * edges * f,
     )
     halves = mesh_steps // 2
-    ready = lead[2]
+    ready = lead[3]
     current = jnp.concatenate([lead[3], seed, seed_back], axis=0)
     chain, turned = [current], []
     for _ in range(STEPS):
@@ -465,22 +463,14 @@
             functools.partial(main_body, chips, first), (halves,),
             [(place, smem), (mesh_live, smem), (as_blocks(mesh_sender, BLOCK), at((BLOCK // 128, 128), 2)),
              (as_rows(mesh_sender, BLOCK), at((1, BLOCK), 2)), (as_rows(mesh_receiver, BLOCK), at((1, BLOCK), 2)), full(need),
-             (process_edge_in, whole((f, f))), held(lead[0]), held(lead[1]), held(back[1]), (mesh_edges, moved),
-             (before, moved), full(row(process_edge_bias)), full(process_edge_out), full(row(process_edge_gain)),
-             (ready, anywhere)] + ([full(totals)] if part else []),
-            [((n, f), F32, whole((n, f)), HBM)],
+             (w_in_near, whole((f, f)), True), held(lead[0]), held(lead[1]), held(back[1]), (edges_near, moved, True),
+             (before, moved, True), full(row(process_edge_bias)), held(out_near), full(row(process_edge_gain)),
+             (ready, anywhere)] + ([held(totals)] if part else []),
+            [((n, f), F32, whole((n, f)), VMEM)],
             [pltpu.VMEM((6 * pair, f), BF)],
             flops=2 * f * f * halves * BLOCK * 2, nbytes=6 * halves * BLOCK * f,
         )
-        ready = chain[0]
-    (grid_before,) = call(
-        grid_before_body, (grid_steps,),
-        [(as_rows(grid_receiver, GRID_BLOCK), row_spec(GRID_BLOCK)), full(grid_nodes), full(decode_edge_in),
-         (grid_edges, tile(GRID_BLOCK)), (chain[1], anywhere)],
-        [((grid_e, f), F32, tile(GRID_BLOCK), HBM)],
-        [pltpu.VMEM((grid_n, f), BF)],
-        flops=2 * f * f * (grid_e * 2 + grid_n), nbytes=6 * grid_e * f,
-    )
+        ready = chain[1]
     far = [lead[2], back[2]] + chain + [back[3]] + turned
     starts, at_row = [], 0
     for v in far:
@@ -488,29 +478,28 @@
         at_row += v.shape[0]
     last = [STEPS + 2, len(far) - 2, len(far) - 1]
     early = [i for i in range(len(far)) if i not in last]
-    late_buffers = [pltpu.VMEM((128, f), F32), pltpu.VMEM((128, f), BF), pltpu.VMEM((128, f), BF), pltpu.VMEM((128, 128), I32),
-                    pltpu.VMEM((128, 128), I32)]
-    vmem = lambda v: ((f if v is process_edge_in or v is decode_edge_in else v.shape[0], f), v.dtype, pl.BlockSpec(memory_space=VMEM), VMEM)
-    far_needs = [mesh_nodes, totals, process_edge_in, process_edge_out, process_node_in, process_node_out]
+    far_needs = [process_node_in, process_node_out]
     grid_needs = [grid_before, decode_edge_in, grid_nodes, grid_edges, decode_edge_out, decode_node_in, decode_node_out]
-    *stored, count, nodes_near, totals_near, head_near, out_near, node_in_near, node_out_near = call(
+    on_chip = lambda dtype, width: ((edges, width), dtype, pl.BlockSpec(memory_space=VMEM), VMEM)
+    *stored, count, node_in_near, node_out_near = call(
         functools.partial(compact_body, chips, offered, tuple(starts[i] for i in early)), (1,),
-        [(place, smem), (mesh_live, smem), full(send_rows), full(receive_rows), full(need), full(process_edge_in), held(table_r),
-         full(mesh_edges)] + [held(far[i]) for i in early] + [(v, hbm) for v in far_needs],
-        [((edges, f), F32, hbm), ((edges, f), BF, hbm), ((edges, f), BF, hbm), ((edges, 128), I32, hbm),
-         ((edges, 128), I32, hbm), ((1,), I32, smem)] + [vmem(v) for v in far_needs],
-        late_buffers + [pltpu.SemaphoreType.DMA((5,)), pltpu.SemaphoreType.DMA((AHEAD_FAR,))],
+        [(place, smem), (mesh_live, smem), full(send_rows), full(receive_rows), full(need),
+         (w_in_near, pl.BlockSpec((f, f), lambda i: (2, 0)), True), held(table_r), held(edges_near)]
+        + [held(far[i]) for i in early] + [(v, hbm) for v in far_needs],
+        [on_chip(F32, f), on_chip(BF, f), on_chip(BF, f), on_chip(I32, 128), on_chip(I32, 128), ((1,), I32, smem)]
+        + [vmem(v) for v in far_needs],
+        [pltpu.SemaphoreType.DMA((AHEAD_FAR,))],
         flops=2 * f * 128 * (edges + 4 * f), nbytes=2 * edges * f,
     )
     mesh_out, mesh_kept, published, grid_before, grid_head, nodes_g, edges_g, out_g, node_in_g, node_out_g = call(
         functools.partial(far_body, tuple(starts[i] for i in last)), (1,),
-        [(count, smem), held(nodes_near), full(boundary), held(totals_near), full(row(process_edge_bias)),
-         full(row(process_edge_gain)), full(row(process_node_bias)), full(row(process_node_gain)), held(head_near), held(out_near),
-         held(node_in_near), held(node_out_near)] + [held(far[i]) for i in last] + [(v, hbm) for v in stored]
-        + [(v, hbm) for v in grid_needs],
+        [(count, smem), held(nodes_near), full(boundary), held(totals), full(row(process_edge_bias)),
+         full(row(process_edge_gain)), full(row(process_node_bias)), full(row(process_node_gain)), (w_in_near, whole((f, f)), True),
+         held(out_near), held(node_in_near), held(node_out_near)] + [held(far[i]) for i in last]
+        + [(v, pl.BlockSpec(memory_space=VMEM), True) for v in stored] + [(v, hbm) for v in grid_needs],
         [((n, f), BF, whole((n, f))), ((n, f), BF, whole((n, f)), VMEM), ((offered, f), BF, whole((offered, f)), VMEM)]
         + [vmem(v) for v in grid_needs],
-        [pltpu.VMEM((n, f), F32)] + late_buffers + [pltpu.SemaphoreType.DMA((5,)), pltpu.SemaphoreType.DMA((AHEAD_GRID,))],
+        [pltpu.VMEM((n, f), F32), pltpu.SemaphoreType.DMA((AHEAD_GRID,))],
         flops=2 * f * f * 4 * n, nbytes=8 * n * f,
     )
     pieces = []

time: 138 us -> 119 us (0.86)
  Pallas kernels: 50 us -> 40.2 us
  waiting for transfers between devices: 66.2 us -> 60.6 us
  starting transfers between devices: 18.5 us -> 15.2 us
    pallas_call x9, Pallas kernels: 50 us -> 40.2 us  [call(): pl.pallas_call(body, grid=grid, in_specs=[i[1] for i in ins], out_specs=[...]
    ppermute x8, waiting for transfers between devices: 62.5 us -> 56.5 us  [shift(): return lax.ppermute(v, REGION, along(steps))]
    ppermute x4, starting transfers between devices: 8.42 us -> 2.65 us  [local(): lax.ppermute(published, REGION, [(s, (s - offset) % regions) for s in ran...]
    ppermute x9, starting transfers between devices: 3.35 us -> 5.78 us  [swap(): return lax.ppermute(v, 'core', [(0, 1), (1, 0)])]
  transfers between devices with their start and end apart: 21 -> 21, of which waited for: 10 -> 9; matrix products, arithmetic and copies ran while one was open for 0% -> 0% of each run, Pallas kernels for 25% -> 23%
where the time goes in v2:
time: 119 us; the launch traced here: 118 us
  waiting for transfers between devices  60.6 us (51%)
  Pallas kernels  40.2 us (34%)
  starting transfers between devices  15.2 us (13%)
  between operations  1.46 us (1%)
    ppermute x8, waiting for transfers between devices, shift(): return lax.ppermute(v, REGION, along(steps))  56.5 us
    pallas_call x9, Pallas kernels, call(): pl.pallas_call(body, grid=grid, in_specs=[i[1] for i in ins], out_specs=[...  40.2 us
    ppermute x8, starting transfers between devices, shift(): return lax.ppermute(v, REGION, along(steps))  6.8 us
    ppermute x9, starting transfers between devices, swap(): return lax.ppermute(v, 'core', [(0, 1), (1, 0)])  5.78 us
    ppermute x4, starting transfers between devices, local(): lax.ppermute(published, REGION, [(s, (s - offset) % regions) for s in ran...  2.65 us
  transfers between devices with their start and end apart: 21, of which 9 were waited for; matrix products, arithmetic and copies ran while one was open for 0% of the time, Pallas kernels for 23%

profile of v2, /device:TPU:44, one launch (start us, length us, event | category | flops | bytes accessed | tf_op | source)
XLA Modules:
  0.0 117.6 jit_solution(14249082825621077752)
XLA Ops:
  0.6 1.3 %shard_map.275 = bf16[32,512]{1,0:T(8,128)(2,1)S(1)} custom-call(s32[1,32]{1,0:T(1,128)} %boundary.1, bf16[512,512]{1,0:T(8,128)(2,1)} %refs_1_.1), custom_call_target="tpu_custom_call" | custom-call | flops 16777216 | bytes 524288 | tf_op jit(solution)/shard_map/pallas_call | solution.py:75
  2.1 1.2 %collective-permute-done = bf16[32,512]{1,0:T(8,128)(2,1)S(1)} collective-permute-done((bf16[32,512]{1,0:T(8,128)(2,1)S(1)}, bf16[32,512]{1,0:T(8,128)(2,1)S(1)}, u32[]{:S(2)}, u32[]{:S(2)}) %collective-permute-start) | collective-permute-done | bytes 32800 | tf_op jit(solution)/shard_map/ppermute | solution.py:412
  3.3 2.1 %collective-permute-start.1 = (bf16[64,512]{1,0:T(8,128)(2,1)S(1)}, bf16[64,512]{1,0:T(8,128)(2,1)S(1)}, u32[]{:S(2)}, u32[]{:S(2)}) collective-permute-start(bf16[64,512]{1,0:T(8,128)(2,1)S(1)} %pad_maximum_fusion.both), channel_id=1, source_target_pairs={{0,2},{1,63},{2,4},{3,1},{4,6},{5,3},{6,8},{7,5},{8,10},{9,7},{10,... | collective-permute-start | bytes 196616 | tf_op jit(solution)/shard_map/ppermute | solution.py:409
  5.4 23.2 %collective-permute-done.1.ready.up = bf16[64,512]{1,0:T(8,128)(2,1)S(1)} collective-permute-done((bf16[64,512]{1,0:T(8,128)(2,1)S(1)}, bf16[64,512]{1,0:T(8,128)(2,1)S(1)}, u32[]{:S(2)}, u32[]{:S(2)}) %collective-permute-start.1) | collective-permute-done | bytes 65568 | tf_op jit(solution)/shard_map/ppermute | solution.py:409
  28.6 4.0 %collective-permute-start.5 = (bf16[64,512]{1,0:T(8,128)(2,1)S(1)}, bf16[64,512]{1,0:T(8,128)(2,1)S(1)}, u32[]{:S(2)}, u32[]{:S(2)}) collective-permute-start(bf16[64,512]{1,0:T(8,128)(2,1)S(1)} %pad_maximum_fusion.both), channel_id=1, source_target_pairs={{0,24},{1,41},{2,26},{3,43},{4,28},{5,45},{6,30},{7,47},{8,32},{9,... | collective-permute-start | bytes 196616 | tf_op jit(solution)/shard_map/ppermute | solution.py:409
  32.5 1.5 %collective-permute-done.2.ready.refs_0_ = bf16[64,512]{1,0:T(8,128)(2,1)S(1)} collective-permute-done((bf16[64,512]{1,0:T(8,128)(2,1)S(1)}, bf16[64,512]{1,0:T(8,128)(2,1)S(1)}, u32[]{:S(2)}, u32[]{:S(2)}) %collective-permute-start.2) | collective-permute-done | bytes 65568 | tf_op jit(solution)/shard_map/ppermute | solution.py:409
  34.7 11.8 %collective-permute-done.5 = bf16[64,512]{1,0:T(8,128)(2,1)S(1)} collective-permute-done((bf16[64,512]{1,0:T(8,128)(2,1)S(1)}, bf16[64,512]{1,0:T(8,128)(2,1)S(1)}, u32[]{:S(2)}, u32[]{:S(2)}) %collective-permute-start.5) | collective-permute-done | bytes 65568 | tf_op jit(solution)/shard_map/ppermute | solution.py:409
  46.5 0.7 collective-permute-start.6
  47.2 0.9 collective-permute-done.6
  48.1 13.8 %collective-permute-done.7.refs_3_.ready = bf16[192,512]{1,0:T(8,128)(2,1)S(1)} collective-permute-done((bf16[192,512]{1,0:T(8,128)(2,1)S(1)}, bf16[192,512]{1,0:T(8,128)(2,1)S(1)}, u32[]{:S(2)}, u32[]{:S(2)}) %collective-permute-start.7) | collective-permute-done | bytes 196640 | tf_op jit(solution)/shard_map/ppermute | solution.py:409
  62.5 6.2 %collective-permute-done.8.refs_4_ = bf16[192,512]{1,0:T(8,128)(2,1)S(1)} collective-permute-done((bf16[192,512]{1,0:T(8,128)(2,1)S(1)}, bf16[192,512]{1,0:T(8,128)(2,1)S(1)}, u32[]{:S(2)}, u32[]{:S(2)}) %collective-permute-start.8) | collective-permute-done | bytes 196640 | tf_op jit(solution)/shard_map/ppermute | solution.py:409
  68.8 0.8 collective-permute-start.13
  69.7 6.4 %shard_map.276 = (f32[1152,512]{1,0:T(8,128)}, bf16[1536,512]{1,0:T(8,128)(2,1)S(1)}, bf16[512,512]{1,0:T(8,128)(2,1)S(1)}, bf16[2048,512]{1,0:T(8,128)(2,1)S(1)}, bf16[512,512]{1,0:T(8,128)(2,1)S(1)}) custom-call(s32[3,1,384]{2,1,0:T(1,128)} %bitcast.35, bf16[384,512]{1,0:T(8,128)(2,1)} %refs_10_.3, bf16[1536,512]{1,0:T(8,128)(2,1)} %refs_9_.3, ...), custom_call_target="tpu_custom_call" | custom-call | flops 1409286144 | bytes 3538944 | tf_op jit(solution)/shard_map/pallas_call | solution.py:75
  76.4 5.6 %shard_map.277 = (f32[2048,512]{1,0:T(8,128)S(1)}, bf16[512,512]{1,0:T(8,128)(2,1)S(1)}) custom-call(s32[4,4,128]{2,1,0:T(4,128)} %bitcast.22, s32[4,4,128]{2,1,0:T(4,128)} %bitcast.28, bf16[512,512]{1,0:T(8,128)(2,1)S(1)} %get-tuple-element.28.nodes, bf16[1536,512]{1,0:T(8,128)(2,1)S(1)} %get-tuple-element.27.w_in.w_e.w_s, ...), custom_call_target="tpu_custom_call" | custom-call | flops 3758096384 | bytes 6291456 | tf_op jit(solution)/shard_map/pallas_call | solution.py:75
  82.0 2.8 %collective-permute-start.11 = (bf16[192,512]{1,0:T(8,128)(2,1)S(1)}, bf16[192,512]{1,0:T(8,128)(2,1)S(1)}, u32[]{:S(2)}, u32[]{:S(2)}) collective-permute-start(bf16[192,512]{1,0:T(8,128)(2,1)S(1)} %collective-permute-done.7.refs_3_.ready), channel_id=1, source_target_pairs={{0,1},{1,0},{2,3},{3,2},{4,5},{5,4},{6,7},{7,6},{8,9},{9,8},{10,11... | collective-permute-start | bytes 589832 | tf_op jit(solution)/shard_map/ppermute | solution.py:412
  85.5 4.2 %shard_map.279.refs_0_ = f32[512,512]{1,0:T(8,128)S(1)} custom-call(s32[2]{0:T(128)S(1)} %pad_add_fusion.place, s32[1]{0:T(128)S(6)} %copy.32.live, s32[4,4,128]{2,1,0:T(4,128)} %bitcast.23, s32[4,1,512]{2,1,0:T(1,128)} %bitcast.24, s32[4,1,512]{2,1,0:T(1,128)} %bitcast.29, s32[8,64]{1,0:T(8,128)} %bitcast.32, ...), custom_call_target="tpu_custom_call" | custom-call | flops 1073741824 | bytes 3145728 | tf_op jit(solution)/shard_map/pallas_call | solution.py:75
  90.1 4.2 %shard_map.280.totals = f32[512,512]{1,0:T(8,128)S(1)} custom-call(s32[2]{0:T(128)S(1)} %pad_add_fusion.place, s32[1]{0:T(128)S(6)} %copy.32.live, s32[4,4,128]{2,1,0:T(4,128)} %bitcast.25, s32[4,1,512]{2,1,0:T(1,128)} %bitcast.26, s32[4,1,512]{2,1,0:T(1,128)} %bitcast.30, s32[8,64]{1,0:T(8,128)} %bitcast.33, ...), custom_call_target="tpu_custom_call" | custom-call | flops 1073741824 | bytes 3145728 | tf_op jit(solution)/shard_map/pallas_call | solution.py:75
  94.4 3.7 %shard_map.278 = (f32[2048,512]{1,0:T(8,128)S(1)}, bf16[2048,512]{1,0:T(8,128)(2,1)S(1)}, bf16[2048,512]{1,0:T(8,128)(2,1)S(1)}, s32[2048,128]{1,0:T(8,128)S(1)}...) custom-call(s32[2]{0:T(128)S(1)} %pad_add_fusion.place, ...), custom_call_target="tpu_custom_call" | custom-call | flops 536870912 | bytes 2097152 | tf_op jit(solution)/shard_map/pallas_call | solution.py:75
  98.1 5.3 %shard_map.281 = (bf16[512,512]{1,0:T(8,128)(2,1)}, bf16[512,512]{1,0:T(8,128)(2,1)S(1)}, bf16[32,512]{1,0:T(8,128)(2,1)S(1)}, f32[1152,512]{1,0:T(8,128)S(1)}, ...) custom-call(s32[1]{0:T(128)} %get-tuple-element.31.count, ...), custom_call_target="tpu_custom_call" | custom-call | flops 1073741824 | bytes 2097152 | tf_op jit(solution)/shard_map/pallas_call | solution.py:75
  103.4 0.8 collective-permute-start.20
  104.2 1.3 %collective-permute-start.19 = (bf16[32,512]{1,0:T(8,128)(2,1)S(1)}, bf16[32,512]{1,0:T(8,128)(2,1)S(1)}, u32[]{:S(2)}, u32[]{:S(2)}) collective-permute-start(bf16[32,512]{1,0:T(8,128)(2,1)S(1)} %get-tuple-element.43), channel_id=1, source_target_pairs={{0,63},{1,0},{2,1},{3,2},{4,3},{5,4},{6,5},{7,6},{8,7},{9,8},{10,9... | collective-permute-start | bytes 98312 | tf_op jit(solution)/shard_map/ppermute | solution.py:507
  106.0 2.7 %shard_map.282.before = f32[1152,512]{1,0:T(8,128)S(1)} custom-call(s32[3,1,384]{2,1,0:T(1,128)} %bitcast.37, bf16[512,512]{1,0:T(8,128)(2,1)S(1)} %get-tuple-element.47.mesh_out, bf16[512,512]{1,0:T(8,128)(2,1)S(1)} %get-tuple-element.44.w_s, f32[1152,512]{1,0:T(8,128)S(1)} %get-tuple-element.48.before), custom_call_target="tpu_custom_call" | custom-call | flops 872415232 | bytes 4718592 | tf_op jit(solution)/shard_map/pallas_call | solution.py:75
  108.8 1.3 %collective-permute-done.18.b = bf16[32,512]{1,0:T(8,128)(2,1)S(1)} collective-permute-done((bf16[32,512]{1,0:T(8,128)(2,1)S(1)}, bf16[32,512]{1,0:T(8,128)(2,1)S(1)}, u32[]{:S(2)}, u32[]{:S(2)}) %collective-permute-start.18) | collective-permute-done | bytes 32800 | tf_op jit(solution)/shard_map/ppermute | solution.py:507
  110.8 6.8 %shard_map.283 = bf16[384,512]{1,0:T(8,128)(2,1)} custom-call(s32[3,1,384]{2,1,0:T(1,128)} %bitcast.38, s32[3,1,384]{2,1,0:T(1,128)} %bitcast.36, s32[4,8]{1,0:T(4,128)} %bitcast.47, bf16[32,512]{1,0:T(8,128)(2,1)S(1)} %collective-permute-done.17.a, bf16[32,512]{1,0:T(8,128)(2,1)S(1)} %collective-permute-done.18.b, ...), custom_call_target="tpu_custom_call" | custom-call | flops 1811939328 | bytes 3538944 | tf_op jit(solution)/shard_map/pallas_call | solution.py:75
  (32 shorter events, 3.6 us)
Async XLA Ops:
  1.9 1.3 %collective-permute-start = (bf16[32,512]{1,0:T(8,128)(2,1)S(1)}, bf16[32,512]{1,0:T(8,128)(2,1)S(1)}, u32[]{:S(2)}, u32[]{:S(2)}) collective-permute-start(bf16[32,512]{1,0:T(8,128)(2,1)S(1)} %shard_map.275), channel_id=1, source_target_pairs={{0,1},{1,0},{2,3},{3,2},{4,5},{5,4},{6,7},{7,6},{8,9},{9,8},{10,11... | collective-permute-start | bytes 98312 | tf_op jit(solution)/shard_map/ppermute | solution.py:412
  3.3 25.3 %collective-permute-start.1 = (bf16[64,512]{1,0:T(8,128)(2,1)S(1)}, bf16[64,512]{1,0:T(8,128)(2,1)S(1)}, u32[]{:S(2)}, u32[]{:S(2)}) collective-permute-start(bf16[64,512]{1,0:T(8,128)(2,1)S(1)} %pad_maximum_fusion.both), channel_id=1, source_target_pairs={{0,2},{1,63},{2,4},{3,1},{4,6},{5,3},{6,8},{7,5},{8,10},{9,7},{10,... | collective-permute-start | bytes 196616 | tf_op jit(solution)/shard_map/ppermute | solution.py:409
  28.6 5.5 %collective-permute-start.2 = (bf16[64,512]{1,0:T(8,128)(2,1)S(1)}, bf16[64,512]{1,0:T(8,128)(2,1)S(1)}, u32[]{:S(2)}, u32[]{:S(2)}) collective-permute-start(bf16[64,512]{1,0:T(8,128)(2,1)S(1)} %collective-permute-done.1.ready.up), channel_id=1, source_target_pairs={{0,2},{1,63},{2,4},{3,1},{4,6},{5,3},{6,8},{7,5},{8,10},{9,7},{10,... | collective-permute-start | bytes 196616 | tf_op jit(solution)/shard_map/ppermute | solution.py:409
  28.6 17.9 %collective-permute-start.5 = (bf16[64,512]{1,0:T(8,128)(2,1)S(1)}, bf16[64,512]{1,0:T(8,128)(2,1)S(1)}, u32[]{:S(2)}, u32[]{:S(2)}) collective-permute-start(bf16[64,512]{1,0:T(8,128)(2,1)S(1)} %pad_maximum_fusion.both), channel_id=1, source_target_pairs={{0,24},{1,41},{2,26},{3,43},{4,28},{5,45},{6,30},{7,47},{8,32},{9,... | collective-permute-start | bytes 196616 | tf_op jit(solution)/shard_map/ppermute | solution.py:409
  34.0 13.1 %collective-permute-start.4 = (bf16[64,512]{1,0:T(8,128)(2,1)S(1)}, bf16[64,512]{1,0:T(8,128)(2,1)S(1)}, u32[]{:S(2)}, u32[]{:S(2)}) collective-permute-start(bf16[64,512]{1,0:T(8,128)(2,1)S(1)} %collective-permute-done.2.ready.refs_0_), channel_id=1, source_target_pairs={{0,2},{1,63},{2,4},{3,1},{4,6},{5,3},{6,8},{7,5},{8,10},{9,7},{10,... | collective-permute-start | bytes 196616 | tf_op jit(solution)/shard_map/ppermute | solution.py:409
  46.5 1.6 %collective-permute-start.6 = (bf16[64,512]{1,0:T(8,128)(2,1)S(1)}, bf16[64,512]{1,0:T(8,128)(2,1)S(1)}, u32[]{:S(2)}, u32[]{:S(2)}) collective-permute-start(bf16[64,512]{1,0:T(8,128)(2,1)S(1)} %collective-permute-done.5), channel_id=1, source_target_pairs={{0,1},{1,0},{2,3},{3,2},{4,5},{5,4},{6,7},{7,6},{8,9},{9,8},{10,11... | collective-permute-start | bytes 196616 | tf_op jit(solution)/shard_map/ppermute | solution.py:412
  48.1 13.8 %collective-permute-start.7 = (bf16[192,512]{1,0:T(8,128)(2,1)S(1)}, bf16[192,512]{1,0:T(8,128)(2,1)S(1)}, u32[]{:S(2)}, u32[]{:S(2)}) collective-permute-start(bf16[192,512]{1,0:T(8,128)(2,1)S(1)} %constant_dynamic-update-slice_fusion.refs_2_), channel_id=1, source_target_pairs={{0,2},{1,63},{2,4},{3,1},{4,6},{5,3},{6,8},{7,5},{8,10},{9,7},{10,... | collective-permute-start | bytes 589832 | tf_op jit(solution)/shard_map/ppermute | solution.py:409
  61.9 6.9 %collective-permute-start.8 = (bf16[192,512]{1,0:T(8,128)(2,1)S(1)}, bf16[192,512]{1,0:T(8,128)(2,1)S(1)}, u32[]{:S(2)}, u32[]{:S(2)}) collective-permute-start(bf16[192,512]{1,0:T(8,128)(2,1)S(1)} %collective-permute-done.7.refs_3_.ready), channel_id=1, source_target_pairs={{0,2},{1,63},{2,4},{3,1},{4,6},{5,3},{6,8},{7,5},{8,10},{9,7},{10,... | collective-permute-start | bytes 589832 | tf_op jit(solution)/shard_map/ppermute | solution.py:409
  68.8 7.5 %collective-permute-start.9 = (bf16[192,512]{1,0:T(8,128)(2,1)S(1)}, bf16[192,512]{1,0:T(8,128)(2,1)S(1)}, u32[]{:S(2)}, u32[]{:S(2)}) collective-permute-start(bf16[192,512]{1,0:T(8,128)(2,1)S(1)} %collective-permute-done.8.refs_4_), channel_id=1, source_target_pairs={{0,2},{1,63},{2,4},{3,1},{4,6},{5,3},{6,8},{7,5},{8,10},{9,7},{10,... | collective-permute-start | bytes 589832 | tf_op jit(solution)/shard_map/ppermute | solution.py:409
  68.8 16.1 %collective-permute-start.13 = (bf16[64,512]{1,0:T(8,128)(2,1)S(1)}, bf16[64,512]{1,0:T(8,128)(2,1)S(1)}, u32[]{:S(2)}, u32[]{:S(2)}) collective-permute-start(bf16[64,512]{1,0:T(8,128)(2,1)S(1)} %collective-permute-done.1.ready.up), channel_id=1, source_target_pairs={{0,1},{1,0},{2,3},{3,2},{4,5},{5,4},{6,7},{7,6},{8,9},{9,8},{10,11... | collective-permute-start | bytes 196616 | tf_op jit(solution)/shard_map/ppermute | solution.py:412
  76.1 13.5 %collective-permute-start.3 = (bf16[64,512]{1,0:T(8,128)(2,1)S(1)}, bf16[64,512]{1,0:T(8,128)(2,1)S(1)}, u32[]{:S(2)}, u32[]{:S(2)}) collective-permute-start(bf16[64,512]{1,0:T(8,128)(2,1)S(1)} %collective-permute-done.2.ready.refs_0_), channel_id=1, source_target_pairs={{0,1},{1,0},{2,3},{3,2},{4,5},{5,4},{6,7},{7,6},{8,9},{9,8},{10,11... | collective-permute-start | bytes 196616 | tf_op jit(solution)/shard_map/ppermute | solution.py:412
  76.3 9.0 %collective-permute-start.14 = (bf16[192,512]{1,0:T(8,128)(2,1)S(1)}, bf16[192,512]{1,0:T(8,128)(2,1)S(1)}, u32[]{:S(2)}, u32[]{:S(2)}) collective-permute-start(bf16[192,512]{1,0:T(8,128)(2,1)S(1)} %collective-permute-done.9.refs_5_), channel_id=1, source_target_pairs={{0,2},{1,63},{2,4},{3,1},{4,6},{5,3},{6,8},{7,5},{8,10},{9,7},{10,... | collective-permute-start | bytes 589832 | tf_op jit(solution)/shard_map/ppermute | solution.py:409
  82.0 12.3 %collective-permute-start.11 = (bf16[192,512]{1,0:T(8,128)(2,1)S(1)}, bf16[192,512]{1,0:T(8,128)(2,1)S(1)}, u32[]{:S(2)}, u32[]{:S(2)}) collective-permute-start(bf16[192,512]{1,0:T(8,128)(2,1)S(1)} %collective-permute-done.7.refs_3_.ready), channel_id=1, source_target_pairs={{0,1},{1,0},{2,3},{3,2},{4,5},{5,4},{6,7},{7,6},{8,9},{9,8},{10,11... | collective-permute-start | bytes 589832 | tf_op jit(solution)/shard_map/ppermute | solution.py:412
  84.8 9.6 %collective-permute-start.12 = (bf16[192,512]{1,0:T(8,128)(2,1)S(1)}, bf16[192,512]{1,0:T(8,128)(2,1)S(1)}, u32[]{:S(2)}, u32[]{:S(2)}) collective-permute-start(bf16[192,512]{1,0:T(8,128)(2,1)S(1)} %collective-permute-done.8.refs_4_), channel_id=1, source_target_pairs={{0,1},{1,0},{2,3},{3,2},{4,5},{5,4},{6,7},{7,6},{8,9},{9,8},{10,11... | collective-permute-start | bytes 589832 | tf_op jit(solution)/shard_map/ppermute | solution.py:412
  84.9 13.2 %collective-permute-start.15 = (bf16[192,512]{1,0:T(8,128)(2,1)S(1)}, bf16[192,512]{1,0:T(8,128)(2,1)S(1)}, u32[]{:S(2)}, u32[]{:S(2)}) collective-permute-start(bf16[192,512]{1,0:T(8,128)(2,1)S(1)} %collective-permute-done.9.refs_5_), channel_id=1, source_target_pairs={{0,1},{1,0},{2,3},{3,2},{4,5},{5,4},{6,7},{7,6},{8,9},{9,8},{10,11... | collective-permute-start | bytes 589832 | tf_op jit(solution)/shard_map/ppermute | solution.py:412
  85.3 12.8 %collective-permute-start.16 = (bf16[192,512]{1,0:T(8,128)(2,1)S(1)}, bf16[192,512]{1,0:T(8,128)(2,1)S(1)}, u32[]{:S(2)}, u32[]{:S(2)}) collective-permute-start(bf16[192,512]{1,0:T(8,128)(2,1)S(1)} %collective-permute-done.14.refs_0_), channel_id=1, source_target_pairs={{0,1},{1,0},{2,3},{3,2},{4,5},{5,4},{6,7},{7,6},{8,9},{9,8},{10,11... | collective-permute-start | bytes 589832 | tf_op jit(solution)/shard_map/ppermute | solution.py:412
  89.6 4.7 %collective-permute-start.10 = (bf16[64,512]{1,0:T(8,128)(2,1)S(1)}, bf16[64,512]{1,0:T(8,128)(2,1)S(1)}, u32[]{:S(2)}, u32[]{:S(2)}) collective-permute-start(bf16[64,512]{1,0:T(8,128)(2,1)S(1)} %collective-permute-done.4.ready), channel_id=1, source_target_pairs={{0,1},{1,0},{2,3},{3,2},{4,5},{5,4},{6,7},{7,6},{8,9},{9,8},{10,11... | collective-permute-start | bytes 196616 | tf_op jit(solution)/shard_map/ppermute | solution.py:412
  103.4 5.4 %collective-permute-start.20 = (bf16[32,512]{1,0:T(8,128)(2,1)S(1)}, bf16[32,512]{1,0:T(8,128)(2,1)S(1)}, u32[]{:S(2)}, u32[]{:S(2)}) collective-permute-start(bf16[32,512]{1,0:T(8,128)(2,1)S(1)} %get-tuple-element.43), channel_id=1, source_target_pairs={{0,62},{1,63},{2,0},{3,1},{4,2},{5,3},{6,4},{7,5},{8,6},{9,7},{10,... | collective-permute-start | bytes 98312 | tf_op jit(solution)/shard_map/ppermute | solution.py:507
  104.2 4.5 %collective-permute-start.19 = (bf16[32,512]{1,0:T(8,128)(2,1)S(1)}, bf16[32,512]{1,0:T(8,128)(2,1)S(1)}, u32[]{:S(2)}, u32[]{:S(2)}) collective-permute-start(bf16[32,512]{1,0:T(8,128)(2,1)S(1)} %get-tuple-element.43), channel_id=1, source_target_pairs={{0,63},{1,0},{2,1},{3,2},{4,3},{5,4},{6,5},{7,6},{8,7},{9,8},{10,9... | collective-permute-start | bytes 98312 | tf_op jit(solution)/shard_map/ppermute | solution.py:507
  105.5 4.6 %collective-permute-start.18 = (bf16[32,512]{1,0:T(8,128)(2,1)S(1)}, bf16[32,512]{1,0:T(8,128)(2,1)S(1)}, u32[]{:S(2)}, u32[]{:S(2)}) collective-permute-start(bf16[32,512]{1,0:T(8,128)(2,1)S(1)} %get-tuple-element.43), channel_id=1, source_target_pairs={{0,1},{1,2},{2,3},{3,4},{4,5},{5,6},{6,7},{7,8},{8,9},{9,10},{10,1... | collective-permute-start | bytes 98312 | tf_op jit(solution)/shard_map/ppermute | solution.py:507
  105.5 5.2 %collective-permute-start.17 = (bf16[32,512]{1,0:T(8,128)(2,1)S(1)}, bf16[32,512]{1,0:T(8,128)(2,1)S(1)}, u32[]{:S(2)}, u32[]{:S(2)}) collective-permute-start(bf16[32,512]{1,0:T(8,128)(2,1)S(1)} %get-tuple-element.43), channel_id=1, source_target_pairs={{0,2},{1,3},{2,4},{3,5},{4,6},{5,7},{6,8},{7,9},{8,10},{9,11},{10,... | collective-permute-start | bytes 98312 | tf_op jit(solution)/shard_map/ppermute | solution.py:507

commit v3 on v2

--- a/solution.py
+++ b/solution.py
@@ -16,7 +16,7 @@
 HBM = pltpu.MemorySpace.HBM
 VMEM = pltpu.MemorySpace.VMEM
 SEED = 12
-LEAD = 3
+REACH = 7
 STEPS = 4
 LATE = 256
 AHEAD_MESH = 4
@@ -126,17 +126,22 @@
             copy.wait()
 
 
+def layout():
+    lead = {("lead", k): [(k, 0)] for k in range(2, REACH + 1)}
+    back = {("back", k): [(-k, 1)] for k in range(2, REACH + 1)}
+    chain = {("chain", k): [(SEED + k, 0), (k - SEED, 1)] for k in range(STEPS + 1)}
+    turn = {("turn", k): [(-SEED - k - 1, 1), (SEED - k - 1, 0)] for k in range(STEPS)}
+    pieces = {**lead, **back, **chain, **turn}
+    last = [("lead", REACH), ("back", REACH - 1), ("back", REACH), ("chain", STEPS), ("turn", STEPS - 2), ("turn", STEPS - 1)]
+    return [(name, pieces[name]) for name in pieces if name not in last], [(name, pieces[name]) for name in last]
+
+
 def pieces_of(chips, offered):
-    pair = 2 * offered
-    far = [(2, 0), (-2, 1)]
-    for step in range(STEPS + 1):
-        far += [(LEAD + step, 0), (SEED + step, 0), (step - SEED, 1)]
-    far += [(-LEAD, 1)]
-    for step in range(1, STEPS + 1):
-        far += [(-LEAD - step, 1), (-SEED - step, 1), (SEED - step, 0)]
+    early, last = layout()
+    held = [item for _, items in early + last for item in items]
     table = {}
-    for i, (offset, flip) in enumerate(far):
-        table.setdefault(offset % chips, (i * pair, flip))
+    for i, (offset, flip) in enumerate(held):
+        table.setdefault(offset % chips, (i * 2 * offered, flip))
     return table
 
 
@@ -203,17 +208,13 @@
     return copies
 
 
-def gathered(at, sources, starts):
-    out = None
-    for source, start in zip(sources, starts):
-        hot = ones_where(iota((at.shape[0], source.shape[0]), 1) + start == at)
-        part = dot(hot, source[...])
-        out = part if out is None else out + part
-    return out
-
-
-def compact_body(chips, offered, starts, place, live, sender, receiver, need, w_e, table_r, edges, *refs):
-    k, m = len(starts), AHEAD_FAR
+def gathered(at, sources, start):
+    rows = jnp.concatenate([source[...] for source in sources], axis=0)
+    return dot(ones_where(iota((at.shape[0], rows.shape[0]), 1) + start == at), rows)
+
+
+def compact_body(chips, offered, k, place, live, sender, receiver, need, w_e, table_r, edges, *refs):
+    m = AHEAD_FAR
     sources, ahead = refs[:k], refs[k : k + m]
     outs, count, near = refs[k + m : k + m + 5], refs[k + m + 5], refs[k + m + 6 : k + 2 * m + 6]
     ahead_sems = refs[-1]
@@ -259,7 +260,7 @@
         at = jnp.where(valid, start + jnp.where(flip == 1, 1 - half, half) * offered + chosen, -1)
         rows[lines, :] = edge
         pre[lines, :] = dot(edge, w_e[...]) + dot(ones_where(iota((LATE, n), 1) == to), table_r[...])
-        source_rows[lines, :] = gathered(at, sources, starts).astype(BF)
+        source_rows[lines, :] = gathered(at, sources, 0).astype(BF)
         at_out[lines, :] = jnp.broadcast_to(at, (LATE, 128))
         target_out[lines, :] = jnp.broadcast_to(to, (LATE, 128))
         return carry
@@ -269,8 +270,8 @@
         fetch.wait()
 
 
-def far_body(starts, count, nodes, boundary, totals, bias, gain, node_bias, node_gain, w_s, w_out, node_in, node_out, *refs):
-    k, m = len(starts), AHEAD_GRID
+def far_body(k, start, count, nodes, boundary, totals, bias, gain, node_bias, node_gain, w_s, w_out, node_in, node_out, *refs):
+    m = AHEAD_GRID
     sources, (pre, rows, source_rows, at, target), ahead = refs[:k], refs[k : k + 5], refs[k + 5 : k + 5 + m]
     result, kept_result, published = refs[k + 5 + m : k + 8 + m]
     near, acc, ahead_sems = refs[k + 8 + m : k + 8 + 2 * m], refs[-2], refs[-1]
@@ -280,7 +281,7 @@
 
     def one(block, carry):
         lines = pl.ds(pl.multiple_of(block * LATE, LATE), LATE)
-        source = (source_rows[lines, :].astype(F32) + gathered(at[lines, :][:, 0:1], sources, starts)).astype(BF)
+        source = (source_rows[lines, :].astype(F32) + gathered(at[lines, :][:, 0:1], sources, start)).astype(BF)
         update = finish(pre[lines, :] + dot(source, w_s[...]), bias[...], w_out[...], gain[...])
         message = (rows[lines, :].astype(F32) + update).astype(BF)
         eye = iota((128, 128), 0) == iota((128, 128), 1)
@@ -424,10 +425,10 @@
     lead = [both]
     lead.append(shift(both, 1))
     seed = shift(both, SEED)
-    lead.append(shift(lead[1], 1))
-    lead.append(shift(lead[2], 1))
+    for _ in range(2, REACH + 1):
+        lead.append(shift(lead[-1], 1))
     back = [None]
-    for k in range(1, LEAD + 1):
+    for k in range(1, REACH + 1):
         back.append(swap(lead[k]))
     seed_back = swap(seed)
     vmem = lambda v: ((f if v is decode_edge_in else v.shape[0], f), v.dtype, pl.BlockSpec(memory_space=VMEM), VMEM)
@@ -450,7 +451,7 @@
     )
     halves = mesh_steps // 2
     ready = lead[3]
-    current = jnp.concatenate([lead[3], seed, seed_back], axis=0)
+    current = jnp.concatenate([seed, seed_back], axis=0)
     chain, turned = [current], []
     for _ in range(STEPS):
         chain.append(shift(chain[-1], 1))
@@ -470,32 +471,28 @@
             [pltpu.VMEM((6 * pair, f), BF)],
             flops=2 * f * f * halves * BLOCK * 2, nbytes=6 * halves * BLOCK * f,
         )
-        ready = chain[1]
-    far = [lead[2], back[2]] + chain + [back[3]] + turned
-    starts, at_row = [], 0
-    for v in far:
-        starts.append(at_row)
-        at_row += v.shape[0]
-    last = [STEPS + 2, len(far) - 2, len(far) - 1]
-    early = [i for i in range(len(far)) if i not in last]
+        ready = lead[4]
+    arrays = {"lead": lead, "back": back, "chain": chain, "turn": turned}
+    early, last = [[arrays[kind][k] for (kind, k), _ in part] for part in layout()]
+    early_rows = sum(v.shape[0] for v in early)
     far_needs = [process_node_in, process_node_out]
     grid_needs = [grid_before, decode_edge_in, grid_nodes, grid_edges, decode_edge_out, decode_node_in, decode_node_out]
     on_chip = lambda dtype, width: ((edges, width), dtype, pl.BlockSpec(memory_space=VMEM), VMEM)
     *stored, count, node_in_near, node_out_near = call(
-        functools.partial(compact_body, chips, offered, tuple(starts[i] for i in early)), (1,),
+        functools.partial(compact_body, chips, offered, len(early)), (1,),
         [(place, smem), (mesh_live, smem), full(send_rows), full(receive_rows), full(need),
          (w_in_near, pl.BlockSpec((f, f), lambda i: (2, 0)), True), held(table_r), held(edges_near)]
-        + [held(far[i]) for i in early] + [(v, hbm) for v in far_needs],
+        + [held(v) for v in early] + [(v, hbm) for v in far_needs],
         [on_chip(F32, f), on_chip(BF, f), on_chip(BF, f), on_chip(I32, 128), on_chip(I32, 128), ((1,), I32, smem)]
         + [vmem(v) for v in far_needs],
         [pltpu.SemaphoreType.DMA((AHEAD_FAR,))],
         flops=2 * f * 128 * (edges + 4 * f), nbytes=2 * edges * f,
     )
     mesh_out, mesh_kept, published, grid_before, grid_head, nodes_g, edges_g, out_g, node_in_g, node_out_g = call(
-        functools.partial(far_body, tuple(starts[i] for i in last)), (1,),
+        functools.partial(far_body, len(last), early_rows), (1,),
         [(count, smem), held(nodes_near), full(boundary), held(totals), full(row(process_edge_bias)),
          full(row(process_edge_gain)), full(row(process_node_bias)), full(row(process_node_gain)), (w_in_near, whole((f, f)), True),
-         held(out_near), held(node_in_near), held(node_out_near)] + [held(far[i]) for i in last]
+         held(out_near), held(node_in_near), held(node_out_near)] + [held(v) for v in last]
         + [(v, pl.BlockSpec(memory_space=VMEM), True) for v in stored] + [(v, hbm) for v in grid_needs],
         [((n, f), BF, whole((n, f))), ((n, f), BF, whole((n, f)), VMEM), ((offered, f), BF, whole((offered, f)), VMEM)]
         + [vmem(v) for v in grid_needs],

time: 119 us -> 121 us (1.017)
  starting transfers between devices: 15.2 us -> 41.4 us
  waiting for transfers between devices: 60.6 us -> 36.7 us
    ppermute x8 -> x12, waiting for transfers between devices: 56.5 us -> 32.6 us  [shift(): return lax.ppermute(v, REGION, along(steps))]
    ppermute x8 -> x12, starting transfers between devices: 6.8 us -> 30 us  [shift(): return lax.ppermute(v, REGION, along(steps))]
    ppermute x9 -> x13, starting transfers between devices: 5.78 us -> 7.26 us  [swap(): return lax.ppermute(v, 'core', [(0, 1), (1, 0)])]
    ppermute x4, starting transfers between devices: 2.65 us -> 4.08 us  [local(): lax.ppermute(published, REGION, [(s, (s - offset) % regions) for s in ran...]
    ppermute x9 -> x13, waiting for transfers between devices: 2.08 us -> 2.45 us  [swap(): return lax.ppermute(v, 'core', [(0, 1), (1, 0)])]
  transfers between devices with their start and end apart: 21 -> 29, of which waited for: 9 -> 9; matrix products, arithmetic and copies ran while one was open for 0% -> 0% of each run, Pallas kernels for 23% -> 22%
where the time goes in v3:
time: 121 us; the launch traced here: 120 us
  starting transfers between devices  41.4 us (34%)
  Pallas kernels  40.3 us (33%)
  waiting for transfers between devices  36.7 us (30%)
  between operations  1.48 us (1%)
    pallas_call x9, Pallas kernels, call(): pl.pallas_call(body, grid=grid, in_specs=[i[1] for i in ins], out_specs=[...  40.3 us
    ppermute x12, waiting for transfers between devices, shift(): return lax.ppermute(v, REGION, along(steps))  32.6 us
    ppermute x12, starting transfers between devices, shift(): return lax.ppermute(v, REGION, along(steps))  30 us
    ppermute x13, starting transfers between devices, swap(): return lax.ppermute(v, 'core', [(0, 1), (1, 0)])  7.26 us
    ppermute x4, starting transfers between devices, local(): lax.ppermute(published, REGION, [(s, (s - offset) % regions) for s in ran...  4.08 us
    ppermute x13, waiting for transfers between devices, swap(): return lax.ppermute(v, 'core', [(0, 1), (1, 0)])  2.45 us
  transfers between devices with their start and end apart: 29, of which 9 were waited for; matrix products, arithmetic and copies ran while one was open for 0% of the time, Pallas kernels for 22%

profile of v3, /device:TPU:44, one launch (start us, length us, event | category | flops | bytes accessed | tf_op | source)
XLA Modules:
  0.0 119.9 jit_solution(4712701168341485731)
XLA Ops:
  0.6 1.3 %shard_map.275 = bf16[32,512]{1,0:T(8,128)(2,1)S(1)} custom-call(s32[1,32]{1,0:T(1,128)} %boundary.1, bf16[512,512]{1,0:T(8,128)(2,1)} %refs_1_.1), custom_call_target="tpu_custom_call" | custom-call | flops 16777216 | bytes 524288 | tf_op jit(solution)/shard_map/pallas_call | solution.py:75
  2.1 1.2 collective-permute-done
  3.3 22.9 %collective-permute-start.11 = (bf16[64,512]{1,0:T(8,128)(2,1)S(1)}, bf16[64,512]{1,0:T(8,128)(2,1)S(1)}, u32[]{:S(2)}, u32[]{:S(2)}) collective-permute-start(bf16[64,512]{1,0:T(8,128)(2,1)S(1)} %pad_maximum_fusion.both), channel_id=1, source_target_pairs={{0,24},{1,41},{2,26},{3,43},{4,28},{5,45},{6,30},{7,47},{8,32},{9,... | collective-permute-start | bytes 196616 | tf_op jit(solution)/shard_map/ppermute | solution.py:410
  26.1 2.1 %collective-permute-start.1 = (bf16[64,512]{1,0:T(8,128)(2,1)S(1)}, bf16[64,512]{1,0:T(8,128)(2,1)S(1)}, u32[]{:S(2)}, u32[]{:S(2)}) collective-permute-start(bf16[64,512]{1,0:T(8,128)(2,1)S(1)} %pad_maximum_fusion.both), channel_id=1, source_target_pairs={{0,2},{1,63},{2,4},{3,1},{4,6},{5,3},{6,8},{7,5},{8,10},{9,7},{10,... | collective-permute-start | bytes 196616 | tf_op jit(solution)/shard_map/ppermute | solution.py:410
  28.3 6.1 %collective-permute-done.11 = bf16[64,512]{1,0:T(8,128)(2,1)S(1)} collective-permute-done((bf16[64,512]{1,0:T(8,128)(2,1)S(1)}, bf16[64,512]{1,0:T(8,128)(2,1)S(1)}, u32[]{:S(2)}, u32[]{:S(2)}) %collective-permute-start.11) | collective-permute-done | bytes 65568 | tf_op jit(solution)/shard_map/ppermute | solution.py:410
  34.4 1.2 %collective-permute-done.12 = bf16[64,512]{1,0:T(8,128)(2,1)S(1)} collective-permute-done((bf16[64,512]{1,0:T(8,128)(2,1)S(1)}, bf16[64,512]{1,0:T(8,128)(2,1)S(1)}, u32[]{:S(2)}, u32[]{:S(2)}) %collective-permute-start.12) | collective-permute-done | bytes 65568 | tf_op jit(solution)/shard_map/ppermute | solution.py:413
  35.6 1.9 %collective-permute-start.13 = (bf16[128,512]{1,0:T(8,128)(2,1)S(1)}, bf16[128,512]{1,0:T(8,128)(2,1)S(1)}, u32[]{:S(2)}, u32[]{:S(2)}) collective-permute-start(bf16[128,512]{1,0:T(8,128)(2,1)S(1)} %constant_dynamic-update-slice_fusion.refs_9_), channel_id=1, source_target_pairs={{0,2},{1,63},{2,4},{3,1},{4,6},{5,3},{6,8},{7,5},{8,10},{9,7},{10,... | collective-permute-start | bytes 393224 | tf_op jit(solution)/shard_map/ppermute | solution.py:410
  37.6 1.9 %collective-permute-start.2 = (bf16[64,512]{1,0:T(8,128)(2,1)S(1)}, bf16[64,512]{1,0:T(8,128)(2,1)S(1)}, u32[]{:S(2)}, u32[]{:S(2)}) collective-permute-start(bf16[64,512]{1,0:T(8,128)(2,1)S(1)} %collective-permute-done.1.ready.up), channel_id=1, source_target_pairs={{0,2},{1,63},{2,4},{3,1},{4,6},{5,3},{6,8},{7,5},{8,10},{9,7},{10,... | collective-permute-start | bytes 196616 | tf_op jit(solution)/shard_map/ppermute | solution.py:410
  39.5 16.6 %collective-permute-done.2.ready.refs_0_ = bf16[64,512]{1,0:T(8,128)(2,1)S(1)} collective-permute-done((bf16[64,512]{1,0:T(8,128)(2,1)S(1)}, bf16[64,512]{1,0:T(8,128)(2,1)S(1)}, u32[]{:S(2)}, u32[]{:S(2)}) %collective-permute-start.2) | collective-permute-done | bytes 65568 | tf_op jit(solution)/shard_map/ppermute | solution.py:410
  56.7 4.8 %collective-permute-done.3.refs_1_.ready = bf16[64,512]{1,0:T(8,128)(2,1)S(1)} collective-permute-done((bf16[64,512]{1,0:T(8,128)(2,1)S(1)}, bf16[64,512]{1,0:T(8,128)(2,1)S(1)}, u32[]{:S(2)}, u32[]{:S(2)}) %collective-permute-start.3) | collective-permute-done | bytes 65568 | tf_op jit(solution)/shard_map/ppermute | solution.py:410
  62.6 4.4 %collective-permute-done.4.refs_2_.ready = bf16[64,512]{1,0:T(8,128)(2,1)S(1)} collective-permute-done((bf16[64,512]{1,0:T(8,128)(2,1)S(1)}, bf16[64,512]{1,0:T(8,128)(2,1)S(1)}, u32[]{:S(2)}, u32[]{:S(2)}) %collective-permute-start.4) | collective-permute-done | bytes 65568 | tf_op jit(solution)/shard_map/ppermute | solution.py:410
  67.0 6.5 %shard_map.276 = (f32[1152,512]{1,0:T(8,128)}, bf16[1536,512]{1,0:T(8,128)(2,1)S(1)}, bf16[512,512]{1,0:T(8,128)(2,1)S(1)}, bf16[2048,512]{1,0:T(8,128)(2,1)S(1)}, bf16[512,512]{1,0:T(8,128)(2,1)S(1)}) custom-call(s32[3,1,384]{2,1,0:T(1,128)} %bitcast.35, bf16[384,512]{1,0:T(8,128)(2,1)} %refs_13_.1, bf16[1536,512]{1,0:T(8,128)(2,1)} %refs_12_.1, ...), custom_call_target="tpu_custom_call" | custom-call | flops 1409286144 | bytes 3538944 | tf_op jit(solution)/shard_map/pallas_call | solution.py:75
  74.5 1.0 collective-permute-start.6
  75.6 5.6 %shard_map.277 = (f32[2048,512]{1,0:T(8,128)S(1)}, bf16[512,512]{1,0:T(8,128)(2,1)S(1)}) custom-call(s32[4,4,128]{2,1,0:T(4,128)} %bitcast.22, s32[4,4,128]{2,1,0:T(4,128)} %bitcast.28, bf16[512,512]{1,0:T(8,128)(2,1)S(1)} %get-tuple-element.28.nodes, bf16[1536,512]{1,0:T(8,128)(2,1)S(1)} %get-tuple-element.27.w_in.w_e.w_s, ...), custom_call_target="tpu_custom_call" | custom-call | flops 3758096384 | bytes 6291456 | tf_op jit(solution)/shard_map/pallas_call | solution.py:75
  81.2 3.8 %collective-permute-start.10 = (bf16[64,512]{1,0:T(8,128)(2,1)S(1)}, bf16[64,512]{1,0:T(8,128)(2,1)S(1)}, u32[]{:S(2)}, u32[]{:S(2)}) collective-permute-start(bf16[64,512]{1,0:T(8,128)(2,1)S(1)} %collective-permute-done.5.refs_3_), channel_id=1, source_target_pairs={{0,1},{1,0},{2,3},{3,2},{4,5},{5,4},{6,7},{7,6},{8,9},{9,8},{10,11... | collective-permute-start | bytes 196616 | tf_op jit(solution)/shard_map/ppermute | solution.py:413
  85.3 4.2 %shard_map.279.refs_0_ = f32[512,512]{1,0:T(8,128)S(1)} custom-call(s32[2]{0:T(128)S(1)} %pad_add_fusion.place, s32[1]{0:T(128)S(6)} %copy.31.live, s32[4,4,128]{2,1,0:T(4,128)} %bitcast.23, s32[4,1,512]{2,1,0:T(1,128)} %bitcast.24, s32[4,1,512]{2,1,0:T(1,128)} %bitcast.29, s32[8,64]{1,0:T(8,128)} %bitcast.32, ...), custom_call_target="tpu_custom_call" | custom-call | flops 1073741824 | bytes 3145728 | tf_op jit(solution)/shard_map/pallas_call | solution.py:75
  91.4 4.2 %shard_map.280.totals = f32[512,512]{1,0:T(8,128)S(1)} custom-call(s32[2]{0:T(128)S(1)} %pad_add_fusion.place, s32[1]{0:T(128)S(6)} %copy.31.live, s32[4,4,128]{2,1,0:T(4,128)} %bitcast.25, s32[4,1,512]{2,1,0:T(1,128)} %bitcast.26, s32[4,1,512]{2,1,0:T(1,128)} %bitcast.30, s32[8,64]{1,0:T(8,128)} %bitcast.33, ...), custom_call_target="tpu_custom_call" | custom-call | flops 1073741824 | bytes 3145728 | tf_op jit(solution)/shard_map/pallas_call | solution.py:75
  95.6 3.7 %shard_map.278 = (f32[2048,512]{1,0:T(8,128)S(1)}, bf16[2048,512]{1,0:T(8,128)(2,1)S(1)}, bf16[2048,512]{1,0:T(8,128)(2,1)S(1)}, s32[2048,128]{1,0:T(8,128)S(1)}...) custom-call(s32[2]{0:T(128)S(1)} %pad_add_fusion.place, ...), custom_call_target="tpu_custom_call" | custom-call | flops 536870912 | bytes 2097152 | tf_op jit(solution)/shard_map/pallas_call | solution.py:75
  99.4 5.3 %shard_map.281 = (bf16[512,512]{1,0:T(8,128)(2,1)}, bf16[512,512]{1,0:T(8,128)(2,1)S(1)}, bf16[32,512]{1,0:T(8,128)(2,1)S(1)}, f32[1152,512]{1,0:T(8,128)S(1)}, ...) custom-call(s32[1]{0:T(128)} %get-tuple-element.31.count, ...), custom_call_target="tpu_custom_call" | custom-call | flops 1073741824 | bytes 2097152 | tf_op jit(solution)/shard_map/pallas_call | solution.py:75
  104.6 2.6 %collective-permute-start.28 = (bf16[32,512]{1,0:T(8,128)(2,1)S(1)}, bf16[32,512]{1,0:T(8,128)(2,1)S(1)}, u32[]{:S(2)}, u32[]{:S(2)}) collective-permute-start(bf16[32,512]{1,0:T(8,128)(2,1)S(1)} %get-tuple-element.43), channel_id=1, source_target_pairs={{0,62},{1,63},{2,0},{3,1},{4,2},{5,3},{6,4},{7,5},{8,6},{9,7},{10,... | collective-permute-start | bytes 98312 | tf_op jit(solution)/shard_map/ppermute | solution.py:504
  107.7 1.0 collective-permute-start.25
  108.7 2.7 %shard_map.282.before = f32[1152,512]{1,0:T(8,128)S(1)} custom-call(s32[3,1,384]{2,1,0:T(1,128)} %bitcast.37, bf16[512,512]{1,0:T(8,128)(2,1)S(1)} %get-tuple-element.47.mesh_out, bf16[512,512]{1,0:T(8,128)(2,1)S(1)} %get-tuple-element.44.w_s, f32[1152,512]{1,0:T(8,128)S(1)} %get-tuple-element.48.before), custom_call_target="tpu_custom_call" | custom-call | flops 872415232 | bytes 4718592 | tf_op jit(solution)/shard_map/pallas_call | solution.py:75
  111.8 1.3 %collective-permute-done.25.a = bf16[32,512]{1,0:T(8,128)(2,1)S(1)} collective-permute-done((bf16[32,512]{1,0:T(8,128)(2,1)S(1)}, bf16[32,512]{1,0:T(8,128)(2,1)S(1)}, u32[]{:S(2)}, u32[]{:S(2)}) %collective-permute-start.25) | collective-permute-done | bytes 32800 | tf_op jit(solution)/shard_map/ppermute | solution.py:504
  113.1 6.8 %shard_map.283 = bf16[384,512]{1,0:T(8,128)(2,1)} custom-call(s32[3,1,384]{2,1,0:T(1,128)} %bitcast.38, s32[3,1,384]{2,1,0:T(1,128)} %bitcast.36, s32[4,8]{1,0:T(4,128)} %bitcast.47, bf16[32,512]{1,0:T(8,128)(2,1)S(1)} %collective-permute-done.25.a, bf16[32,512]{1,0:T(8,128)(2,1)S(1)} %collective-permute-done.26.b, ...), custom_call_target="tpu_custom_call" | custom-call | flops 1811939328 | bytes 3538944 | tf_op jit(solution)/shard_map/pallas_call | solution.py:75
  (47 shorter events, 5.3 us)
Async XLA Ops:
  3.3 31.1 %collective-permute-start.11 = (bf16[64,512]{1,0:T(8,128)(2,1)S(1)}, bf16[64,512]{1,0:T(8,128)(2,1)S(1)}, u32[]{:S(2)}, u32[]{:S(2)}) collective-permute-start(bf16[64,512]{1,0:T(8,128)(2,1)S(1)} %pad_maximum_fusion.both), channel_id=1, source_target_pairs={{0,24},{1,41},{2,26},{3,43},{4,28},{5,45},{6,30},{7,47},{8,32},{9,... | collective-permute-start | bytes 196616 | tf_op jit(solution)/shard_map/ppermute | solution.py:410
  26.1 11.4 %collective-permute-start.1 = (bf16[64,512]{1,0:T(8,128)(2,1)S(1)}, bf16[64,512]{1,0:T(8,128)(2,1)S(1)}, u32[]{:S(2)}, u32[]{:S(2)}) collective-permute-start(bf16[64,512]{1,0:T(8,128)(2,1)S(1)} %pad_maximum_fusion.both), channel_id=1, source_target_pairs={{0,2},{1,63},{2,4},{3,1},{4,6},{5,3},{6,8},{7,5},{8,10},{9,7},{10,... | collective-permute-start | bytes 196616 | tf_op jit(solution)/shard_map/ppermute | solution.py:410
  35.6 20.4 %collective-permute-start.13 = (bf16[128,512]{1,0:T(8,128)(2,1)S(1)}, bf16[128,512]{1,0:T(8,128)(2,1)S(1)}, u32[]{:S(2)}, u32[]{:S(2)}) collective-permute-start(bf16[128,512]{1,0:T(8,128)(2,1)S(1)} %constant_dynamic-update-slice_fusion.refs_9_), channel_id=1, source_target_pairs={{0,2},{1,63},{2,4},{3,1},{4,6},{5,3},{6,8},{7,5},{8,10},{9,7},{10,... | collective-permute-start | bytes 393224 | tf_op jit(solution)/shard_map/ppermute | solution.py:410
  37.6 18.5 %collective-permute-start.2 = (bf16[64,512]{1,0:T(8,128)(2,1)S(1)}, bf16[64,512]{1,0:T(8,128)(2,1)S(1)}, u32[]{:S(2)}, u32[]{:S(2)}) collective-permute-start(bf16[64,512]{1,0:T(8,128)(2,1)S(1)} %collective-permute-done.1.ready.up), channel_id=1, source_target_pairs={{0,2},{1,63},{2,4},{3,1},{4,6},{5,3},{6,8},{7,5},{8,10},{9,7},{10,... | collective-permute-start | bytes 196616 | tf_op jit(solution)/shard_map/ppermute | solution.py:410
  56.0 5.5 %collective-permute-start.3 = (bf16[64,512]{1,0:T(8,128)(2,1)S(1)}, bf16[64,512]{1,0:T(8,128)(2,1)S(1)}, u32[]{:S(2)}, u32[]{:S(2)}) collective-permute-start(bf16[64,512]{1,0:T(8,128)(2,1)S(1)} %collective-permute-done.2.ready.refs_0_), channel_id=1, source_target_pairs={{0,2},{1,63},{2,4},{3,1},{4,6},{5,3},{6,8},{7,5},{8,10},{9,7},{10,... | collective-permute-start | bytes 196616 | tf_op jit(solution)/shard_map/ppermute | solution.py:410
  56.1 11.0 %collective-permute-start.14 = (bf16[128,512]{1,0:T(8,128)(2,1)S(1)}, bf16[128,512]{1,0:T(8,128)(2,1)S(1)}, u32[]{:S(2)}, u32[]{:S(2)}) collective-permute-start(bf16[128,512]{1,0:T(8,128)(2,1)S(1)} %collective-permute-done.13.refs_10_), channel_id=1, source_target_pairs={{0,2},{1,63},{2,4},{3,1},{4,6},{5,3},{6,8},{7,5},{8,10},{9,7},{10,... | collective-permute-start | bytes 393224 | tf_op jit(solution)/shard_map/ppermute | solution.py:410
  61.5 5.5 %collective-permute-start.4 = (bf16[64,512]{1,0:T(8,128)(2,1)S(1)}, bf16[64,512]{1,0:T(8,128)(2,1)S(1)}, u32[]{:S(2)}, u32[]{:S(2)}) collective-permute-start(bf16[64,512]{1,0:T(8,128)(2,1)S(1)} %collective-permute-done.3.refs_1_.ready), channel_id=1, source_target_pairs={{0,2},{1,63},{2,4},{3,1},{4,6},{5,3},{6,8},{7,5},{8,10},{9,7},{10,... | collective-permute-start | bytes 196616 | tf_op jit(solution)/shard_map/ppermute | solution.py:410
  61.6 12.1 %collective-permute-start.18 = (bf16[64,512]{1,0:T(8,128)(2,1)S(1)}, bf16[64,512]{1,0:T(8,128)(2,1)S(1)}, u32[]{:S(2)}, u32[]{:S(2)}) collective-permute-start(bf16[64,512]{1,0:T(8,128)(2,1)S(1)} %collective-permute-done.1.ready.up), channel_id=1, source_target_pairs={{0,1},{1,0},{2,3},{3,2},{4,5},{5,4},{6,7},{7,6},{8,9},{9,8},{10,11... | collective-permute-start | bytes 196616 | tf_op jit(solution)/shard_map/ppermute | solution.py:413
  62.5 11.7 %collective-permute-start.7 = (bf16[64,512]{1,0:T(8,128)(2,1)S(1)}, bf16[64,512]{1,0:T(8,128)(2,1)S(1)}, u32[]{:S(2)}, u32[]{:S(2)}) collective-permute-start(bf16[64,512]{1,0:T(8,128)(2,1)S(1)} %collective-permute-done.2.ready.refs_0_), channel_id=1, source_target_pairs={{0,1},{1,0},{2,3},{3,2},{4,5},{5,4},{6,7},{7,6},{8,9},{9,8},{10,11... | collective-permute-start | bytes 196616 | tf_op jit(solution)/shard_map/ppermute | solution.py:413
  67.0 7.5 %collective-permute-start.5 = (bf16[64,512]{1,0:T(8,128)(2,1)S(1)}, bf16[64,512]{1,0:T(8,128)(2,1)S(1)}, u32[]{:S(2)}, u32[]{:S(2)}) collective-permute-start(bf16[64,512]{1,0:T(8,128)(2,1)S(1)} %collective-permute-done.4.refs_2_.ready), channel_id=1, source_target_pairs={{0,2},{1,63},{2,4},{3,1},{4,6},{5,3},{6,8},{7,5},{8,10},{9,7},{10,... | collective-permute-start | bytes 196616 | tf_op jit(solution)/shard_map/ppermute | solution.py:410
  67.0 8.5 %collective-permute-start.15 = (bf16[128,512]{1,0:T(8,128)(2,1)S(1)}, bf16[128,512]{1,0:T(8,128)(2,1)S(1)}, u32[]{:S(2)}, u32[]{:S(2)}) collective-permute-start(bf16[128,512]{1,0:T(8,128)(2,1)S(1)} %collective-permute-done.14.refs_11_), channel_id=1, source_target_pairs={{0,2},{1,63},{2,4},{3,1},{4,6},{5,3},{6,8},{7,5},{8,10},{9,7},{10,... | collective-permute-start | bytes 393224 | tf_op jit(solution)/shard_map/ppermute | solution.py:410
  73.5 7.7 %collective-permute-start.8 = (bf16[64,512]{1,0:T(8,128)(2,1)S(1)}, bf16[64,512]{1,0:T(8,128)(2,1)S(1)}, u32[]{:S(2)}, u32[]{:S(2)}) collective-permute-start(bf16[64,512]{1,0:T(8,128)(2,1)S(1)} %collective-permute-done.3.refs_1_.ready), channel_id=1, source_target_pairs={{0,1},{1,0},{2,3},{3,2},{4,5},{5,4},{6,7},{7,6},{8,9},{9,8},{10,11... | collective-permute-start | bytes 196616 | tf_op jit(solution)/shard_map/ppermute | solution.py:413
  73.7 17.1 %collective-permute-start.16 = (bf16[128,512]{1,0:T(8,128)(2,1)S(1)}, bf16[128,512]{1,0:T(8,128)(2,1)S(1)}, u32[]{:S(2)}, u32[]{:S(2)}) collective-permute-start(bf16[128,512]{1,0:T(8,128)(2,1)S(1)} %collective-permute-done.13.refs_10_), channel_id=1, source_target_pairs={{0,1},{1,0},{2,3},{3,2},{4,5},{5,4},{6,7},{7,6},{8,9},{9,8},{10,11... | collective-permute-start | bytes 393224 | tf_op jit(solution)/shard_map/ppermute | solution.py:413
  74.1 10.9 %collective-permute-start.9 = (bf16[64,512]{1,0:T(8,128)(2,1)S(1)}, bf16[64,512]{1,0:T(8,128)(2,1)S(1)}, u32[]{:S(2)}, u32[]{:S(2)}) collective-permute-start(bf16[64,512]{1,0:T(8,128)(2,1)S(1)} %collective-permute-done.4.refs_2_.ready), channel_id=1, source_target_pairs={{0,1},{1,0},{2,3},{3,2},{4,5},{5,4},{6,7},{7,6},{8,9},{9,8},{10,11... | collective-permute-start | bytes 196616 | tf_op jit(solution)/shard_map/ppermute | solution.py:413
  74.5 10.8 %collective-permute-start.6 = (bf16[64,512]{1,0:T(8,128)(2,1)S(1)}, bf16[64,512]{1,0:T(8,128)(2,1)S(1)}, u32[]{:S(2)}, u32[]{:S(2)}) collective-permute-start(bf16[64,512]{1,0:T(8,128)(2,1)S(1)} %collective-permute-done.5.refs_3_), channel_id=1, source_target_pairs={{0,2},{1,63},{2,4},{3,1},{4,6},{5,3},{6,8},{7,5},{8,10},{9,7},{10,... | collective-permute-start | bytes 196616 | tf_op jit(solution)/shard_map/ppermute | solution.py:410
  75.5 15.7 %collective-permute-start.22 = (bf16[128,512]{1,0:T(8,128)(2,1)S(1)}, bf16[128,512]{1,0:T(8,128)(2,1)S(1)}, u32[]{:S(2)}, u32[]{:S(2)}) collective-permute-start(bf16[128,512]{1,0:T(8,128)(2,1)S(1)} %collective-permute-done.15.refs_12_), channel_id=1, source_target_pairs={{0,2},{1,63},{2,4},{3,1},{4,6},{5,3},{6,8},{7,5},{8,10},{9,7},{10,... | collective-permute-start | bytes 393224 | tf_op jit(solution)/shard_map/ppermute | solution.py:410
  81.2 8.2 %collective-permute-start.10 = (bf16[64,512]{1,0:T(8,128)(2,1)S(1)}, bf16[64,512]{1,0:T(8,128)(2,1)S(1)}, u32[]{:S(2)}, u32[]{:S(2)}) collective-permute-start(bf16[64,512]{1,0:T(8,128)(2,1)S(1)} %collective-permute-done.5.refs_3_), channel_id=1, source_target_pairs={{0,1},{1,0},{2,3},{3,2},{4,5},{5,4},{6,7},{7,6},{8,9},{9,8},{10,11... | collective-permute-start | bytes 196616 | tf_op jit(solution)/shard_map/ppermute | solution.py:413
  85.1 10.5 %collective-permute-start.17 = (bf16[128,512]{1,0:T(8,128)(2,1)S(1)}, bf16[128,512]{1,0:T(8,128)(2,1)S(1)}, u32[]{:S(2)}, u32[]{:S(2)}) collective-permute-start(bf16[128,512]{1,0:T(8,128)(2,1)S(1)} %collective-permute-done.14.refs_11_), channel_id=1, source_target_pairs={{0,1},{1,0},{2,3},{3,2},{4,5},{5,4},{6,7},{7,6},{8,9},{9,8},{10,11... | collective-permute-start | bytes 393224 | tf_op jit(solution)/shard_map/ppermute | solution.py:413
  85.2 5.5 %collective-permute-start.19 = (bf16[64,512]{1,0:T(8,128)(2,1)S(1)}, bf16[64,512]{1,0:T(8,128)(2,1)S(1)}, u32[]{:S(2)}, u32[]{:S(2)}) collective-permute-start(bf16[64,512]{1,0:T(8,128)(2,1)S(1)} %collective-permute-done.6.refs_4_), channel_id=1, source_target_pairs={{0,2},{1,63},{2,4},{3,1},{4,6},{5,3},{6,8},{7,5},{8,10},{9,7},{10,... | collective-permute-start | bytes 196616 | tf_op jit(solution)/shard_map/ppermute | solution.py:410
  89.4 9.9 %collective-permute-start.20 = (bf16[64,512]{1,0:T(8,128)(2,1)S(1)}, bf16[64,512]{1,0:T(8,128)(2,1)S(1)}, u32[]{:S(2)}, u32[]{:S(2)}) collective-permute-start(bf16[64,512]{1,0:T(8,128)(2,1)S(1)} %collective-permute-done.6.refs_4_), channel_id=1, source_target_pairs={{0,1},{1,0},{2,3},{3,2},{4,5},{5,4},{6,7},{7,6},{8,9},{9,8},{10,11... | collective-permute-start | bytes 196616 | tf_op jit(solution)/shard_map/ppermute | solution.py:413
  90.7 8.6 %collective-permute-start.21 = (bf16[64,512]{1,0:T(8,128)(2,1)S(1)}, bf16[64,512]{1,0:T(8,128)(2,1)S(1)}, u32[]{:S(2)}, u32[]{:S(2)}) collective-permute-start(bf16[64,512]{1,0:T(8,128)(2,1)S(1)} %collective-permute-done.19.refs_0_), channel_id=1, source_target_pairs={{0,1},{1,0},{2,3},{3,2},{4,5},{5,4},{6,7},{7,6},{8,9},{9,8},{10,11... | collective-permute-start | bytes 196616 | tf_op jit(solution)/shard_map/ppermute | solution.py:413
  90.7 8.6 %collective-permute-start.23 = (bf16[128,512]{1,0:T(8,128)(2,1)S(1)}, bf16[128,512]{1,0:T(8,128)(2,1)S(1)}, u32[]{:S(2)}, u32[]{:S(2)}) collective-permute-start(bf16[128,512]{1,0:T(8,128)(2,1)S(1)} %collective-permute-done.15.refs_12_), channel_id=1, source_target_pairs={{0,1},{1,0},{2,3},{3,2},{4,5},{5,4},{6,7},{7,6},{8,9},{9,8},{10,11... | collective-permute-start | bytes 393224 | tf_op jit(solution)/shard_map/ppermute | solution.py:413
  91.2 8.1 %collective-permute-start.24 = (bf16[128,512]{1,0:T(8,128)(2,1)S(1)}, bf16[128,512]{1,0:T(8,128)(2,1)S(1)}, u32[]{:S(2)}, u32[]{:S(2)}) collective-permute-start(bf16[128,512]{1,0:T(8,128)(2,1)S(1)} %collective-permute-done.22.refs_3_), channel_id=1, source_target_pairs={{0,1},{1,0},{2,3},{3,2},{4,5},{5,4},{6,7},{7,6},{8,9},{9,8},{10,11... | collective-permute-start | bytes 393224 | tf_op jit(solution)/shard_map/ppermute | solution.py:413
  104.6 6.8 %collective-permute-start.28 = (bf16[32,512]{1,0:T(8,128)(2,1)S(1)}, bf16[32,512]{1,0:T(8,128)(2,1)S(1)}, u32[]{:S(2)}, u32[]{:S(2)}) collective-permute-start(bf16[32,512]{1,0:T(8,128)(2,1)S(1)} %get-tuple-element.43), channel_id=1, source_target_pairs={{0,62},{1,63},{2,0},{3,1},{4,2},{5,3},{6,4},{7,5},{8,6},{9,7},{10,... | collective-permute-start | bytes 98312 | tf_op jit(solution)/shard_map/ppermute | solution.py:504
  (5 other events, 16.7 us)

commit v4 on v2

--- a/solution.py
+++ b/solution.py
@@ -54,7 +54,8 @@
 
 
 def silu(x):
-    return x * (0.5 + 0.5 * jnp.tanh(0.5 * x))
+    half = 0.5 * x
+    return half + half * jnp.tanh(half)
 
 
 def finish(pre, bias, w_out, gain):
@@ -269,7 +270,12 @@
         fetch.wait()
 
 
-def far_body(starts, count, nodes, boundary, totals, bias, gain, node_bias, node_gain, w_s, w_out, node_in, node_out, *refs):
+def node_part_body(nodes, w_in, grid_nodes, grid_w_in, ready, out, grid_out):
+    out[...] = dot(nodes[...], w_in[...])
+    grid_out[...] = dot(grid_nodes[...], grid_w_in[...])
+
+
+def far_body(starts, count, nodes, node_part, boundary, totals, bias, gain, node_bias, node_gain, w_s, w_out, node_in, node_out, *refs):
     k, m = len(starts), AHEAD_GRID
     sources, (pre, rows, source_rows, at, target), ahead = refs[:k], refs[k : k + 5], refs[k + 5 : k + 5 + m]
     result, kept_result, published = refs[k + 5 + m : k + 8 + m]
@@ -290,7 +296,7 @@
         return carry
 
     lax.fori_loop(0, count[0], one, 0)
-    pre_node = dot(nodes[...], node_in[0:f, :]) + dot(acc[...].astype(BF), node_in[f : 2 * f, :])
+    pre_node = node_part[...] + dot(acc[...].astype(BF), node_in[f : 2 * f, :])
     update = finish(pre_node, node_bias[...], node_out[...], node_gain[...])
     value = (nodes[...].astype(F32) + update).astype(BF)
     result[...] = value
@@ -311,7 +317,7 @@
     out[...] = before[...] + dot(rows_hot(sender[0], n), table[...])
 
 
-def grid_body(mesh_count, pair, sender, receiver_row, wanted, a, b, c, d, w_s, nodes, edges, before, bias, w_out, gain,
+def grid_body(mesh_count, pair, sender, receiver_row, wanted, a, b, c, d, w_s, nodes, node_part, edges, before, bias, w_out, gain,
               node_in, node_bias, node_out, node_gain, result, totals, table):
     n, f = nodes.shape
     step = pl.program_id(0)
@@ -342,7 +348,7 @@
     @pl.when(step == pl.num_programs(0) - 1)
     def _():
         summed = totals[...].astype(BF)
-        pre = dot(nodes[...], node_in[0:f, :]) + dot(summed, node_in[f : 2 * f, :])
+        pre = node_part[...] + dot(summed, node_in[f : 2 * f, :])
         update = finish(pre, node_bias[...], node_out[...], node_gain[...])
         result[...] = (nodes[...].astype(F32) + update).astype(BF)
 
@@ -481,6 +487,13 @@
     far_needs = [process_node_in, process_node_out]
     grid_needs = [grid_before, decode_edge_in, grid_nodes, grid_edges, decode_edge_out, decode_node_in, decode_node_out]
     on_chip = lambda dtype, width: ((edges, width), dtype, pl.BlockSpec(memory_space=VMEM), VMEM)
+    mesh_part, grid_part = call(
+        node_part_body, (1,),
+        [held(nodes_near), (process_node_in, whole((f, f))), full(grid_nodes), (decode_node_in, whole((f, f))),
+         (chain[2], anywhere)],
+        [((n, f), F32, whole((n, f)), VMEM), ((grid_n, f), F32, whole((grid_n, f)), VMEM)],
+        flops=2 * f * f * (n + grid_n), nbytes=4 * n * f,
+    )
     *stored, count, node_in_near, node_out_near = call(
         functools.partial(compact_body, chips, offered, tuple(starts[i] for i in early)), (1,),
         [(place, smem), (mesh_live, smem), full(send_rows), full(receive_rows), full(need),
@@ -493,7 +506,7 @@
     )
     mesh_out, mesh_kept, published, grid_before, grid_head, nodes_g, edges_g, out_g, node_in_g, node_out_g = call(
         functools.partial(far_body, tuple(starts[i] for i in last)), (1,),
-        [(count, smem), held(nodes_near), full(boundary), held(totals), full(row(process_edge_bias)),
+        [(count, smem), held(nodes_near), held(mesh_part), full(boundary), held(totals), full(row(process_edge_bias)),
          full(row(process_edge_gain)), full(row(process_node_bias)), full(row(process_node_gain)), (w_in_near, whole((f, f)), True),
          held(out_near), held(node_in_near), held(node_out_near)] + [held(far[i]) for i in last]
         + [(v, pl.BlockSpec(memory_space=VMEM), True) for v in stored] + [(v, hbm) for v in grid_needs],
@@ -517,7 +530,7 @@
         functools.partial(grid_body, n, pair), (grid_steps,),
         [(as_rows(grid_sender, GRID_BLOCK), row_spec(GRID_BLOCK)), (as_rows(grid_receiver, GRID_BLOCK), row_spec(GRID_BLOCK)),
          full(grid_need[0]), held(pieces[0]), held(pieces[1]), held(pieces[2]), held(pieces[3]),
-         held(grid_head), held(nodes_g), (edges_g, tile(GRID_BLOCK), True), (grid_local, tile(GRID_BLOCK), True),
+         held(grid_head), held(nodes_g), held(grid_part), (edges_g, tile(GRID_BLOCK), True), (grid_local, tile(GRID_BLOCK), True),
          full(row(decode_edge_bias)), held(out_g), full(row(decode_edge_gain)), held(node_in_g),
          full(row(decode_node_bias)), held(node_out_g), full(row(decode_node_gain))],
         [((grid_n, f), BF, whole((grid_n, f)))],

time: 119 us -> 121 us (1.017)
  Pallas kernels: 40.2 us -> 42.1 us
    pallas_call x9 -> x10, Pallas kernels: 40.2 us -> 42.1 us  [call(): pl.pallas_call(body, grid=grid, in_specs=[i[1] for i in ins], out_specs=[...]
  transfers between devices with their start and end apart: 21 -> 21, of which waited for: 9 -> 9; matrix products, arithmetic and copies ran while one was open for 0% -> 0% of each run, Pallas kernels for 23% -> 24%
where the time goes in v4:
time: 121 us; the launch traced here: 119 us
  waiting for transfers between devices  60.6 us (50%)
  Pallas kernels  42.1 us (35%)
  starting transfers between devices  15.2 us (13%)
  between operations  1.46 us (1%)
    ppermute x8, waiting for transfers between devices, shift(): return lax.ppermute(v, REGION, along(steps))  56.5 us
    pallas_call x10, Pallas kernels, call(): pl.pallas_call(body, grid=grid, in_specs=[i[1] for i in ins], out_specs=[...  42.1 us
    ppermute x8, starting transfers between devices, shift(): return lax.ppermute(v, REGION, along(steps))  6.8 us
    ppermute x9, starting transfers between devices, swap(): return lax.ppermute(v, 'core', [(0, 1), (1, 0)])  5.79 us
    ppermute x4, starting transfers between devices, local(): lax.ppermute(published, REGION, [(s, (s - offset) % regions) for s in ran...  2.65 us
  transfers between devices with their start and end apart: 21, of which 9 were waited for; matrix products, arithmetic and copies ran while one was open for 0% of the time, Pallas kernels for 24%

profile of v4, /device:TPU:44, one launch (start us, length us, event | category | flops | bytes accessed | tf_op | source)
XLA Modules:
  0.0 119.5 jit_solution(127989640130983252)
XLA Ops:
  0.6 1.3 %shard_map.275 = bf16[32,512]{1,0:T(8,128)(2,1)S(1)} custom-call(s32[1,32]{1,0:T(1,128)} %boundary.1, bf16[512,512]{1,0:T(8,128)(2,1)} %refs_1_.1), custom_call_target="tpu_custom_call" | custom-call | flops 16777216 | bytes 524288 | tf_op jit(solution)/shard_map/pallas_call | solution.py:76
  2.1 1.2 collective-permute-done
  3.3 2.1 %collective-permute-start.1 = (bf16[64,512]{1,0:T(8,128)(2,1)S(1)}, bf16[64,512]{1,0:T(8,128)(2,1)S(1)}, u32[]{:S(2)}, u32[]{:S(2)}) collective-permute-start(bf16[64,512]{1,0:T(8,128)(2,1)S(1)} %pad_maximum_fusion.both), channel_id=1, source_target_pairs={{0,2},{1,63},{2,4},{3,1},{4,6},{5,3},{6,8},{7,5},{8,10},{9,7},{10,... | collective-permute-start | bytes 196616 | tf_op jit(solution)/shard_map/ppermute | solution.py:415
  5.4 23.2 %collective-permute-done.1.ready.up = bf16[64,512]{1,0:T(8,128)(2,1)S(1)} collective-permute-done((bf16[64,512]{1,0:T(8,128)(2,1)S(1)}, bf16[64,512]{1,0:T(8,128)(2,1)S(1)}, u32[]{:S(2)}, u32[]{:S(2)}) %collective-permute-start.1) | collective-permute-done | bytes 65568 | tf_op jit(solution)/shard_map/ppermute | solution.py:415
  28.6 4.0 %collective-permute-start.5 = (bf16[64,512]{1,0:T(8,128)(2,1)S(1)}, bf16[64,512]{1,0:T(8,128)(2,1)S(1)}, u32[]{:S(2)}, u32[]{:S(2)}) collective-permute-start(bf16[64,512]{1,0:T(8,128)(2,1)S(1)} %pad_maximum_fusion.both), channel_id=1, source_target_pairs={{0,24},{1,41},{2,26},{3,43},{4,28},{5,45},{6,30},{7,47},{8,32},{9,... | collective-permute-start | bytes 196616 | tf_op jit(solution)/shard_map/ppermute | solution.py:415
  32.5 1.5 %collective-permute-done.2.ready.refs_0_ = bf16[64,512]{1,0:T(8,128)(2,1)S(1)} collective-permute-done((bf16[64,512]{1,0:T(8,128)(2,1)S(1)}, bf16[64,512]{1,0:T(8,128)(2,1)S(1)}, u32[]{:S(2)}, u32[]{:S(2)}) %collective-permute-start.2) | collective-permute-done | bytes 65568 | tf_op jit(solution)/shard_map/ppermute | solution.py:415
  34.7 11.8 %collective-permute-done.5 = bf16[64,512]{1,0:T(8,128)(2,1)S(1)} collective-permute-done((bf16[64,512]{1,0:T(8,128)(2,1)S(1)}, bf16[64,512]{1,0:T(8,128)(2,1)S(1)}, u32[]{:S(2)}, u32[]{:S(2)}) %collective-permute-start.5) | collective-permute-done | bytes 65568 | tf_op jit(solution)/shard_map/ppermute | solution.py:415
  47.2 0.9 collective-permute-done.6
  48.1 13.8 %collective-permute-done.7.refs_3_.ready = bf16[192,512]{1,0:T(8,128)(2,1)S(1)} collective-permute-done((bf16[192,512]{1,0:T(8,128)(2,1)S(1)}, bf16[192,512]{1,0:T(8,128)(2,1)S(1)}, u32[]{:S(2)}, u32[]{:S(2)}) %collective-permute-start.7) | collective-permute-done | bytes 196640 | tf_op jit(solution)/shard_map/ppermute | solution.py:415
  62.5 6.2 %collective-permute-done.8.refs_4_.ready = bf16[192,512]{1,0:T(8,128)(2,1)S(1)} collective-permute-done((bf16[192,512]{1,0:T(8,128)(2,1)S(1)}, bf16[192,512]{1,0:T(8,128)(2,1)S(1)}, u32[]{:S(2)}, u32[]{:S(2)}) %collective-permute-start.8) | collective-permute-done | bytes 196640 | tf_op jit(solution)/shard_map/ppermute | solution.py:415
  68.8 0.8 collective-permute-start.13
  69.7 6.4 %shard_map.276 = (f32[1152,512]{1,0:T(8,128)}, bf16[1536,512]{1,0:T(8,128)(2,1)S(1)}, bf16[512,512]{1,0:T(8,128)(2,1)S(1)}, bf16[2048,512]{1,0:T(8,128)(2,1)S(1)}, bf16[512,512]{1,0:T(8,128)(2,1)S(1)}) custom-call(s32[3,1,384]{2,1,0:T(1,128)} %bitcast.35, bf16[384,512]{1,0:T(8,128)(2,1)} %refs_10_.3, bf16[1536,512]{1,0:T(8,128)(2,1)} %refs_9_.3, ...), custom_call_target="tpu_custom_call" | custom-call | flops 1409286144 | bytes 3538944 | tf_op jit(solution)/shard_map/pallas_call | solution.py:76
  76.4 5.6 %shard_map.277 = (f32[2048,512]{1,0:T(8,128)S(1)}, bf16[512,512]{1,0:T(8,128)(2,1)S(1)}) custom-call(s32[4,4,128]{2,1,0:T(4,128)} %bitcast.22, s32[4,4,128]{2,1,0:T(4,128)} %bitcast.28, bf16[512,512]{1,0:T(8,128)(2,1)S(1)} %get-tuple-element.30.nodes, bf16[1536,512]{1,0:T(8,128)(2,1)S(1)} %get-tuple-element.29.w_in.w_e.w_s, ...), custom_call_target="tpu_custom_call" | custom-call | flops 3758096384 | bytes 6291456 | tf_op jit(solution)/shard_map/pallas_call | solution.py:76
  82.0 2.7 %collective-permute-start.11 = (bf16[192,512]{1,0:T(8,128)(2,1)S(1)}, bf16[192,512]{1,0:T(8,128)(2,1)S(1)}, u32[]{:S(2)}, u32[]{:S(2)}) collective-permute-start(bf16[192,512]{1,0:T(8,128)(2,1)S(1)} %collective-permute-done.7.refs_3_.ready), channel_id=1, source_target_pairs={{0,1},{1,0},{2,3},{3,2},{4,5},{5,4},{6,7},{7,6},{8,9},{9,8},{10,11... | collective-permute-start | bytes 589832 | tf_op jit(solution)/shard_map/ppermute | solution.py:418
  85.4 4.2 %shard_map.280.refs_0_ = f32[512,512]{1,0:T(8,128)S(1)} custom-call(s32[2]{0:T(128)S(1)} %pad_add_fusion.place, s32[1]{0:T(128)S(6)} %copy.32.live, s32[4,4,128]{2,1,0:T(4,128)} %bitcast.23, s32[4,1,512]{2,1,0:T(1,128)} %bitcast.24, s32[4,1,512]{2,1,0:T(1,128)} %bitcast.29, s32[8,64]{1,0:T(8,128)} %bitcast.32, ...), custom_call_target="tpu_custom_call" | custom-call | flops 1073741824 | bytes 3145728 | tf_op jit(solution)/shard_map/pallas_call | solution.py:76
  90.2 4.3 %shard_map.281.totals = f32[512,512]{1,0:T(8,128)S(1)} custom-call(s32[2]{0:T(128)S(1)} %pad_add_fusion.place, s32[1]{0:T(128)S(6)} %copy.32.live, s32[4,4,128]{2,1,0:T(4,128)} %bitcast.25, s32[4,1,512]{2,1,0:T(1,128)} %bitcast.26, s32[4,1,512]{2,1,0:T(1,128)} %bitcast.30, s32[8,64]{1,0:T(8,128)} %bitcast.33, ...), custom_call_target="tpu_custom_call" | custom-call | flops 1073741824 | bytes 3145728 | tf_op jit(solution)/shard_map/pallas_call | solution.py:76
  94.5 2.0 %shard_map.279 = (f32[512,512]{1,0:T(8,128)S(1)}, f32[384,512]{1,0:T(8,128)S(1)}) custom-call(bf16[512,512]{1,0:T(8,128)(2,1)S(1)} %get-tuple-element.30.nodes, bf16[1024,512]{1,0:T(8,128)(2,1)} %w_in.3, bf16[384,512]{1,0:T(8,128)(2,1)} %refs_10_.3, bf16[1024,512]{1,0:T(8,128)(2,1)} %refs_13_.1, bf16[192,512]{1,0:T(8,128)(2,1)S(1)} %collective-permute-done.8.refs_4_.ready), custom_call_target="tpu_custom_call" | custom-call | flops 469762048 | bytes 1048576 | tf_op jit(solution)/shard_map/pallas_call | solution.py:76
  96.4 3.7 %shard_map.278 = (f32[2048,512]{1,0:T(8,128)S(1)}, bf16[2048,512]{1,0:T(8,128)(2,1)S(1)}, bf16[2048,512]{1,0:T(8,128)(2,1)S(1)}, s32[2048,128]{1,0:T(8,128)S(1)}...) custom-call(s32[2]{0:T(128)S(1)} %pad_add_fusion.place, ...), custom_call_target="tpu_custom_call" | custom-call | flops 536870912 | bytes 2097152 | tf_op jit(solution)/shard_map/pallas_call | solution.py:76
  100.2 5.1 %shard_map.282 = (bf16[512,512]{1,0:T(8,128)(2,1)}, bf16[512,512]{1,0:T(8,128)(2,1)S(1)}, bf16[32,512]{1,0:T(8,128)(2,1)S(1)}, f32[1152,512]{1,0:T(8,128)S(1)}, ...) custom-call(s32[1]{0:T(128)} %get-tuple-element.33.count, ...), custom_call_target="tpu_custom_call" | custom-call | flops 1073741824 | bytes 2097152 | tf_op jit(solution)/shard_map/pallas_call | solution.py:76
  105.3 0.8 collective-permute-start.20
  106.2 1.3 %collective-permute-start.19 = (bf16[32,512]{1,0:T(8,128)(2,1)S(1)}, bf16[32,512]{1,0:T(8,128)(2,1)S(1)}, u32[]{:S(2)}, u32[]{:S(2)}) collective-permute-start(bf16[32,512]{1,0:T(8,128)(2,1)S(1)} %get-tuple-element.46), channel_id=1, source_target_pairs={{0,63},{1,0},{2,1},{3,2},{4,3},{5,4},{6,5},{7,6},{8,7},{9,8},{10,9... | collective-permute-start | bytes 98312 | tf_op jit(solution)/shard_map/ppermute | solution.py:520
  108.0 2.7 %shard_map.283.before = f32[1152,512]{1,0:T(8,128)S(1)} custom-call(s32[3,1,384]{2,1,0:T(1,128)} %bitcast.37, bf16[512,512]{1,0:T(8,128)(2,1)S(1)} %get-tuple-element.51.mesh_out, bf16[512,512]{1,0:T(8,128)(2,1)S(1)} %get-tuple-element.47.w_s, f32[1152,512]{1,0:T(8,128)S(1)} %get-tuple-element.52.before), custom_call_target="tpu_custom_call" | custom-call | flops 872415232 | bytes 4718592 | tf_op jit(solution)/shard_map/pallas_call | solution.py:76
  110.7 1.3 %collective-permute-done.18.b = bf16[32,512]{1,0:T(8,128)(2,1)S(1)} collective-permute-done((bf16[32,512]{1,0:T(8,128)(2,1)S(1)}, bf16[32,512]{1,0:T(8,128)(2,1)S(1)}, u32[]{:S(2)}, u32[]{:S(2)}) %collective-permute-start.18) | collective-permute-done | bytes 32800 | tf_op jit(solution)/shard_map/ppermute | solution.py:520
  112.7 6.8 %shard_map.284 = bf16[384,512]{1,0:T(8,128)(2,1)} custom-call(s32[3,1,384]{2,1,0:T(1,128)} %bitcast.38, s32[3,1,384]{2,1,0:T(1,128)} %bitcast.36, s32[4,8]{1,0:T(4,128)} %bitcast.47, bf16[32,512]{1,0:T(8,128)(2,1)S(1)} %collective-permute-done.17.a, bf16[32,512]{1,0:T(8,128)(2,1)S(1)} %collective-permute-done.18.b, ...), custom_call_target="tpu_custom_call" | custom-call | flops 1811939328 | bytes 3538944 | tf_op jit(solution)/shard_map/pallas_call | solution.py:76
  (33 shorter events, 4.3 us)
Async XLA Ops:
  1.9 1.3 %collective-permute-start = (bf16[32,512]{1,0:T(8,128)(2,1)S(1)}, bf16[32,512]{1,0:T(8,128)(2,1)S(1)}, u32[]{:S(2)}, u32[]{:S(2)}) collective-permute-start(bf16[32,512]{1,0:T(8,128)(2,1)S(1)} %shard_map.275), channel_id=1, source_target_pairs={{0,1},{1,0},{2,3},{3,2},{4,5},{5,4},{6,7},{7,6},{8,9},{9,8},{10,11... | collective-permute-start | bytes 98312 | tf_op jit(solution)/shard_map/ppermute | solution.py:418
  3.3 25.3 %collective-permute-start.1 = (bf16[64,512]{1,0:T(8,128)(2,1)S(1)}, bf16[64,512]{1,0:T(8,128)(2,1)S(1)}, u32[]{:S(2)}, u32[]{:S(2)}) collective-permute-start(bf16[64,512]{1,0:T(8,128)(2,1)S(1)} %pad_maximum_fusion.both), channel_id=1, source_target_pairs={{0,2},{1,63},{2,4},{3,1},{4,6},{5,3},{6,8},{7,5},{8,10},{9,7},{10,... | collective-permute-start | bytes 196616 | tf_op jit(solution)/shard_map/ppermute | solution.py:415
  28.6 5.5 %collective-permute-start.2 = (bf16[64,512]{1,0:T(8,128)(2,1)S(1)}, bf16[64,512]{1,0:T(8,128)(2,1)S(1)}, u32[]{:S(2)}, u32[]{:S(2)}) collective-permute-start(bf16[64,512]{1,0:T(8,128)(2,1)S(1)} %collective-permute-done.1.ready.up), channel_id=1, source_target_pairs={{0,2},{1,63},{2,4},{3,1},{4,6},{5,3},{6,8},{7,5},{8,10},{9,7},{10,... | collective-permute-start | bytes 196616 | tf_op jit(solution)/shard_map/ppermute | solution.py:415
  28.6 17.9 %collective-permute-start.5 = (bf16[64,512]{1,0:T(8,128)(2,1)S(1)}, bf16[64,512]{1,0:T(8,128)(2,1)S(1)}, u32[]{:S(2)}, u32[]{:S(2)}) collective-permute-start(bf16[64,512]{1,0:T(8,128)(2,1)S(1)} %pad_maximum_fusion.both), channel_id=1, source_target_pairs={{0,24},{1,41},{2,26},{3,43},{4,28},{5,45},{6,30},{7,47},{8,32},{9,... | collective-permute-start | bytes 196616 | tf_op jit(solution)/shard_map/ppermute | solution.py:415
  34.0 13.1 %collective-permute-start.4 = (bf16[64,512]{1,0:T(8,128)(2,1)S(1)}, bf16[64,512]{1,0:T(8,128)(2,1)S(1)}, u32[]{:S(2)}, u32[]{:S(2)}) collective-permute-start(bf16[64,512]{1,0:T(8,128)(2,1)S(1)} %collective-permute-done.2.ready.refs_0_), channel_id=1, source_target_pairs={{0,2},{1,63},{2,4},{3,1},{4,6},{5,3},{6,8},{7,5},{8,10},{9,7},{10,... | collective-permute-start | bytes 196616 | tf_op jit(solution)/shard_map/ppermute | solution.py:415
  46.5 1.6 %collective-permute-start.6 = (bf16[64,512]{1,0:T(8,128)(2,1)S(1)}, bf16[64,512]{1,0:T(8,128)(2,1)S(1)}, u32[]{:S(2)}, u32[]{:S(2)}) collective-permute-start(bf16[64,512]{1,0:T(8,128)(2,1)S(1)} %collective-permute-done.5), channel_id=1, source_target_pairs={{0,1},{1,0},{2,3},{3,2},{4,5},{5,4},{6,7},{7,6},{8,9},{9,8},{10,11... | collective-permute-start | bytes 196616 | tf_op jit(solution)/shard_map/ppermute | solution.py:418
  48.1 13.8 %collective-permute-start.7 = (bf16[192,512]{1,0:T(8,128)(2,1)S(1)}, bf16[192,512]{1,0:T(8,128)(2,1)S(1)}, u32[]{:S(2)}, u32[]{:S(2)}) collective-permute-start(bf16[192,512]{1,0:T(8,128)(2,1)S(1)} %constant_dynamic-update-slice_fusion.refs_2_), channel_id=1, source_target_pairs={{0,2},{1,63},{2,4},{3,1},{4,6},{5,3},{6,8},{7,5},{8,10},{9,7},{10,... | collective-permute-start | bytes 589832 | tf_op jit(solution)/shard_map/ppermute | solution.py:415
  61.9 6.9 %collective-permute-start.8 = (bf16[192,512]{1,0:T(8,128)(2,1)S(1)}, bf16[192,512]{1,0:T(8,128)(2,1)S(1)}, u32[]{:S(2)}, u32[]{:S(2)}) collective-permute-start(bf16[192,512]{1,0:T(8,128)(2,1)S(1)} %collective-permute-done.7.refs_3_.ready), channel_id=1, source_target_pairs={{0,2},{1,63},{2,4},{3,1},{4,6},{5,3},{6,8},{7,5},{8,10},{9,7},{10,... | collective-permute-start | bytes 589832 | tf_op jit(solution)/shard_map/ppermute | solution.py:415
  68.8 7.5 %collective-permute-start.9 = (bf16[192,512]{1,0:T(8,128)(2,1)S(1)}, bf16[192,512]{1,0:T(8,128)(2,1)S(1)}, u32[]{:S(2)}, u32[]{:S(2)}) collective-permute-start(bf16[192,512]{1,0:T(8,128)(2,1)S(1)} %collective-permute-done.8.refs_4_.ready), channel_id=1, source_target_pairs={{0,2},{1,63},{2,4},{3,1},{4,6},{5,3},{6,8},{7,5},{8,10},{9,7},{10,... | collective-permute-start | bytes 589832 | tf_op jit(solution)/shard_map/ppermute | solution.py:415
  68.8 16.1 %collective-permute-start.13 = (bf16[64,512]{1,0:T(8,128)(2,1)S(1)}, bf16[64,512]{1,0:T(8,128)(2,1)S(1)}, u32[]{:S(2)}, u32[]{:S(2)}) collective-permute-start(bf16[64,512]{1,0:T(8,128)(2,1)S(1)} %collective-permute-done.1.ready.up), channel_id=1, source_target_pairs={{0,1},{1,0},{2,3},{3,2},{4,5},{5,4},{6,7},{7,6},{8,9},{9,8},{10,11... | collective-permute-start | bytes 196616 | tf_op jit(solution)/shard_map/ppermute | solution.py:418
  76.1 13.6 %collective-permute-start.3 = (bf16[64,512]{1,0:T(8,128)(2,1)S(1)}, bf16[64,512]{1,0:T(8,128)(2,1)S(1)}, u32[]{:S(2)}, u32[]{:S(2)}) collective-permute-start(bf16[64,512]{1,0:T(8,128)(2,1)S(1)} %collective-permute-done.2.ready.refs_0_), channel_id=1, source_target_pairs={{0,1},{1,0},{2,3},{3,2},{4,5},{5,4},{6,7},{7,6},{8,9},{9,8},{10,11... | collective-permute-start | bytes 196616 | tf_op jit(solution)/shard_map/ppermute | solution.py:418
  76.3 9.0 %collective-permute-start.14 = (bf16[192,512]{1,0:T(8,128)(2,1)S(1)}, bf16[192,512]{1,0:T(8,128)(2,1)S(1)}, u32[]{:S(2)}, u32[]{:S(2)}) collective-permute-start(bf16[192,512]{1,0:T(8,128)(2,1)S(1)} %collective-permute-done.9.refs_5_), channel_id=1, source_target_pairs={{0,2},{1,63},{2,4},{3,1},{4,6},{5,3},{6,8},{7,5},{8,10},{9,7},{10,... | collective-permute-start | bytes 589832 | tf_op jit(solution)/shard_map/ppermute | solution.py:415
  82.0 14.4 %collective-permute-start.11 = (bf16[192,512]{1,0:T(8,128)(2,1)S(1)}, bf16[192,512]{1,0:T(8,128)(2,1)S(1)}, u32[]{:S(2)}, u32[]{:S(2)}) collective-permute-start(bf16[192,512]{1,0:T(8,128)(2,1)S(1)} %collective-permute-done.7.refs_3_.ready), channel_id=1, source_target_pairs={{0,1},{1,0},{2,3},{3,2},{4,5},{5,4},{6,7},{7,6},{8,9},{9,8},{10,11... | collective-permute-start | bytes 589832 | tf_op jit(solution)/shard_map/ppermute | solution.py:418
  84.8 11.7 %collective-permute-start.12 = (bf16[192,512]{1,0:T(8,128)(2,1)S(1)}, bf16[192,512]{1,0:T(8,128)(2,1)S(1)}, u32[]{:S(2)}, u32[]{:S(2)}) collective-permute-start(bf16[192,512]{1,0:T(8,128)(2,1)S(1)} %collective-permute-done.8.refs_4_.ready), channel_id=1, source_target_pairs={{0,1},{1,0},{2,3},{3,2},{4,5},{5,4},{6,7},{7,6},{8,9},{9,8},{10,11... | collective-permute-start | bytes 589832 | tf_op jit(solution)/shard_map/ppermute | solution.py:418
  84.9 15.3 %collective-permute-start.15 = (bf16[192,512]{1,0:T(8,128)(2,1)S(1)}, bf16[192,512]{1,0:T(8,128)(2,1)S(1)}, u32[]{:S(2)}, u32[]{:S(2)}) collective-permute-start(bf16[192,512]{1,0:T(8,128)(2,1)S(1)} %collective-permute-done.9.refs_5_), channel_id=1, source_target_pairs={{0,1},{1,0},{2,3},{3,2},{4,5},{5,4},{6,7},{7,6},{8,9},{9,8},{10,11... | collective-permute-start | bytes 589832 | tf_op jit(solution)/shard_map/ppermute | solution.py:418
  85.3 14.9 %collective-permute-start.16 = (bf16[192,512]{1,0:T(8,128)(2,1)S(1)}, bf16[192,512]{1,0:T(8,128)(2,1)S(1)}, u32[]{:S(2)}, u32[]{:S(2)}) collective-permute-start(bf16[192,512]{1,0:T(8,128)(2,1)S(1)} %collective-permute-done.14.refs_0_), channel_id=1, source_target_pairs={{0,1},{1,0},{2,3},{3,2},{4,5},{5,4},{6,7},{7,6},{8,9},{9,8},{10,11... | collective-permute-start | bytes 589832 | tf_op jit(solution)/shard_map/ppermute | solution.py:418
  89.7 6.7 %collective-permute-start.10 = (bf16[64,512]{1,0:T(8,128)(2,1)S(1)}, bf16[64,512]{1,0:T(8,128)(2,1)S(1)}, u32[]{:S(2)}, u32[]{:S(2)}) collective-permute-start(bf16[64,512]{1,0:T(8,128)(2,1)S(1)} %collective-permute-done.4.ready), channel_id=1, source_target_pairs={{0,1},{1,0},{2,3},{3,2},{4,5},{5,4},{6,7},{7,6},{8,9},{9,8},{10,11... | collective-permute-start | bytes 196616 | tf_op jit(solution)/shard_map/ppermute | solution.py:418
  105.3 5.4 %collective-permute-start.20 = (bf16[32,512]{1,0:T(8,128)(2,1)S(1)}, bf16[32,512]{1,0:T(8,128)(2,1)S(1)}, u32[]{:S(2)}, u32[]{:S(2)}) collective-permute-start(bf16[32,512]{1,0:T(8,128)(2,1)S(1)} %get-tuple-element.46), channel_id=1, source_target_pairs={{0,62},{1,63},{2,0},{3,1},{4,2},{5,3},{6,4},{7,5},{8,6},{9,7},{10,... | collective-permute-start | bytes 98312 | tf_op jit(solution)/shard_map/ppermute | solution.py:520
  106.2 4.5 %collective-permute-start.19 = (bf16[32,512]{1,0:T(8,128)(2,1)S(1)}, bf16[32,512]{1,0:T(8,128)(2,1)S(1)}, u32[]{:S(2)}, u32[]{:S(2)}) collective-permute-start(bf16[32,512]{1,0:T(8,128)(2,1)S(1)} %get-tuple-element.46), channel_id=1, source_target_pairs={{0,63},{1,0},{2,1},{3,2},{4,3},{5,4},{6,5},{7,6},{8,7},{9,8},{10,9... | collective-permute-start | bytes 98312 | tf_op jit(solution)/shard_map/ppermute | solution.py:520
  107.4 4.6 %collective-permute-start.18 = (bf16[32,512]{1,0:T(8,128)(2,1)S(1)}, bf16[32,512]{1,0:T(8,128)(2,1)S(1)}, u32[]{:S(2)}, u32[]{:S(2)}) collective-permute-start(bf16[32,512]{1,0:T(8,128)(2,1)S(1)} %get-tuple-element.46), channel_id=1, source_target_pairs={{0,1},{1,2},{2,3},{3,4},{4,5},{5,6},{6,7},{7,8},{8,9},{9,10},{10,1... | collective-permute-start | bytes 98312 | tf_op jit(solution)/shard_map/ppermute | solution.py:520
  107.4 5.2 %collective-permute-start.17 = (bf16[32,512]{1,0:T(8,128)(2,1)S(1)}, bf16[32,512]{1,0:T(8,128)(2,1)S(1)}, u32[]{:S(2)}, u32[]{:S(2)}) collective-permute-start(bf16[32,512]{1,0:T(8,128)(2,1)S(1)} %get-tuple-element.46), channel_id=1, source_target_pairs={{0,2},{1,3},{2,4},{3,5},{4,6},{5,7},{6,8},{7,9},{8,10},{9,11},{10,... | collective-permute-start | bytes 98312 | tf_op jit(solution)/shard_map/ppermute | solution.py:520

commit v5 on v4

--- a/solution.py
+++ b/solution.py
@@ -519,18 +519,18 @@
     for offset in (-2, -1, 1, 2):
         pieces.append(lax.ppermute(published, REGION, [(s, (s - offset) % regions) for s in range(regions)]))
     (grid_local,) = call(
-        grid_local_body, (grid_steps,),
-        [(as_rows(grid_sender, GRID_BLOCK), row_spec(GRID_BLOCK)), held(mesh_kept), held(grid_head),
-         (grid_before, tile(GRID_BLOCK), True)],
-        [((grid_e, f), F32, tile(GRID_BLOCK), VMEM)],
+        grid_local_body, (1,),
+        [(as_rows(grid_sender, grid_e), row_spec(grid_e)), held(mesh_kept), held(grid_head),
+         (grid_before, tile(grid_e), True)],
+        [((grid_e, f), F32, tile(grid_e), VMEM)],
         [pltpu.VMEM((n, f), BF)],
         flops=2 * f * f * (grid_e + n), nbytes=8 * grid_e * f,
     )
     (grid_out,) = call(
-        functools.partial(grid_body, n, pair), (grid_steps,),
-        [(as_rows(grid_sender, GRID_BLOCK), row_spec(GRID_BLOCK)), (as_rows(grid_receiver, GRID_BLOCK), row_spec(GRID_BLOCK)),
+        functools.partial(grid_body, n, pair), (1,),
+        [(as_rows(grid_sender, grid_e), row_spec(grid_e)), (as_rows(grid_receiver, grid_e), row_spec(grid_e)),
          full(grid_need[0]), held(pieces[0]), held(pieces[1]), held(pieces[2]), held(pieces[3]),
-         held(grid_head), held(nodes_g), held(grid_part), (edges_g, tile(GRID_BLOCK), True), (grid_local, tile(GRID_BLOCK), True),
+         held(grid_head), held(nodes_g), held(grid_part), (edges_g, tile(grid_e), True), (grid_local, tile(grid_e), True),
          full(row(decode_edge_bias)), held(out_g), full(row(decode_edge_gain)), held(node_in_g),
          full(row(decode_node_bias)), held(node_out_g), full(row(decode_node_gain))],
         [((grid_n, f), BF, whole((grid_n, f)))],

time: 121 us -> 119 us (0.983)
  Pallas kernels: 42.1 us -> 39.5 us
    pallas_call x10, Pallas kernels: 42.1 us -> 39.5 us  [call(): pl.pallas_call(body, grid=grid, in_specs=[i[1] for i in ins], out_specs=[...]
where the time goes in v5:
time: 119 us; the launch traced here: 118 us
  waiting for transfers between devices  61.4 us (52%)
  Pallas kernels  39.5 us (33%)
  starting transfers between devices  15.2 us (13%)
  between operations  1.46 us (1%)
    ppermute x8, waiting for transfers between devices, shift(): return lax.ppermute(v, REGION, along(steps))  56.5 us
    pallas_call x10, Pallas kernels, call(): pl.pallas_call(body, grid=grid, in_specs=[i[1] for i in ins], out_specs=[...  39.5 us
    ppermute x8, starting transfers between devices, shift(): return lax.ppermute(v, REGION, along(steps))  6.8 us
    ppermute x9, starting transfers between devices, swap(): return lax.ppermute(v, 'core', [(0, 1), (1, 0)])  5.79 us
    ppermute x4, waiting for transfers between devices, local(): lax.ppermute(published, REGION, [(s, (s - offset) % regions) for s in ran...  2.82 us
    ppermute x4, starting transfers between devices, local(): lax.ppermute(published, REGION, [(s, (s - offset) % regions) for s in ran...  2.65 us
  transfers between devices with their start and end apart: 21, of which 9 were waited for; matrix products, arithmetic and copies ran while one was open for 0% of the time, Pallas kernels for 24%

profile of v5, /device:TPU:44, one launch (start us, length us, event | category | flops | bytes accessed | tf_op | source)
XLA Modules:
  0.0 117.8 jit_solution(1539339772082191541)
XLA Ops:
  0.6 1.3 %shard_map.275 = bf16[32,512]{1,0:T(8,128)(2,1)S(1)} custom-call(s32[1,32]{1,0:T(1,128)} %boundary.1, bf16[512,512]{1,0:T(8,128)(2,1)} %refs_1_.1), custom_call_target="tpu_custom_call" | custom-call | flops 16777216 | bytes 524288 | tf_op jit(solution)/shard_map/pallas_call | solution.py:76
  2.1 1.2 %collective-permute-done = bf16[32,512]{1,0:T(8,128)(2,1)S(1)} collective-permute-done((bf16[32,512]{1,0:T(8,128)(2,1)S(1)}, bf16[32,512]{1,0:T(8,128)(2,1)S(1)}, u32[]{:S(2)}, u32[]{:S(2)}) %collective-permute-start) | collective-permute-done | bytes 32800 | tf_op jit(solution)/shard_map/ppermute | solution.py:418
  3.3 2.1 %collective-permute-start.1 = (bf16[64,512]{1,0:T(8,128)(2,1)S(1)}, bf16[64,512]{1,0:T(8,128)(2,1)S(1)}, u32[]{:S(2)}, u32[]{:S(2)}) collective-permute-start(bf16[64,512]{1,0:T(8,128)(2,1)S(1)} %pad_maximum_fusion.both), channel_id=1, source_target_pairs={{0,2},{1,63},{2,4},{3,1},{4,6},{5,3},{6,8},{7,5},{8,10},{9,7},{10,... | collective-permute-start | bytes 196616 | tf_op jit(solution)/shard_map/ppermute | solution.py:415
  5.4 23.2 %collective-permute-done.1.ready.up = bf16[64,512]{1,0:T(8,128)(2,1)S(1)} collective-permute-done((bf16[64,512]{1,0:T(8,128)(2,1)S(1)}, bf16[64,512]{1,0:T(8,128)(2,1)S(1)}, u32[]{:S(2)}, u32[]{:S(2)}) %collective-permute-start.1) | collective-permute-done | bytes 65568 | tf_op jit(solution)/shard_map/ppermute | solution.py:415
  28.6 4.0 %collective-permute-start.5 = (bf16[64,512]{1,0:T(8,128)(2,1)S(1)}, bf16[64,512]{1,0:T(8,128)(2,1)S(1)}, u32[]{:S(2)}, u32[]{:S(2)}) collective-permute-start(bf16[64,512]{1,0:T(8,128)(2,1)S(1)} %pad_maximum_fusion.both), channel_id=1, source_target_pairs={{0,24},{1,41},{2,26},{3,43},{4,28},{5,45},{6,30},{7,47},{8,32},{9,... | collective-permute-start | bytes 196616 | tf_op jit(solution)/shard_map/ppermute | solution.py:415
  32.5 1.5 %collective-permute-done.2.ready.refs_0_ = bf16[64,512]{1,0:T(8,128)(2,1)S(1)} collective-permute-done((bf16[64,512]{1,0:T(8,128)(2,1)S(1)}, bf16[64,512]{1,0:T(8,128)(2,1)S(1)}, u32[]{:S(2)}, u32[]{:S(2)}) %collective-permute-start.2) | collective-permute-done | bytes 65568 | tf_op jit(solution)/shard_map/ppermute | solution.py:415
  34.7 11.8 %collective-permute-done.5 = bf16[64,512]{1,0:T(8,128)(2,1)S(1)} collective-permute-done((bf16[64,512]{1,0:T(8,128)(2,1)S(1)}, bf16[64,512]{1,0:T(8,128)(2,1)S(1)}, u32[]{:S(2)}, u32[]{:S(2)}) %collective-permute-start.5) | collective-permute-done | bytes 65568 | tf_op jit(solution)/shard_map/ppermute | solution.py:415
  47.2 0.9 collective-permute-done.6
  48.1 13.8 %collective-permute-done.7.refs_3_.ready = bf16[192,512]{1,0:T(8,128)(2,1)S(1)} collective-permute-done((bf16[192,512]{1,0:T(8,128)(2,1)S(1)}, bf16[192,512]{1,0:T(8,128)(2,1)S(1)}, u32[]{:S(2)}, u32[]{:S(2)}) %collective-permute-start.7) | collective-permute-done | bytes 196640 | tf_op jit(solution)/shard_map/ppermute | solution.py:415
  62.5 6.2 %collective-permute-done.8.refs_4_.ready = bf16[192,512]{1,0:T(8,128)(2,1)S(1)} collective-permute-done((bf16[192,512]{1,0:T(8,128)(2,1)S(1)}, bf16[192,512]{1,0:T(8,128)(2,1)S(1)}, u32[]{:S(2)}, u32[]{:S(2)}) %collective-permute-start.8) | collective-permute-done | bytes 196640 | tf_op jit(solution)/shard_map/ppermute | solution.py:415
  68.8 0.8 collective-permute-start.13
  69.7 6.4 %shard_map.276 = (f32[1152,512]{1,0:T(8,128)}, bf16[1536,512]{1,0:T(8,128)(2,1)S(1)}, bf16[512,512]{1,0:T(8,128)(2,1)S(1)}, bf16[2048,512]{1,0:T(8,128)(2,1)S(1)}, bf16[512,512]{1,0:T(8,128)(2,1)S(1)}) custom-call(s32[3,1,384]{2,1,0:T(1,128)} %bitcast.36, bf16[384,512]{1,0:T(8,128)(2,1)} %refs_10_.3, bf16[1536,512]{1,0:T(8,128)(2,1)} %refs_9_.3, ...), custom_call_target="tpu_custom_call" | custom-call | flops 1409286144 | bytes 3538944 | tf_op jit(solution)/shard_map/pallas_call | solution.py:76
  76.4 5.6 %shard_map.277 = (f32[2048,512]{1,0:T(8,128)S(1)}, bf16[512,512]{1,0:T(8,128)(2,1)S(1)}) custom-call(s32[4,4,128]{2,1,0:T(4,128)} %bitcast.23, s32[4,4,128]{2,1,0:T(4,128)} %bitcast.29, bf16[512,512]{1,0:T(8,128)(2,1)S(1)} %get-tuple-element.30.nodes, bf16[1536,512]{1,0:T(8,128)(2,1)S(1)} %get-tuple-element.29.w_in.w_e.w_s, ...), custom_call_target="tpu_custom_call" | custom-call | flops 3758096384 | bytes 6291456 | tf_op jit(solution)/shard_map/pallas_call | solution.py:76
  82.0 2.7 %collective-permute-start.11 = (bf16[192,512]{1,0:T(8,128)(2,1)S(1)}, bf16[192,512]{1,0:T(8,128)(2,1)S(1)}, u32[]{:S(2)}, u32[]{:S(2)}) collective-permute-start(bf16[192,512]{1,0:T(8,128)(2,1)S(1)} %collective-permute-done.7.refs_3_.ready), channel_id=1, source_target_pairs={{0,1},{1,0},{2,3},{3,2},{4,5},{5,4},{6,7},{7,6},{8,9},{9,8},{10,11... | collective-permute-start | bytes 589832 | tf_op jit(solution)/shard_map/ppermute | solution.py:418
  85.4 4.2 %shard_map.280.refs_0_ = f32[512,512]{1,0:T(8,128)S(1)} custom-call(s32[2]{0:T(128)S(1)} %pad_add_fusion.place, s32[1]{0:T(128)S(6)} %copy.32.live, s32[4,4,128]{2,1,0:T(4,128)} %bitcast.24, s32[4,1,512]{2,1,0:T(1,128)} %bitcast.25, s32[4,1,512]{2,1,0:T(1,128)} %bitcast.30, s32[8,64]{1,0:T(8,128)} %bitcast.33, ...), custom_call_target="tpu_custom_call" | custom-call | flops 1073741824 | bytes 3145728 | tf_op jit(solution)/shard_map/pallas_call | solution.py:76
  90.2 4.3 %shard_map.281.totals = f32[512,512]{1,0:T(8,128)S(1)} custom-call(s32[2]{0:T(128)S(1)} %pad_add_fusion.place, s32[1]{0:T(128)S(6)} %copy.32.live, s32[4,4,128]{2,1,0:T(4,128)} %bitcast.26, s32[4,1,512]{2,1,0:T(1,128)} %bitcast.27, s32[4,1,512]{2,1,0:T(1,128)} %bitcast.31, s32[8,64]{1,0:T(8,128)} %bitcast.34, ...), custom_call_target="tpu_custom_call" | custom-call | flops 1073741824 | bytes 3145728 | tf_op jit(solution)/shard_map/pallas_call | solution.py:76
  94.5 2.0 %shard_map.279 = (f32[512,512]{1,0:T(8,128)S(1)}, f32[384,512]{1,0:T(8,128)S(1)}) custom-call(bf16[512,512]{1,0:T(8,128)(2,1)S(1)} %get-tuple-element.30.nodes, bf16[1024,512]{1,0:T(8,128)(2,1)} %w_in.3, bf16[384,512]{1,0:T(8,128)(2,1)} %refs_10_.3, bf16[1024,512]{1,0:T(8,128)(2,1)} %refs_13_.1, bf16[192,512]{1,0:T(8,128)(2,1)S(1)} %collective-permute-done.8.refs_4_.ready), custom_call_target="tpu_custom_call" | custom-call | flops 469762048 | bytes 1048576 | tf_op jit(solution)/shard_map/pallas_call | solution.py:76
  96.4 3.7 %shard_map.278 = (f32[2048,512]{1,0:T(8,128)S(1)}, bf16[2048,512]{1,0:T(8,128)(2,1)S(1)}, bf16[2048,512]{1,0:T(8,128)(2,1)S(1)}, s32[2048,128]{1,0:T(8,128)S(1)}...) custom-call(s32[2]{0:T(128)S(1)} %pad_add_fusion.place, ...), custom_call_target="tpu_custom_call" | custom-call | flops 536870912 | bytes 2097152 | tf_op jit(solution)/shard_map/pallas_call | solution.py:76
  100.2 5.1 %shard_map.282 = (bf16[512,512]{1,0:T(8,128)(2,1)}, bf16[512,512]{1,0:T(8,128)(2,1)S(1)}, bf16[32,512]{1,0:T(8,128)(2,1)S(1)}, f32[1152,512]{1,0:T(8,128)S(1)}, ...) custom-call(s32[1]{0:T(128)} %get-tuple-element.33.count, ...), custom_call_target="tpu_custom_call" | custom-call | flops 1073741824 | bytes 2097152 | tf_op jit(solution)/shard_map/pallas_call | solution.py:76
  105.3 0.8 collective-permute-start.20
  106.2 1.3 %collective-permute-start.19 = (bf16[32,512]{1,0:T(8,128)(2,1)S(1)}, bf16[32,512]{1,0:T(8,128)(2,1)S(1)}, u32[]{:S(2)}, u32[]{:S(2)}) collective-permute-start(bf16[32,512]{1,0:T(8,128)(2,1)S(1)} %get-tuple-element.46), channel_id=1, source_target_pairs={{0,63},{1,0},{2,1},{3,2},{4,3},{5,4},{6,5},{7,6},{8,7},{9,8},{10,9... | collective-permute-start | bytes 98312 | tf_op jit(solution)/shard_map/ppermute | solution.py:520
  108.0 1.9 %shard_map.283.before = f32[1152,512]{1,0:T(8,128)S(1)} custom-call(s32[1,1,1152]{2,1,0:T(1,128)} %bitcast.38, bf16[512,512]{1,0:T(8,128)(2,1)S(1)} %get-tuple-element.51.mesh_out, bf16[512,512]{1,0:T(8,128)(2,1)S(1)} %get-tuple-element.47.w_s, f32[1152,512]{1,0:T(8,128)S(1)} %get-tuple-element.52.before), custom_call_target="tpu_custom_call" | custom-call | flops 872415232 | bytes 4718592 | tf_op jit(solution)/shard_map/pallas_call | solution.py:76
  109.9 2.1 %collective-permute-done.18.b = bf16[32,512]{1,0:T(8,128)(2,1)S(1)} collective-permute-done((bf16[32,512]{1,0:T(8,128)(2,1)S(1)}, bf16[32,512]{1,0:T(8,128)(2,1)S(1)}, u32[]{:S(2)}, u32[]{:S(2)}) %collective-permute-start.18) | collective-permute-done | bytes 32800 | tf_op jit(solution)/shard_map/ppermute | solution.py:520
  112.7 5.1 %shard_map.284 = bf16[384,512]{1,0:T(8,128)(2,1)} custom-call(s32[1,1,1152]{2,1,0:T(1,128)} %bitcast.39, s32[1,1,1152]{2,1,0:T(1,128)} %bitcast.37, s32[4,8]{1,0:T(4,128)} %bitcast.48, bf16[32,512]{1,0:T(8,128)(2,1)S(1)} %collective-permute-done.17.a, bf16[32,512]{1,0:T(8,128)(2,1)S(1)} %collective-permute-done.18.b, ...), custom_call_target="tpu_custom_call" | custom-call | flops 1811939328 | bytes 3538944 | tf_op jit(solution)/shard_map/pallas_call | solution.py:76
  (33 shorter events, 4.3 us)
Async XLA Ops:
  1.9 1.3 %collective-permute-start = (bf16[32,512]{1,0:T(8,128)(2,1)S(1)}, bf16[32,512]{1,0:T(8,128)(2,1)S(1)}, u32[]{:S(2)}, u32[]{:S(2)}) collective-permute-start(bf16[32,512]{1,0:T(8,128)(2,1)S(1)} %shard_map.275), channel_id=1, source_target_pairs={{0,1},{1,0},{2,3},{3,2},{4,5},{5,4},{6,7},{7,6},{8,9},{9,8},{10,11... | collective-permute-start | bytes 98312 | tf_op jit(solution)/shard_map/ppermute | solution.py:418
  3.3 25.3 %collective-permute-start.1 = (bf16[64,512]{1,0:T(8,128)(2,1)S(1)}, bf16[64,512]{1,0:T(8,128)(2,1)S(1)}, u32[]{:S(2)}, u32[]{:S(2)}) collective-permute-start(bf16[64,512]{1,0:T(8,128)(2,1)S(1)} %pad_maximum_fusion.both), channel_id=1, source_target_pairs={{0,2},{1,63},{2,4},{3,1},{4,6},{5,3},{6,8},{7,5},{8,10},{9,7},{10,... | collective-permute-start | bytes 196616 | tf_op jit(solution)/shard_map/ppermute | solution.py:415
  28.6 5.5 %collective-permute-start.2 = (bf16[64,512]{1,0:T(8,128)(2,1)S(1)}, bf16[64,512]{1,0:T(8,128)(2,1)S(1)}, u32[]{:S(2)}, u32[]{:S(2)}) collective-permute-start(bf16[64,512]{1,0:T(8,128)(2,1)S(1)} %collective-permute-done.1.ready.up), channel_id=1, source_target_pairs={{0,2},{1,63},{2,4},{3,1},{4,6},{5,3},{6,8},{7,5},{8,10},{9,7},{10,... | collective-permute-start | bytes 196616 | tf_op jit(solution)/shard_map/ppermute | solution.py:415
  28.6 17.9 %collective-permute-start.5 = (bf16[64,512]{1,0:T(8,128)(2,1)S(1)}, bf16[64,512]{1,0:T(8,128)(2,1)S(1)}, u32[]{:S(2)}, u32[]{:S(2)}) collective-permute-start(bf16[64,512]{1,0:T(8,128)(2,1)S(1)} %pad_maximum_fusion.both), channel_id=1, source_target_pairs={{0,24},{1,41},{2,26},{3,43},{4,28},{5,45},{6,30},{7,47},{8,32},{9,... | collective-permute-start | bytes 196616 | tf_op jit(solution)/shard_map/ppermute | solution.py:415
  34.0 13.1 %collective-permute-start.4 = (bf16[64,512]{1,0:T(8,128)(2,1)S(1)}, bf16[64,512]{1,0:T(8,128)(2,1)S(1)}, u32[]{:S(2)}, u32[]{:S(2)}) collective-permute-start(bf16[64,512]{1,0:T(8,128)(2,1)S(1)} %collective-permute-done.2.ready.refs_0_), channel_id=1, source_target_pairs={{0,2},{1,63},{2,4},{3,1},{4,6},{5,3},{6,8},{7,5},{8,10},{9,7},{10,... | collective-permute-start | bytes 196616 | tf_op jit(solution)/shard_map/ppermute | solution.py:415
  46.5 1.6 %collective-permute-start.6 = (bf16[64,512]{1,0:T(8,128)(2,1)S(1)}, bf16[64,512]{1,0:T(8,128)(2,1)S(1)}, u32[]{:S(2)}, u32[]{:S(2)}) collective-permute-start(bf16[64,512]{1,0:T(8,128)(2,1)S(1)} %collective-permute-done.5), channel_id=1, source_target_pairs={{0,1},{1,0},{2,3},{3,2},{4,5},{5,4},{6,7},{7,6},{8,9},{9,8},{10,11... | collective-permute-start | bytes 196616 | tf_op jit(solution)/shard_map/ppermute | solution.py:418
  48.1 13.8 %collective-permute-start.7 = (bf16[192,512]{1,0:T(8,128)(2,1)S(1)}, bf16[192,512]{1,0:T(8,128)(2,1)S(1)}, u32[]{:S(2)}, u32[]{:S(2)}) collective-permute-start(bf16[192,512]{1,0:T(8,128)(2,1)S(1)} %constant_dynamic-update-slice_fusion.refs_2_), channel_id=1, source_target_pairs={{0,2},{1,63},{2,4},{3,1},{4,6},{5,3},{6,8},{7,5},{8,10},{9,7},{10,... | collective-permute-start | bytes 589832 | tf_op jit(solution)/shard_map/ppermute | solution.py:415
  61.9 6.9 %collective-permute-start.8 = (bf16[192,512]{1,0:T(8,128)(2,1)S(1)}, bf16[192,512]{1,0:T(8,128)(2,1)S(1)}, u32[]{:S(2)}, u32[]{:S(2)}) collective-permute-start(bf16[192,512]{1,0:T(8,128)(2,1)S(1)} %collective-permute-done.7.refs_3_.ready), channel_id=1, source_target_pairs={{0,2},{1,63},{2,4},{3,1},{4,6},{5,3},{6,8},{7,5},{8,10},{9,7},{10,... | collective-permute-start | bytes 589832 | tf_op jit(solution)/shard_map/ppermute | solution.py:415
  68.8 7.5 %collective-permute-start.9 = (bf16[192,512]{1,0:T(8,128)(2,1)S(1)}, bf16[192,512]{1,0:T(8,128)(2,1)S(1)}, u32[]{:S(2)}, u32[]{:S(2)}) collective-permute-start(bf16[192,512]{1,0:T(8,128)(2,1)S(1)} %collective-permute-done.8.refs_4_.ready), channel_id=1, source_target_pairs={{0,2},{1,63},{2,4},{3,1},{4,6},{5,3},{6,8},{7,5},{8,10},{9,7},{10,... | collective-permute-start | bytes 589832 | tf_op jit(solution)/shard_map/ppermute | solution.py:415
  68.8 16.1 %collective-permute-start.13 = (bf16[64,512]{1,0:T(8,128)(2,1)S(1)}, bf16[64,512]{1,0:T(8,128)(2,1)S(1)}, u32[]{:S(2)}, u32[]{:S(2)}) collective-permute-start(bf16[64,512]{1,0:T(8,128)(2,1)S(1)} %collective-permute-done.1.ready.up), channel_id=1, source_target_pairs={{0,1},{1,0},{2,3},{3,2},{4,5},{5,4},{6,7},{7,6},{8,9},{9,8},{10,11... | collective-permute-start | bytes 196616 | tf_op jit(solution)/shard_map/ppermute | solution.py:418
  76.1 13.6 %collective-permute-start.3 = (bf16[64,512]{1,0:T(8,128)(2,1)S(1)}, bf16[64,512]{1,0:T(8,128)(2,1)S(1)}, u32[]{:S(2)}, u32[]{:S(2)}) collective-permute-start(bf16[64,512]{1,0:T(8,128)(2,1)S(1)} %collective-permute-done.2.ready.refs_0_), channel_id=1, source_target_pairs={{0,1},{1,0},{2,3},{3,2},{4,5},{5,4},{6,7},{7,6},{8,9},{9,8},{10,11... | collective-permute-start | bytes 196616 | tf_op jit(solution)/shard_map/ppermute | solution.py:418
  76.3 9.0 %collective-permute-start.14 = (bf16[192,512]{1,0:T(8,128)(2,1)S(1)}, bf16[192,512]{1,0:T(8,128)(2,1)S(1)}, u32[]{:S(2)}, u32[]{:S(2)}) collective-permute-start(bf16[192,512]{1,0:T(8,128)(2,1)S(1)} %collective-permute-done.9.refs_5_), channel_id=1, source_target_pairs={{0,2},{1,63},{2,4},{3,1},{4,6},{5,3},{6,8},{7,5},{8,10},{9,7},{10,... | collective-permute-start | bytes 589832 | tf_op jit(solution)/shard_map/ppermute | solution.py:415
  82.0 14.4 %collective-permute-start.11 = (bf16[192,512]{1,0:T(8,128)(2,1)S(1)}, bf16[192,512]{1,0:T(8,128)(2,1)S(1)}, u32[]{:S(2)}, u32[]{:S(2)}) collective-permute-start(bf16[192,512]{1,0:T(8,128)(2,1)S(1)} %collective-permute-done.7.refs_3_.ready), channel_id=1, source_target_pairs={{0,1},{1,0},{2,3},{3,2},{4,5},{5,4},{6,7},{7,6},{8,9},{9,8},{10,11... | collective-permute-start | bytes 589832 | tf_op jit(solution)/shard_map/ppermute | solution.py:418
  84.8 11.7 %collective-permute-start.12 = (bf16[192,512]{1,0:T(8,128)(2,1)S(1)}, bf16[192,512]{1,0:T(8,128)(2,1)S(1)}, u32[]{:S(2)}, u32[]{:S(2)}) collective-permute-start(bf16[192,512]{1,0:T(8,128)(2,1)S(1)} %collective-permute-done.8.refs_4_.ready), channel_id=1, source_target_pairs={{0,1},{1,0},{2,3},{3,2},{4,5},{5,4},{6,7},{7,6},{8,9},{9,8},{10,11... | collective-permute-start | bytes 589832 | tf_op jit(solution)/shard_map/ppermute | solution.py:418
  84.9 15.3 %collective-permute-start.15 = (bf16[192,512]{1,0:T(8,128)(2,1)S(1)}, bf16[192,512]{1,0:T(8,128)(2,1)S(1)}, u32[]{:S(2)}, u32[]{:S(2)}) collective-permute-start(bf16[192,512]{1,0:T(8,128)(2,1)S(1)} %collective-permute-done.9.refs_5_), channel_id=1, source_target_pairs={{0,1},{1,0},{2,3},{3,2},{4,5},{5,4},{6,7},{7,6},{8,9},{9,8},{10,11... | collective-permute-start | bytes 589832 | tf_op jit(solution)/shard_map/ppermute | solution.py:418
  85.3 14.9 %collective-permute-start.16 = (bf16[192,512]{1,0:T(8,128)(2,1)S(1)}, bf16[192,512]{1,0:T(8,128)(2,1)S(1)}, u32[]{:S(2)}, u32[]{:S(2)}) collective-permute-start(bf16[192,512]{1,0:T(8,128)(2,1)S(1)} %collective-permute-done.14.refs_0_), channel_id=1, source_target_pairs={{0,1},{1,0},{2,3},{3,2},{4,5},{5,4},{6,7},{7,6},{8,9},{9,8},{10,11... | collective-permute-start | bytes 589832 | tf_op jit(solution)/shard_map/ppermute | solution.py:418
  89.7 6.7 %collective-permute-start.10 = (bf16[64,512]{1,0:T(8,128)(2,1)S(1)}, bf16[64,512]{1,0:T(8,128)(2,1)S(1)}, u32[]{:S(2)}, u32[]{:S(2)}) collective-permute-start(bf16[64,512]{1,0:T(8,128)(2,1)S(1)} %collective-permute-done.4.ready), channel_id=1, source_target_pairs={{0,1},{1,0},{2,3},{3,2},{4,5},{5,4},{6,7},{7,6},{8,9},{9,8},{10,11... | collective-permute-start | bytes 196616 | tf_op jit(solution)/shard_map/ppermute | solution.py:418
  105.3 4.5 %collective-permute-start.20 = (bf16[32,512]{1,0:T(8,128)(2,1)S(1)}, bf16[32,512]{1,0:T(8,128)(2,1)S(1)}, u32[]{:S(2)}, u32[]{:S(2)}) collective-permute-start(bf16[32,512]{1,0:T(8,128)(2,1)S(1)} %get-tuple-element.46), channel_id=1, source_target_pairs={{0,62},{1,63},{2,0},{3,1},{4,2},{5,3},{6,4},{7,5},{8,6},{9,7},{10,... | collective-permute-start | bytes 98312 | tf_op jit(solution)/shard_map/ppermute | solution.py:520
  106.2 3.7 %collective-permute-start.19 = (bf16[32,512]{1,0:T(8,128)(2,1)S(1)}, bf16[32,512]{1,0:T(8,128)(2,1)S(1)}, u32[]{:S(2)}, u32[]{:S(2)}) collective-permute-start(bf16[32,512]{1,0:T(8,128)(2,1)S(1)} %get-tuple-element.46), channel_id=1, source_target_pairs={{0,63},{1,0},{2,1},{3,2},{4,3},{5,4},{6,5},{7,6},{8,7},{9,8},{10,9... | collective-permute-start | bytes 98312 | tf_op jit(solution)/shard_map/ppermute | solution.py:520
  107.4 4.6 %collective-permute-start.18 = (bf16[32,512]{1,0:T(8,128)(2,1)S(1)}, bf16[32,512]{1,0:T(8,128)(2,1)S(1)}, u32[]{:S(2)}, u32[]{:S(2)}) collective-permute-start(bf16[32,512]{1,0:T(8,128)(2,1)S(1)} %get-tuple-element.46), channel_id=1, source_target_pairs={{0,1},{1,2},{2,3},{3,4},{4,5},{5,6},{6,7},{7,8},{8,9},{9,10},{10,1... | collective-permute-start | bytes 98312 | tf_op jit(solution)/shard_map/ppermute | solution.py:520
  107.4 5.2 %collective-permute-start.17 = (bf16[32,512]{1,0:T(8,128)(2,1)S(1)}, bf16[32,512]{1,0:T(8,128)(2,1)S(1)}, u32[]{:S(2)}, u32[]{:S(2)}) collective-permute-start(bf16[32,512]{1,0:T(8,128)(2,1)S(1)} %get-tuple-element.46), channel_id=1, source_target_pairs={{0,2},{1,3},{2,4},{3,5},{4,6},{5,7},{6,8},{7,9},{8,10},{9,11},{10,... | collective-permute-start | bytes 98312 | tf_op jit(solution)/shard_map/ppermute | solution.py:520
